TPU v7x, 32 devices: a whole 2x2x4 slice. The times are simulated.
32 devices in a mesh: seq: 4 (over y, core), fsdp: 8 (over z, x).
Axes of the slice: x: 2, y: 2, z: 4, core: 2. Of those that a mesh axis runs over, the one named last changes fastest.
Arguments:
- tokens: bfloat16 [8, 1536, 1024], P('fsdp', 'seq'), may hold values from -6 to 6
- lengths: int32 [8, 3], P('fsdp'), may hold values from 1 to 1024, 1536 in all within a row
- time_steps: int32 [8, 3], P('fsdp'), may hold values from 0 to 999
- order: int32 [8, 1536], P('fsdp', 'seq'), may hold values from 0 to 1535, each once within a row
- w_time: bfloat16 [256, 2048], P('fsdp'), may hold values from -0.375 to 0.375
- w_qkv: bfloat16 [1024, 3072], P('fsdp'), may hold values from -0.1875 to 0.1875
- w_out: bfloat16 [1024, 1024], P('fsdp'), may hold values from -1.5 to 1.5
- w_up: bfloat16 [1024, 4096], P('fsdp'), may hold values from -0.1875 to 0.1875
- w_down: bfloat16 [4096, 1024], P('fsdp'), may hold values from -0.09375 to 0.09375
- cotangent: bfloat16 [8, 1536, 1024], P('fsdp', 'seq'), may hold values from -6 to 6
Outputs:
- output: bfloat16 [8, 1536, 1024], P('fsdp', 'seq')
- input_grad: float32 [8, 1536, 1024], P('fsdp', 'seq')
- grad_time: float32 [256, 2048], P('fsdp')
- grad_qkv: float32 [1024, 3072], P('fsdp')
- grad_out: float32 [1024, 1024], P('fsdp')
- grad_up: float32 [1024, 4096], P('fsdp')
- grad_down: float32 [4096, 1024], P('fsdp')
Inputs may be any that keep to these rules, and one draw needn't show every extreme that they name: Each group's 3 lengths sum to 1536; the longest is exactly 1024. `order`: each group's row is a permutation of the indices 0 to 1535.
All inputs are finite; a program needn't handle non-finite values.
Results may differ from a plain program's by a relative error of at most 0.02.
Values may be sent and summed in bfloat16 or wider, within the bound.
A program may use at most 192 MiB of HBM per device.

v0:
```python
import math

import jax
import jax.numpy as jnp
from jax import lax
from jax.sharding import PartitionSpec as P

D = 1024
H = 16
HD = 64
TEMB = 256
NSEQ = 3


EPS = 1e-05
NEG = -1e30
BASE = 10000.0
BLOCK_ROWS = 512


def time_embedding(steps):
    half = TEMB // 2
    freqs = jnp.exp(-math.log(BASE) * jnp.arange(half, dtype=jnp.float32) / half)
    angles = steps.astype(jnp.float32)[:, None] * freqs[None, :]
    return jnp.concatenate([jnp.sin(angles), jnp.cos(angles)], axis=-1)


def layout(lens, places):
    ends = jnp.cumsum(lens)
    starts = ends - lens
    member = (places[:, None] >= starts[None, :]) & (places[:, None] < ends[None, :])
    labels = jnp.arange(NSEQ, dtype=jnp.int32)
    segment = jnp.sum(jnp.where(member, labels[None, :], 0), axis=1)
    offset = places - jnp.sum(jnp.where(member, starts[None, :], 0), axis=1)
    return (member.astype(jnp.float32), segment, offset)


def rotate(values, offset, sign):
    half = HD // 2
    freqs = jnp.exp(-math.log(BASE) * jnp.arange(half, dtype=jnp.float32) * 2.0 / HD)
    angles = offset.astype(jnp.float32)[:, None] * freqs[None, :]
    cosine = jnp.cos(angles)[:, None, :]
    sine = sign * jnp.sin(angles)[:, None, :]
    first = values[..., :half]
    second = values[..., half:]
    return jnp.concatenate(
        [first * cosine - second * sine, second * cosine + first * sine], axis=-1
    )


def norm_mod(values, scale):
    centre = jnp.mean(values, axis=-1, keepdims=True)
    centred = values - centre
    spread = jnp.mean(centred * centred, axis=-1, keepdims=True)
    return centred * lax.rsqrt(spread + EPS) * (1.0 + scale)


def contract_rows(left, right):
    return lax.dot_general(
        left, right, (((0,), (0,)), ((), ())), preferred_element_type=jnp.float32
    )


def contract_cols(left, right):
    return lax.dot_general(
        left, right, (((1,), (1,)), ((), ())), preferred_element_type=jnp.float32
    )


def weight_rows(left, weight):
    return (
        jnp.dot(
            left,
            lax.all_gather(weight, "fsdp", axis=0, tiled=True),
            preferred_element_type=jnp.float32,
        ),
        weight,
    )


def weight_cols(grad, weight):
    return contract_cols(grad, lax.all_gather(weight, "fsdp", axis=0, tiled=True))


def weight_grad(left, grad):

    def term():
        if grad.dtype == jnp.float32:
            return lax.dot_general(
                left.astype(jnp.float32),
                grad,
                (((0,), (0,)), ((), ())),
                precision=lax.Precision.HIGHEST,
                preferred_element_type=jnp.float32,
            )
        return contract_rows(left, grad)

    shard = lax.psum_scatter(
        term().astype(jnp.bfloat16), "fsdp", scatter_dimension=0, tiled=True
    ).astype(jnp.float32)
    shard = lax.psum(shard.astype(jnp.bfloat16), "seq").astype(jnp.float32)
    return shard


def to_heads(packed):
    return lax.all_to_all(packed, "seq", split_axis=2, concat_axis=0, tiled=True)


def to_rows(packed):
    return lax.all_to_all(packed, "seq", split_axis=0, concat_axis=2, tiled=True)


def reorder(data, wanted, labels):
    pick = (wanted[:, None] == labels[None, :]).astype(jnp.bfloat16)
    return jnp.dot(
        pick, lax.all_gather(data, "seq", axis=0, tiled=True), preferred_element_type=jnp.float32
    )


def slice_cols(matrix, start):
    return lax.dynamic_slice_in_dim(matrix, start, HD, 1)


def head_forward(query, key, value, segment, block):
    group = query.shape[0]
    factor = HD ** (-0.5)

    def one_block(index):
        start = index * block
        q_blk = lax.dynamic_slice_in_dim(query, start, block, 0)
        s_blk = lax.dynamic_slice_in_dim(segment, start, block, 0)
        scores = contract_cols(q_blk, key) * factor
        scores = jnp.where(s_blk[:, None] == segment[None, :], scores, NEG)
        peak = jnp.max(scores, axis=1, keepdims=True)
        expo = jnp.exp(scores - peak)
        total = jnp.sum(expo, axis=1, keepdims=True)
        probs = (expo / total).astype(jnp.bfloat16)
        mixed = jnp.dot(probs, value, preferred_element_type=jnp.float32)
        return (mixed.astype(jnp.bfloat16), (peak + jnp.log(total))[:, 0])

    mixed, logsum = lax.map(one_block, jnp.arange(group // block))
    return (mixed.reshape(group, HD), logsum.reshape(group))


def head_backward(query, key, value, logsum, d_mixed, segment, offset, block):
    group = query.shape[0]
    factor = HD ** (-0.5)

    def step(carry, index):
        d_key, d_value = carry
        start = index * block
        q_blk = lax.dynamic_slice_in_dim(query, start, block, 0)
        s_blk = lax.dynamic_slice_in_dim(segment, start, block, 0)
        l_blk = lax.dynamic_slice_in_dim(logsum, start, block, 0)
        g_blk = lax.dynamic_slice_in_dim(d_mixed, start, block, 0)
        scores = contract_cols(q_blk, key) * factor
        probs = jnp.where(s_blk[:, None] == segment[None, :], jnp.exp(scores - l_blk[:, None]), 0.0)
        probs_low = probs.astype(jnp.bfloat16)
        d_value = d_value + contract_rows(probs_low, g_blk)
        d_probs = contract_cols(g_blk, value)
        delta = jnp.sum(probs * d_probs, axis=1, keepdims=True)
        d_scores = (probs * (d_probs - delta)).astype(jnp.bfloat16)
        d_query = jnp.dot(d_scores, key, preferred_element_type=jnp.float32) * factor
        d_key = d_key + contract_rows(d_scores, q_blk) * factor
        return ((d_key, d_value), d_query)

    zeros = jnp.zeros((group, HD), jnp.float32)
    (d_key, d_value), d_query = lax.scan(step, (zeros, zeros), jnp.arange(group // block))
    d_query = d_query.reshape(group, HD)
    back_query = rotate(d_query[:, None, :], offset, -1.0)[:, 0, :]
    back_key = rotate(d_key[:, None, :], offset, -1.0)[:, 0, :]
    return (back_query, back_key, d_value)


def on_device(tokens, lengths, time_steps, order, w_time, w_qkv, w_out, w_up, w_down, cotangent):
    rows = tokens.shape[1]
    slices = lax.axis_size("seq")
    local_heads = H // slices
    group = rows * slices
    block = min(BLOCK_ROWS, group)
    lens = lengths[0]
    places = order[0]
    order_all = lax.all_gather(places, "seq", axis=0, tiled=True)
    member_mine, segment_mine, offset_mine = layout(lens, places)
    member_all, segment_all, offset_all = layout(lens, order_all)
    emb = time_embedding(time_steps[0]).astype(jnp.bfloat16)
    scales_seq, whole_time = weight_rows(emb, w_time)
    scales = jnp.dot(member_mine, scales_seq, precision=lax.Precision.HIGHEST)
    scale_one = scales[:, :D]
    scale_two = scales[:, D:]
    inputs = tokens[0].astype(jnp.float32)
    normed_one, pull_one = jax.vjp(norm_mod, inputs, scale_one)
    h_one = normed_one.astype(jnp.bfloat16)
    projected, whole_qkv = weight_rows(h_one, w_qkv)
    query = rotate(projected[:, :D].reshape(rows, H, HD), offset_mine, 1.0).reshape(rows, D)
    key = rotate(projected[:, D : 2 * D].reshape(rows, H, HD), offset_mine, 1.0).reshape(rows, D)
    packed = jnp.stack([query, key, projected[:, 2 * D :]], axis=1).astype(jnp.bfloat16)
    heads_qkv = to_heads(packed.reshape(rows, 3, slices, local_heads * HD))
    q_heads = heads_qkv[:, 0, 0]
    k_heads = heads_qkv[:, 1, 0]
    v_heads = heads_qkv[:, 2, 0]

    def forward_head(index):
        start = index * HD
        return head_forward(
            slice_cols(q_heads, start),
            slice_cols(k_heads, start),
            slice_cols(v_heads, start),
            segment_all,
            block,
        )

    mixed_heads, logsum_heads = lax.map(forward_head, jnp.arange(local_heads))
    mixed_cat = mixed_heads.transpose(1, 0, 2).reshape(group, 1, 1, local_heads * HD)
    mixed = to_rows(mixed_cat).reshape(rows, D)
    attn_out, whole_out = weight_rows(mixed, w_out)
    x_two = inputs + attn_out
    normed_two, pull_two = jax.vjp(norm_mod, x_two, scale_two)
    h_two = normed_two.astype(jnp.bfloat16)
    up, whole_up = weight_rows(h_two, w_up)
    activated, pull_gelu = jax.vjp(jax.nn.gelu, up)
    hidden = activated.astype(jnp.bfloat16)
    ffn_out, whole_down = weight_rows(hidden, w_down)
    result = (x_two + ffn_out).astype(jnp.bfloat16)
    mine = lax.axis_index("seq") * rows + jnp.arange(rows, dtype=jnp.int32)
    output = reorder(result, mine, order_all).astype(jnp.bfloat16)
    every = jnp.arange(group, dtype=jnp.int32)
    d_result = reorder(cotangent[0], places, every)
    d_low = d_result.astype(jnp.bfloat16)
    d_hidden = weight_cols(d_low, w_down)
    grad_down = weight_grad(hidden, d_low)
    d_up = pull_gelu(d_hidden)[0].astype(jnp.bfloat16)
    grad_up = weight_grad(h_two, d_up)
    d_htwo = weight_cols(d_up, w_up)
    d_xpart, d_scale_two = pull_two(d_htwo)
    d_xtwo = d_result + d_xpart
    d_attn = d_xtwo.astype(jnp.bfloat16)
    grad_out = weight_grad(mixed, d_attn)
    d_mixed = weight_cols(d_attn, w_out).astype(jnp.bfloat16)
    d_heads = to_heads(d_mixed.reshape(rows, 1, slices, local_heads * HD))[:, 0, 0]

    def backward_head(index):
        start = index * HD
        return head_backward(
            slice_cols(q_heads, start),
            slice_cols(k_heads, start),
            slice_cols(v_heads, start),
            logsum_heads[index],
            slice_cols(d_heads, start),
            segment_all,
            offset_all,
            block,
        )

    d_query, d_key, d_value = lax.map(backward_head, jnp.arange(local_heads))
    stacked = jnp.stack([d_query, d_key, d_value], axis=1)
    stacked = (
        stacked.transpose(2, 1, 0, 3).reshape(group, 3, 1, local_heads * HD).astype(jnp.bfloat16)
    )
    d_qkv = to_rows(stacked).reshape(rows, 3 * D)
    grad_qkv = weight_grad(h_one, d_qkv)
    d_hone = weight_cols(d_qkv, w_qkv)
    d_xone, d_scale_one = pull_one(d_hone)
    input_grad = d_xtwo + d_xone
    d_scales = lax.dot_general(
        member_mine,
        jnp.concatenate([d_scale_one, d_scale_two], axis=1),
        (((0,), (0,)), ((), ())),
        precision=lax.Precision.HIGHEST,
        preferred_element_type=jnp.float32,
    )
    grad_time = weight_grad(emb, d_scales)
    grads = (grad_time, grad_qkv, grad_out, grad_up, grad_down)
    return (output[None], input_grad[None], grads[0], grads[1], grads[2], grads[3], grads[4])


def solution(mesh):
    return jax.shard_map(
        on_device,
        mesh=mesh,
        in_specs=(
            P("fsdp", "seq", None),
            P("fsdp", None),
            P("fsdp", None),
            P("fsdp", "seq"),
            P("fsdp", None),
            P("fsdp", None),
            P("fsdp", None),
            P("fsdp", None),
            P("fsdp", None),
            P("fsdp", "seq", None),
        ),
        out_specs=(
            P("fsdp", "seq", None),
            P("fsdp", "seq", None),
            P("fsdp", None),
            P("fsdp", None),
            P("fsdp", None),
            P("fsdp", None),
            P("fsdp", None),
        ),
        check_vma=False,
    )
```

profile of v0, /device:TPU:0, one launch (start us, length us, event | category | flops | bytes accessed | tf_op | source)
XLA Modules:
  0.0 1447.4 jit_solution(13211309296788337764)
XLA Ops:
  11.9 41.2 %all-gather.10.cloned.1.call-done = bf16[256,2048]{1,0:T(8,128)(2,1)} async-done(((bf16[32,2048]{1,0:T(8,128)(2,1)}), bf16[256,2048]{1,0:T(8,128)(2,1)}) %all-gather.10.cloned.1.call-update) | async-done | bytes 1048592 | tf_op jit(solution)/shard_map/all_gather | solution.py:74
  58.2 94.6 %all-gather.12.cloned.1.call-done = bf16[1024,3072]{1,0:T(8,128)(2,1)} async-done(((bf16[128,3072]{1,0:T(8,128)(2,1)}), bf16[1024,3072]{1,0:T(8,128)(2,1)}) %all-gather.12.cloned.1.call-update) | async-done | bytes 6291472 | tf_op jit(solution)/shard_map/all_gather | solution.py:74
  152.8 4.7 fusion.97
  174.5 31.2 %all-gather = s32[1,1536]{1,0:T(1,128)S(1)} all-gather(s32[1,384]{1,0:T(1,128)S(1)} %copy-done.57), channel_id=2, replica_groups=mesh['seq'=4,'fsdp'=8] {'seq'}, dimensions={1}, use_global_device_ids=true | all-gather | bytes 7680 | tf_op jit(solution)/shard_map/all_gather | solution.py:183
  212.0 64.9 %while.88 = (s32[]{:T(128)}, bf16[4,1536,64]{1,2,0:T(8,128)(2,1)S(1)}, f32[4,1536]{1,0:T(4,128)}, s32[4]{0:T(128)S(1)}, bf16[1536,256]{1,0:T(8,128)(2,1)}, /*ind...) while((s32[]{:T(128)}, ...), condition=%wide.region_10.11_spmd, body=%wide.region_5.0_spmd.sunk | while | flops 208436736 | bytes 12839458 | solution.py:213
  215.7 10.6 while.91
  231.9 10.6 while.91
  248.2 10.6 while.91
  264.4 10.6 while.91
  288.4 7.1 all-to-all-done.1
  303.1 59.5 %all-gather.16.cloned.1.call-done = bf16[1024,4096]{1,0:T(8,128)(2,1)} async-done(((bf16[128,4096]{1,0:T(8,128)(2,1)}), bf16[1024,4096]{1,0:T(8,128)(2,1)}) %all-gather.16.cloned.1.call-update) | async-done | bytes 8388624 | tf_op jit(solution)/shard_map/all_gather | solution.py:74
  362.6 9.9 fusion.98
  372.5 114.8 %all-gather.18.cloned.1.call-done = bf16[4096,1024]{1,0:T(8,128)(2,1)} async-done(((bf16[512,1024]{1,0:T(8,128)(2,1)}), bf16[4096,1024]{1,0:T(8,128)(2,1)}) %all-gather.18.cloned.1.call-update) | async-done | bytes 8388624 | tf_op jit(solution)/shard_map/all_gather | solution.py:74
  487.2 10.7 fusion.44
  516.9 8.2 all-to-all-done.2
  525.7 255.7 %while.90 = (s32[]{:T(128)}, bf16[4,1536,64]{1,2,0:T(8,128)(2,1)}, bf16[4,1536,64]{1,2,0:T(8,128)(2,1)}, bf16[4,1536,64]{1,2,0:T(8,128)(2,1)}, s32[4]{0:T(128)},...) while((s32[]{:T(128)}, bf16[4,1536,64]{1,2,0:T(8,128)(2,1)}, ...), condition=%wide.region_20.21_spmd, body=%wide.region_16.20_spmd.sunk | while | flops 513375776 | bytes 57267424 | solution.py:255
  535.7 48.1 %while.92 = (s32[]{:T(128)}, f32[1536,64]{0,1:T(8,128)}, f32[1536,64]{0,1:T(8,128)}, f32[3,512,64]{1,0,2:T(4,128)}, s32[3]{0:T(128)}, /*index=5*/s32[1536]{0:T(1...) while((s32[]{:T(128)}, f32[1536,64]{0,1:T(8,128)}, ...), condition=%wide.region_19.19_spmd.clone, body=%wide.region_17.18_spmd.clone.sunk | while | flops 511704576 | bytes 37968256 | solution.py:168
  599.7 48.1 %while.92 = (s32[]{:T(128)}, f32[1536,64]{0,1:T(8,128)}, f32[1536,64]{0,1:T(8,128)}, f32[3,512,64]{1,0,2:T(4,128)}, s32[3]{0:T(128)}, /*index=5*/s32[1536]{0:T(1...) while((s32[]{:T(128)}, f32[1536,64]{0,1:T(8,128)}, ...), condition=%wide.region_19.19_spmd.clone, body=%wide.region_17.18_spmd.clone.sunk | while | flops 511704576 | bytes 37968256 | solution.py:168
  663.6 48.1 %while.92 = (s32[]{:T(128)}, f32[1536,64]{0,1:T(8,128)}, f32[1536,64]{0,1:T(8,128)}, f32[3,512,64]{1,0,2:T(4,128)}, s32[3]{0:T(128)}, /*index=5*/s32[1536]{0:T(1...) while((s32[]{:T(128)}, f32[1536,64]{0,1:T(8,128)}, ...), condition=%wide.region_19.19_spmd.clone, body=%wide.region_17.18_spmd.clone.sunk | while | flops 511704576 | bytes 37968256 | solution.py:168
  727.5 48.1 %while.92 = (s32[]{:T(128)}, f32[1536,64]{0,1:T(8,128)}, f32[1536,64]{0,1:T(8,128)}, f32[3,512,64]{1,0,2:T(4,128)}, s32[3]{0:T(128)}, /*index=5*/s32[1536]{0:T(1...) while((s32[]{:T(128)}, f32[1536,64]{0,1:T(8,128)}, ...), condition=%wide.region_19.19_spmd.clone, body=%wide.region_17.18_spmd.clone.sunk | while | flops 511704576 | bytes 37968256 | solution.py:168
  789.0 39.6 %all_to_all.63 = bf16[1536,3,1,256]{3,1,2,0:T(4,128)(2,1)S(1)} all-to-all(bf16[1536,3,1,256]{3,1,2,0:T(4,128)(2,1)S(1)} %copy.79), channel_id=1, replica_groups=mesh['seq'=4,'fsdp'=8] {'seq'}, dimensions={0} | all-to-all | bytes 4718592 | tf_op jit(solution)/shard_map/all_to_all | solution.py:110
  834.8 6.7 fusion.63
  846.7 5.6 convolution_convert_fusion.2
  853.4 8.6 convolution_convert_fusion.1
  863.4 10.9 convolution_convert_fusion
  875.7 10.1 add_convert_fusion
  885.9 22.4 %reduce-scatter.6.cloned.1.call-done = bf16[32,2048]{1,0:T(8,128)(2,1)} async-done(((bf16[256,2048]{1,0:T(8,128)(2,1)}), bf16[32,2048]{1,0:T(8,128)(2,1)}) %reduce-scatter.6.cloned.1.call-update) | async-done | bytes 131088 | tf_op jit(solution)/shard_map/reduce_scatter | solution.py:98
  908.2 120.6 %reduce-scatter.8.cloned.1.call-done = bf16[128,3072]{1,0:T(8,128)(2,1)} async-done(((bf16[1024,3072]{1,0:T(8,128)(2,1)}), bf16[128,3072]{1,0:T(8,128)(2,1)}) %reduce-scatter.8.cloned.1.call-update) | async-done | bytes 786448 | tf_op jit(solution)/shard_map/reduce_scatter | solution.py:98
  1028.8 150.2 %reduce-scatter.12.cloned.1.call-done = bf16[128,4096]{1,0:T(8,128)(2,1)} async-done(((bf16[1024,4096]{1,0:T(8,128)(2,1)}), bf16[128,4096]{1,0:T(8,128)(2,1)}) %reduce-scatter.12.cloned.1.call-update) | async-done | bytes 1048592 | tf_op jit(solution)/shard_map/reduce_scatter | solution.py:98
  1179.0 150.2 %reduce-scatter.14.cloned.1.call-done = bf16[512,1024]{1,0:T(8,128)(2,1)} async-done(((bf16[4096,1024]{1,0:T(8,128)(2,1)}), bf16[512,1024]{1,0:T(8,128)(2,1)}) %reduce-scatter.14.cloned.1.call-update) | async-done | bytes 1048592 | tf_op jit(solution)/shard_map/reduce_scatter | solution.py:98
  1330.7 28.2 %all-gather.20.cloned.1.call-done = bf16[1536,1024]{1,0:T(8,128)(2,1)} async-done(((bf16[384,1024]{1,0:T(8,128)(2,1)}), bf16[1536,1024]{1,0:T(8,128)(2,1)}) %all-gather.20.cloned.1.call-update) | async-done | bytes 3145744 | tf_op jit(solution)/shard_map/all_gather | solution.py:116
  1363.1 69.2 %all-reduce.3.cloned.1.call-done = (bf16[32,2048]{1,0:T(8,128)(2,1)}, bf16[128,3072]{1,0:T(8,128)(2,1)}, bf16[128,1024]{1,0:T(8,128)(2,1)}, bf16[128,4096]{1,0:T(8,128)(2,1)}, bf16[512,1024]{1,0:T(8,128)(2,1)}) async-done(((bf16[32,2048]{1,0:T(8,128)(2,1)}, bf16[128,3072]{1,0:T(8,128)(2,1)}, bf16[128,1024]{1,0:T(8,128)(2,1)}, bf16[128,4096]{1,0:T(8,128)(2,1)}, bf16[512,1024]{1,0:T(8,128)(2,1)}), ...) | async-done | bytes 3276816 | tf_op jit(solution)/shard_map/psum | solution.py:101
  (699 shorter events, 400.3 us)
Async XLA Ops:
  7.2 46.0 %all-gather.10.cloned.1.call-start = ((), (), s32[]{:S(2)}) async-start(), calls=%async_computation.9 | async-start | bytes 1179648 | tf_op jit(solution)/shard_map/all_gather | solution.py:74
  7.9 144.8 %all-gather.12.cloned.1.call-start = ((), (), s32[]{:S(2)}) async-start(), calls=%async_computation.10 | async-start | bytes 7077888 | tf_op jit(solution)/shard_map/all_gather | solution.py:74
  8.7 275.2 %all-gather.22.cloned.1.call-start = ((), (), s32[]{:S(2)}) async-start(), calls=%async_computation.20 | async-start | bytes 3932160 | tf_op jit(solution)/shard_map/all_gather | solution.py:116
  9.4 288.0 %all-gather.14.cloned.1.call-start = ((), (), s32[]{:S(2)}) async-start(), calls=%async_computation.11 | async-start | bytes 2359296 | tf_op jit(solution)/shard_map/all_gather | solution.py:74
  10.0 352.6 %all-gather.16.cloned.1.call-start = ((), (), s32[]{:S(2)}) async-start(), calls=%async_computation.12 | async-start | bytes 9437184 | tf_op jit(solution)/shard_map/all_gather | solution.py:74
  10.6 44.0 %copy-start.39 = (s32[384]{0:T(512)}, s32[384]{0:T(512)S(1)}, u32[]{:S(2)}) copy-start(s32[384]{0:T(512)S(1)} %reduce.4) | copy-start | bytes 4612
  10.8 195.0 %copy-start.53 = (s32[3,1]{0,1:T(1,128)}, s32[3,1]{0,1:T(1,128)S(1)}, u32[]{:S(2)}) copy-start(s32[3,1]{0,1:T(1,128)S(1)} %reduce-window.4) | copy-start | bytes 40
  10.9 194.9 %copy-start.55 = (s32[3]{0:T(128)}, s32[3]{0:T(128)S(1)}, u32[]{:S(2)}) copy-start(s32[3]{0:T(128)S(1)} %fusion.87) | copy-start | bytes 40
  11.1 45.0 %copy-start.43 = (f32[384]{0:T(512)}, f32[384]{0:T(512)S(1)}, u32[]{:S(2)}) copy-start(f32[384]{0:T(512)S(1)} %broadcast_multiply_fusion.1) | copy-start | bytes 4612
  11.5 41.7 %copy-start.45 = (f32[384]{0:T(512)}, f32[384]{0:T(512)S(1)}, u32[]{:S(2)}) copy-start(f32[384]{0:T(512)S(1)} %fusion.62) | copy-start | bytes 4612
  11.6 43.0 %copy-start.49 = (bf16[3,128]{1,0:T(4,128)(2,1)}, bf16[3,128]{1,0:T(4,128)(2,1)S(1)}, u32[]{:S(2)}) copy-start(bf16[3,128]{1,0:T(4,128)(2,1)S(1)} %get-tuple-element.551) | copy-start | bytes 2308
  11.6 43.0 %copy-start.51 = (bf16[3,128]{1,0:T(4,128)(2,1)}, bf16[3,128]{1,0:T(4,128)(2,1)S(1)}, u32[]{:S(2)}) copy-start(bf16[3,128]{1,0:T(4,128)(2,1)S(1)} %get-tuple-element.552) | copy-start | bytes 2308
  11.7 46.5 %copy-start.47 = (f32[384]{0:T(512)}, f32[384]{0:T(512)S(1)}, u32[]{:S(2)}) copy-start(f32[384]{0:T(512)S(1)} %fusion.84) | copy-start | bytes 4612
  58.2 99.3 %copy-start.32 = (bf16[384,1024]{1,0:T(8,128)(2,1)}, bf16[384,1024]{1,0:T(8,128)(2,1)S(1)}, u32[]{:S(2)}) copy-start(bf16[384,1024]{1,0:T(8,128)(2,1)S(1)} %fusion.61) | copy-start | bytes 2359300
  170.3 36.2 %all-to-all-start = ((bf16[384,3,4,256]{0,3,1,2:T(8,128)(2,1)}), bf16[384,3,4,256]{0,3,1,2:T(8,128)(2,1)S(1)}, u32[]{:S(2)}, u32[]{:S(2)}) async-start(bf16[384,3,4,256]{0,3,1,2:T(8,128)(2,1)} %copy.73), calls=%async_computation | async-start | bytes 4718592 | tf_op jit(solution)/shard_map/all_to_all | solution.py:106
  173.9 313.3 %all-gather.18.cloned.1.call-start = ((), (), s32[]{:S(2)}) async-start(), calls=%async_computation.13 | async-start | bytes 9437184 | tf_op jit(solution)/shard_map/all_gather | solution.py:74
  279.9 15.5 %all-to-all-start.1 = ((bf16[4,2,49152]{2,1,0:T(2,128)(2,1)}), bf16[4,2,49152]{2,1,0:T(2,128)(2,1)S(1)}, u32[]{:S(2)}, u32[]{:S(2)}) async-start(bf16[4,2,49152]{2,1,0:T(2,128)(2,1)} %reshape.383), calls=%async_computation.1 | async-start | bytes 1572864 | tf_op jit(solution)/shard_map/all_to_all | solution.py:110
  487.2 10.7 copy-start.11
  487.2 10.7 copy-start.58
  510.1 15.1 %all-to-all-start.2 = ((bf16[384,1,4,256]{3,0,1,2:T(8,128)(2,1)}), bf16[384,1,4,256]{3,0,1,2:T(8,128)(2,1)S(1)}, u32[]{:S(2)}, u32[]{:S(2)}) async-start(bf16[384,1,4,256]{3,0,1,2:T(8,128)(2,1)} %copy.78), calls=%async_computation.2 | async-start | bytes 1572864 | tf_op jit(solution)/shard_map/all_to_all | solution.py:106
  513.6 372.3 %reduce-scatter.10.cloned.1.call-start = ((), (), s32[]{:S(2)}) async-start(), calls=%async_computation.17 | async-start | bytes 2359296 | tf_op jit(solution)/shard_map/reduce_scatter | solution.py:98
  516.9 391.4 %reduce-scatter.6.cloned.1.call-start = ((), (), s32[]{:S(2)}) async-start(), calls=%async_computation.15 | async-start | bytes 1179648 | tf_op jit(solution)/shard_map/reduce_scatter | solution.py:98
  525.7 10.0 copy-start.17
  589.7 10.0 copy-start.17
  846.6 182.2 %reduce-scatter.8.cloned.1.call-start = ((), (), s32[]{:S(2)}) async-start(), calls=%async_computation.16 | async-start | bytes 7077888 | tf_op jit(solution)/shard_map/reduce_scatter | solution.py:98
  852.3 326.7 %reduce-scatter.12.cloned.1.call-start = ((), (), s32[]{:S(2)}) async-start(), calls=%async_computation.18 | async-start | bytes 9437184 | tf_op jit(solution)/shard_map/reduce_scatter | solution.py:98
  862.0 467.2 %reduce-scatter.14.cloned.1.call-start = ((), (), s32[]{:S(2)}) async-start(), calls=%async_computation.19 | async-start | bytes 9437184 | tf_op jit(solution)/shard_map/reduce_scatter | solution.py:98
  874.3 484.6 %all-gather.20.cloned.1.call-start = ((), (), s32[]{:S(2)}) async-start(), calls=%async_computation.14 | async-start | bytes 3932160 | tf_op jit(solution)/shard_map/all_gather | solution.py:116
  885.8 443.5 %copy-start.16 = (f32[384,1024]{1,0:T(8,128)S(1)}, f32[384,1024]{1,0:T(8,128)}, u32[]{:S(2)}) copy-start(f32[384,1024]{1,0:T(8,128)} %copy-done.15) | copy-start | bytes 4718596
  885.8 443.5 %copy-start.21 = (f32[384,1024]{1,0:T(8,128)S(1)}, f32[384,1024]{1,0:T(8,128)}, u32[]{:S(2)}) copy-start(f32[384,1024]{1,0:T(8,128)} %get-tuple-element.519) | copy-start | bytes 4718596
  885.8 546.5 %all-reduce.3.cloned.1.call-start = ((), (), s32[]{:S(2)}) async-start(), calls=%async_computation.21 | async-start | bytes 6553600 | tf_op jit(solution)/shard_map/psum | solution.py:101
  1329.3 29.6 %copy-start.38 = (s32[1536]{0:T(1024)S(1)}, s32[1536]{0:T(1024)}, u32[]{:S(2)}) copy-start(s32[1536]{0:T(1024)} %copy-done.36) | copy-start | bytes 18436
  (116 other events, 374.6 us)
Sparse Core Ops, SparseCore 0:
  10.1 42.9 all-gather.9
  55.4 97.3 all-gather.11
  154.4 29.1 all-gather.21
  185.5 51.9 all-gather.13
  239.5 123.0 all-gather.15
  364.6 122.6 all-gather.17
  518.5 66.9 reduce-scatter.9
  846.8 61.4 reduce-scatter.5
  911.8 116.9 reduce-scatter.7
  1032.3 146.6 reduce-scatter.11
  1182.7 146.5 reduce-scatter.13
  1331.2 27.6 all-gather.19
  1361.6 70.6 all-reduce.2
where the time goes:
time: 1460 us; the launch traced here: 1450 us
  waiting for transfers between devices  870 us (60%)
  matrix products  213 us (15%)
  local copies, waits for them, and re-layouts  174 us (12%)
  blocking collectives  70.8 us (5%)
  other arithmetic  65.3 us (4%)
  loops' own time  27.9 us (2%)
  between operations  15.1 us (1%)
    reduce_scatter x5, waiting for transfers between devices, weight_grad(): lax.psum_scatter(term().astype(jnp.bfloat16), 'fsdp', scatter_dimension=0...  443 us
    all_gather x5, waiting for transfers between devices, weight_rows(): lax.all_gather(weight, 'fsdp', axis=0, tiled=True)  310 us
    dot_general x28, matrix products, contract_rows(): lax.dot_general(left, right, (((0,), (0,)), ((), ())), preferred_element_...  78.3 us
    dot_general x40, matrix products, contract_cols(): lax.dot_general(left, right, (((1,), (1,)), ((), ())), preferred_element_...  74.3 us
    psum x1, waiting for transfers between devices, weight_grad(): shard = lax.psum(shard.astype(jnp.bfloat16), 'seq').astype(jnp.float32)  69.2 us
    dynamic_update_slice x24, local copies, waits for them, and re-layouts, head_backward(): lax.scan(step, (zeros, zeros), jnp.arange(group // block))  45.4 us
    all_to_all x1, blocking collectives, to_rows(): lax.all_to_all(packed, 'seq', split_axis=0, concat_axis=2, tiled=True)  39.6 us
    all_gather x1, blocking collectives, on_device(): order_all = lax.all_gather(places, 'seq', axis=0, tiled=True)  31.2 us
  transfers between devices with their start and end apart: 16, of which 12 were waited for; matrix products, arithmetic and copies ran while one was open for 28% of the time, Pallas kernels for 0%

commit v1 on v0

v1 whole, which is shorter than its diff:
```python
import functools
import math

import jax
import jax.numpy as jnp
from jax import lax
from jax.experimental import pallas as pl
from jax.experimental.pallas import tpu as pltpu
from jax.sharding import PartitionSpec as P

H = 16
HD = 64
TEMB = 256
NSEQ = 3

EPS = 1e-05
NEG = -1e30
BASE = 10000.0
LOG2E = math.log2(math.e)
CORES = 2
XS = 2
BF = jnp.bfloat16

ANY = pl.BlockSpec(memory_space=pl.ANY)
VM = pl.BlockSpec(memory_space=pltpu.VMEM)
DMA = pltpu.SemaphoreType.DMA
MESH = pl.DeviceIdType.MESH
VMEM_ALL = 67043328

GATHER_CLASS = {"t": "D", "q": "DCD", "o": "D", "u": "CDDC", "d": "DCDD"}
SUM_CLASS = {"t": "DD", "q": "CDC", "o": "D", "u": "CDCD", "d": "CDCC"}


class Place:
    def __init__(self, slices, shards):
        self.Y, self.Z = slices // CORES, shards // XS
        seq, fsdp = lax.axis_index("seq"), lax.axis_index("fsdp")
        self.y, self.c = lax.div(seq, CORES), lax.rem(seq, CORES)
        self.z, self.x = lax.div(fsdp, XS), lax.rem(fsdp, XS)

    def at(self, z=None, x=None, y=None, c=None):
        z = self.z if z is None else z
        x = self.x if x is None else x
        y = self.y if y is None else y
        c = self.c if c is None else c
        return {"seq": y * CORES + c, "fsdp": z * XS + x}

    def next_y(self, d):
        return lax.rem(self.y + d, self.Y)

    def next_z(self, d):
        return lax.rem(self.z + d, self.Z)


def greet(place, fsdp=True):
    barrier = pltpu.get_barrier_semaphore()
    others = [place.at(c=1 - place.c)]
    others += [place.at(y=place.next_y(d)) for d in range(1, place.Y)]
    if fsdp:
        others += [place.at(x=1 - place.x)]
        others += [place.at(z=place.next_z(d)) for d in range(1, place.Z)]
    for other in others:
        pl.semaphore_signal(barrier, inc=1, device_id=other, device_id_type=MESH)
    pl.semaphore_wait(barrier, len(others))


def push(src, dst, send_sem, recv_sem, device):
    copy = pltpu.make_async_remote_copy(
        src_ref=src,
        dst_ref=dst,
        send_sem=send_sem,
        recv_sem=recv_sem,
        device_id=device,
        device_id_type=MESH,
    )
    copy.start()
    return copy


def keep(src, dst, sem):
    copy = pltpu.make_async_copy(src, dst, sem)
    copy.start()
    return copy


def pipeline(plan, stages):
    for t in range(len(plan) + len(stages) - 1):
        for k, stage in enumerate(stages):
            if stage is not None and 0 <= t - k < len(plan):
                stage(plan[t - k])


class RowGather:
    def __init__(self, place, src, out, bounce, sems, rsems, lsem):
        self.place, self.src, self.out = place, src, out
        self.bounce, self.sems, self.rsems, self.lsem = bounce, sems, rsems, lsem

    def load(self):
        self.own = keep(self.src, self.bounce, self.lsem)

    def start(self):
        p = self.place
        slot = self.out.at[p.y, p.c]
        self.over_y = [
            push(self.src, slot, self.sems.at[d], self.rsems.at[d], p.at(y=p.next_y(d)))
            for d in range(1, p.Y)
        ]
        self.own.wait()
        self.own = keep(self.bounce, slot, self.lsem)

    def middle(self):
        p = self.place
        for copy in self.over_y:
            copy.wait_recv()
        self.own.wait()
        half = self.out.at[:, p.c]
        self.over_c = push(half, half, self.sems.at[0], self.rsems.at[0], p.at(c=1 - p.c))

    def end(self):
        for copy in self.over_y:
            copy.wait_send()
        self.over_c.wait()


def pieces(rows, width, which, classes):
    out = []
    for j, name in enumerate(which):
        if name == "t":
            for k, kind in enumerate(classes["t"]):
                span = 2 * width // len(classes["t"])
                out.append((j, 0, rows // 4, k * span, span, kind))
        elif name == "d":
            for k, kind in enumerate(classes["d"]):
                out.append((j, k * rows, rows, 0, width, kind))
        else:
            for k, kind in enumerate(classes[name]):
                out.append((j, 0, rows, k * width, width, kind))
    return out


class WeightGather:
    def __init__(self, place, items, shards, outs, bounce, ssem, rsem, lsem):
        self.place = place
        self.shards, self.outs, self.bounce = shards, outs, bounce
        self.ssem, self.rsem, self.lsem = ssem, rsem, lsem
        self.plan = []
        for i, (w, r0, rn, c0, cn, kind) in enumerate(items):
            half = cn // CORES
            width = half // place.Y if kind == "D" else half
            first = c0 + place.c * half
            if kind == "D":
                first = first + place.y * width
            self.plan.append(
                dict(
                    i=i,
                    w=w,
                    kind=kind,
                    rows=pl.ds(r0, rn),
                    cols=pl.ds(pl.multiple_of(first, 128), width),
                    half=pl.ds(pl.multiple_of(c0 + place.c * half, 128), half),
                    held=bounce.at[i, pl.ds(0, rn), pl.ds(0, width)],
                )
            )

    def region(self, p, z, x, cols):
        return self.outs[p["w"]].at[z, x, p["rows"], cols]

    def load(self):
        for p in self.plan:
            p["own"] = keep(
                self.shards[p["w"]].at[p["rows"], p["cols"]], p["held"], self.lsem.at[p["i"]]
            )

    def store(self):
        place = self.place
        for p in self.plan:
            p["own"].wait()
            p["own"] = keep(
                p["held"], self.region(p, place.z, place.x, p["cols"]), self.lsem.at[p["i"]]
            )

    def post(self, p, slot, src, dst, device):
        return push(src, dst, self.ssem.at[p["i"], slot], self.rsem.at[p["i"], slot], device)

    def over_z(self, p):
        place = self.place
        src = self.shards[p["w"]].at[p["rows"], p["cols"]]
        dst = self.region(p, place.z, place.x, p["cols"])
        p["z"] = [
            self.post(p, d - 1, src, dst, place.at(z=place.next_z(d))) for d in range(1, place.Z)
        ]

    def over_x(self, p):
        place = self.place
        for copy in p["z"]:
            copy.wait_recv()
        p["own"].wait()
        part = self.region(p, pl.ds(0, place.Z), place.x, p["cols"])
        p["x"] = self.post(p, place.Z - 1, part, part, place.at(x=1 - place.x))

    def over_y(self, p):
        place = self.place
        p["x"].wait_recv()
        p["y"] = []
        if p["kind"] == "D":
            part = self.region(p, pl.ds(0, place.Z), pl.ds(0, XS), p["cols"])
            p["y"] = [
                self.post(p, place.Z - 1 + d, part, part, place.at(y=place.next_y(d)))
                for d in range(1, place.Y)
            ]

    def over_c(self, p):
        place = self.place
        for copy in p["y"]:
            copy.wait_recv()
        part = self.region(p, pl.ds(0, place.Z), pl.ds(0, XS), p["half"])
        p["c"] = self.post(p, place.Z - 1 + place.Y, part, part, place.at(c=1 - place.c))

    def finish(self, p):
        p["c"].wait()
        for copy in p["z"] + p["y"] + [p["x"]]:
            copy.wait_send()

    def stages(self):
        return [self.over_z, self.over_x, self.over_y, self.over_c, self.finish]


def gather_body(slices, shards, items, nw, *refs):
    ws, rows_in = refs[:nw], refs[nw : nw + 2]
    outs, rows_out = refs[nw + 2 : 2 * nw + 2], refs[2 * nw + 2 : 2 * nw + 4]
    bounce, ssem, rsem, lsem, b0, b1, sseq, rseq, lseq = refs[2 * nw + 4 :]
    place = Place(slices, shards)
    gather = WeightGather(place, items, ws, outs, bounce, ssem, rsem, lsem)
    rows = [
        RowGather(place, src, out, b, sseq.at[k], rseq.at[k], lseq.at[k])
        for k, (src, out, b) in enumerate(zip(rows_in, rows_out, (b0, b1)))
    ]
    gather.load()
    for r in rows:
        r.load()
    greet(place)
    gather.over_z(gather.plan[0])
    rows[0].start()
    rows[1].start()
    gather.store()
    stages = gather.stages()
    first = gather.plan[0]
    stages[0] = lambda p: None if p is first else gather.over_z(p)
    pipeline(gather.plan, stages)
    for r in rows:
        r.middle()
    for r in rows:
        r.end()


def gather_all(slices, shards, width, ws, rows_in):
    Y, Z = slices // CORES, shards // XS
    rows = ws[1].shape[0]
    items = pieces(rows, width, "tqoud", GATHER_CLASS)
    n, nw = len(items), len(ws)
    widest = max(cn // CORES // (Y if kind == "D" else 1) for _, _, _, _, cn, kind in items)
    out = pl.pallas_call(
        functools.partial(gather_body, slices, shards, items, nw),
        out_shape=[jax.ShapeDtypeStruct((Z, XS) + w.shape, w.dtype) for w in ws]
        + [jax.ShapeDtypeStruct((Y, CORES) + r.shape, r.dtype) for r in rows_in],
        in_specs=[ANY] * (nw + 2),
        out_specs=[ANY] * (nw + 2),
        scratch_shapes=[
            pltpu.VMEM((n, rows, widest), BF),
            DMA((n, Z + Y)),
            DMA((n, Z + Y)),
            DMA((n,)),
        ]
        + [pltpu.VMEM(r.shape, r.dtype) for r in rows_in]
        + [DMA((2, Y)), DMA((2, Y)), DMA((2,))],
        compiler_params=pltpu.CompilerParams(
            collective_id=0, has_side_effects=True, vmem_limit_bytes=VMEM_ALL
        ),
    )(*ws, *rows_in)
    full = [g.reshape(-1, g.shape[-1]) for g in out[:nw]]
    return full, [g.reshape((slices,) + r.shape) for g, r in zip(out[nw:], rows_in)]


def add_into(dst, src, rn):
    lead = dst.shape[:-2]

    def step(k, _):
        idx, rest = [], k
        for size in reversed(lead[1:]):
            idx.append(lax.rem(rest, size))
            rest = lax.div(rest, size)
        idx = tuple(reversed(idx + [rest]))
        a, b = dst.at[idx], src.at[idx]
        rows = pl.ds(0, rn)
        a[rows, :] = (a[rows, :].astype(jnp.float32) + b[rows, :].astype(jnp.float32)).astype(BF)
        return 0

    lax.fori_loop(0, math.prod(lead), step, 0)


class GradSum:
    def __init__(self, place, items, grads, outs, acc, rc, ry, rx, rz, fin, rf, lsem, ssem, rsem):
        self.place, self.grads, self.outs = place, grads, outs
        self.acc, self.rc, self.ry, self.rx, self.rz = acc, rc, ry, rx, rz
        self.fin, self.rf = fin, rf
        self.lsem, self.ssem, self.rsem = lsem, ssem, rsem
        self.wide = acc.shape[-1]
        self.plan = []
        for i, (w, r0, rn, c0, cn, kind) in enumerate(items):
            p = dict(i=i, w=w, kind=kind, rn=rn, c0=c0, half=cn // CORES)
            p.update(rows=pl.ds(r0, rn), vr=pl.ds(0, rn), sends=[])
            self.plan.append(p)

    def post(self, p, slot, src, dst, device):
        copy = push(src, dst, self.ssem.at[p["i"], slot], self.rsem.at[p["i"], slot], device)
        p["sends"].append(copy)
        return copy

    def cols(self, p, core, part=None):
        first = p["c0"] + core * p["half"]
        if part is None:
            return pl.ds(pl.multiple_of(first, 128), p["half"])
        return pl.ds(pl.multiple_of(first + part * self.wide, 128), self.wide)

    def parts(self, p):
        return [self.place.y] if p["kind"] == "D" else list(range(self.place.Y))

    def over_c(self, p):
        place, i, vr = self.place, p["i"], p["vr"]
        g = self.grads[p["w"]]
        first = place.Z + place.Y + place.Y
        p["own"], p["c"] = [], []
        for part in range(place.Y):
            p["own"].append(
                keep(
                    g.at[:, :, p["rows"], self.cols(p, place.c, part)],
                    self.acc.at[i, part, :, :, vr, :],
                    self.lsem.at[i, part],
                )
            )
            p["c"].append(
                self.post(
                    p,
                    first + part,
                    g.at[:, :, p["rows"], self.cols(p, 1 - place.c, part)],
                    self.rc.at[i, part, :, :, vr, :],
                    place.at(c=1 - place.c),
                )
            )

    def over_y(self, p):
        place, i, vr = self.place, p["i"], p["vr"]
        for copy in p["own"]:
            copy.wait()
        for copy in p["c"]:
            copy.wait_recv()
        for part in range(place.Y):
            add_into(self.acc.at[i, part], self.rc.at[i, part], p["rn"])
        p["y"] = []
        if p["kind"] == "D":
            for d in range(1, place.Y):
                y = place.next_y(d)
                p["y"].append(
                    self.post(
                        p,
                        d,
                        self.acc.at[i, y, :, :, vr, :],
                        self.ry.at[i, d - 1, :, :, vr, :],
                        place.at(y=y),
                    )
                )

    def over_x(self, p):
        place, i, vr = self.place, p["i"], p["vr"]
        for d, copy in enumerate(p["y"]):
            copy.wait_recv()
            add_into(self.acc.at[i, place.y], self.ry.at[i, d], p["rn"])
        other = 1 - place.x
        if p["kind"] == "D":
            src, dst = self.acc.at[i, place.y, :, other, vr, :], self.rx.at[i, 0, :, vr, :]
        else:
            src, dst = self.acc.at[i, :, :, other, vr, :], self.rx.at[i, :, :, vr, :]
        p["x"] = self.post(p, place.Y, src, dst, place.at(x=other))

    def over_z(self, p):
        place, i, vr = self.place, p["i"], p["vr"]
        p["x"].wait_recv()
        for k, part in enumerate(self.parts(p)):
            add_into(self.acc.at[i, part, :, place.x], self.rx.at[i, k], p["rn"])
        p["z"] = []
        for d in range(1, place.Z):
            z = place.next_z(d)
            if p["kind"] == "D":
                src = self.acc.at[i, place.y, z, place.x, vr, :]
                dst = self.rz.at[i, d - 1, 0, vr, :]
            else:
                src = self.acc.at[i, :, z, place.x, vr, :]
                dst = self.rz.at[i, d - 1, :, vr, :]
            p["z"].append(self.post(p, place.Y + d, src, dst, place.at(z=z)))

    def region(self, p, core, part=None):
        return self.outs[p["w"]].at[p["rows"], self.cols(p, core, part)]

    def back_y(self, p):
        place, i, vr = self.place, p["i"], p["vr"]
        for copy in p["z"]:
            copy.wait_recv()
        for k, part in enumerate(self.parts(p)):
            total = self.acc[i, part, place.z, place.x, vr, :].astype(jnp.float32)
            for d in range(1, place.Z):
                total = total + self.rz[i, d - 1, k, vr, :].astype(jnp.float32)
            if p["kind"] == "D":
                self.fin[i, 0, vr, :] = total.astype(BF)
            else:
                self.rf[i, place.y, part, vr, :] = total.astype(BF)
        first = place.Z + place.Y - 1
        p["f"], p["st"] = [], []
        if p["kind"] == "D":
            src, dst = self.fin.at[i, 0, vr, :], self.region(p, place.c, place.y)
            p["st"].append(keep(src, dst, self.lsem.at[i, 0]))
        else:
            src = dst = self.rf.at[i, place.y, :, vr, :]
        for d in range(1, place.Y):
            p["f"].append(self.post(p, first + d, src, dst, place.at(y=place.next_y(d))))

    def back_c(self, p):
        place, i, vr = self.place, p["i"], p["vr"]
        for copy in p["f"]:
            copy.wait_recv()
        if p["kind"] == "C":
            for part in range(place.Y):
                total = self.rf[i, 0, part, vr, :].astype(jnp.float32)
                for y in range(1, place.Y):
                    total = total + self.rf[i, y, part, vr, :].astype(jnp.float32)
                self.fin[i, part, vr, :] = total.astype(BF)
                src, dst = self.fin.at[i, part, vr, :], self.region(p, place.c, part)
                p["st"].append(keep(src, dst, self.lsem.at[i, part]))
        for copy in p["st"]:
            copy.wait()
        part = self.region(p, place.c)
        p["e"] = self.post(p, 0, part, part, place.at(c=1 - place.c))

    def finish(self, p):
        p["e"].wait_recv()
        for copy in p["sends"]:
            copy.wait_send()

    def stages(self):
        return [
            self.over_c,
            self.over_y,
            self.over_x,
            self.over_z,
            self.back_y,
            self.back_c,
            self.finish,
        ]


def sum_scratch(slices, shards, items, rows):
    Y, Z = slices // CORES, shards // XS
    n, wide = len(items), items[0][4] // CORES // Y
    return [
        pltpu.VMEM((n, Y, Z, XS, rows, wide), BF),
        pltpu.VMEM((n, Y, Z, XS, rows, wide), BF),
        pltpu.VMEM((n, Y - 1, Z, XS, rows, wide), BF),
        pltpu.VMEM((n, Y, Z, rows, wide), BF),
        pltpu.VMEM((n, Z - 1, Y, rows, wide), BF),
        pltpu.VMEM((n, Y, rows, wide), BF),
        pltpu.VMEM((n, Y, Y, rows, wide), BF),
        DMA((n, Y)),
        DMA((n, Z + 3 * Y)),
        DMA((n, Z + 3 * Y)),
    ]


def sum_body(slices, shards, items, nw, nr, *refs):
    grads, rows_in = refs[:nw], refs[nw : nw + nr]
    outs, rows_out = refs[nw + nr : 2 * nw + nr], refs[2 * nw + nr : 2 * (nw + nr)]
    scratch = refs[2 * (nw + nr) :]
    place = Place(slices, shards)
    sums = GradSum(place, items, grads, outs, *scratch[:10])
    rows = []
    for k in range(nr):
        b, s, r, m = scratch[10 + 4 * k : 14 + 4 * k]
        rows.append(RowGather(place, rows_in[k], rows_out[k], b, s, r, m.at[0]))
    for r in rows:
        r.load()
    greet(place)
    for r in rows:
        r.start()
    pipeline(sums.plan, sums.stages())
    for r in rows:
        r.middle()
    for r in rows:
        r.end()


def sum_grads(slices, shards, width, which, grads, rows_in, cid):
    Y, Z = slices // CORES, shards // XS
    rows = width // shards
    items = pieces(rows, width, which, SUM_CLASS)
    nw, nr = len(grads), len(rows_in)
    grads = [g.reshape(Z, XS, -1, g.shape[1]) for g in grads]
    extra = []
    for r in rows_in:
        extra += [pltpu.VMEM(r.shape, r.dtype), DMA((Y,)), DMA((Y,)), DMA((1,))]
    out = pl.pallas_call(
        functools.partial(sum_body, slices, shards, items, nw, nr),
        out_shape=[jax.ShapeDtypeStruct(g.shape[2:], BF) for g in grads]
        + [jax.ShapeDtypeStruct((Y, CORES) + r.shape, r.dtype) for r in rows_in],
        in_specs=[ANY] * (nw + nr),
        out_specs=[ANY] * (nw + nr),
        scratch_shapes=sum_scratch(slices, shards, items, rows) + extra,
        compiler_params=pltpu.CompilerParams(
            collective_id=cid, has_side_effects=True, vmem_limit_bytes=VMEM_ALL
        ),
    )(*grads, *rows_in)
    return out[:nw], [g.reshape((slices,) + r.shape) for g, r in zip(out[nw:], rows_in)]


def dot(a, b, ca, cb):
    return lax.dot_general(a, b, (((ca,), (cb,)), ((), ())), preferred_element_type=jnp.float32)


def swap_halves(v):
    lane = lax.broadcasted_iota(jnp.int32, v.shape, 1)
    left = pltpu.roll(v, v.shape[1] - HD // 2, 1)
    right = pltpu.roll(v, HD // 2, 1)
    return jnp.where(lax.rem(lane, HD) < HD // 2, left, right)


def forward_block(qkv, seg_col, seg_row, mixed, logsum, h, rows):
    lanes = slice(h * HD, (h + 1) * HD)
    s = dot(qkv[1, :, lanes], qkv[0, rows, lanes], 1, 1) * (LOG2E * HD**-0.5)
    s = jnp.where(seg_col[...] == seg_row[:, rows], s, NEG)
    peak = jnp.max(s, axis=0, keepdims=True)
    expo = jnp.exp2(s - peak)
    total = jnp.sum(expo, axis=0, keepdims=True)
    out = dot(expo.astype(BF), qkv[2, :, lanes], 0, 0)
    mixed[rows, lanes] = (out / total.T).astype(BF)
    logsum[h : h + 1, rows] = peak + jnp.log2(total)


def backward_block(qkv, mixed, logsum, g, seg_col, seg_row, dk, dv, dq, h, rows):
    lanes = slice(h * HD, (h + 1) * HD)
    q, gb = qkv[0, rows, lanes], g[rows, lanes]
    k, v = qkv[1, :, lanes], qkv[2, :, lanes]
    prod = gb.astype(jnp.float32) * mixed[rows, lanes].astype(jnp.float32)
    delta = jnp.sum(prod, axis=1, keepdims=True).T
    s = dot(k, q, 1, 1) * (LOG2E * HD**-0.5)
    same = seg_col[...] == seg_row[:, rows]
    probs = jnp.where(same, jnp.exp2(s - logsum[h : h + 1, rows]), 0.0)
    ds = (probs * (dot(v, gb, 1, 1) - delta)).astype(BF)
    dv[:, lanes] += dot(probs.astype(BF), gb, 1, 0)
    dk[:, lanes] += dot(ds, q, 1, 0)
    dq[rows, lanes] = dot(ds, k, 0, 0)


def forward_body(heads, block, qkv, seg_col, seg_row, mixed, logsum):
    for h in range(heads):

        def step(i, _):
            rows = pl.ds(pl.multiple_of(i * block, block), block)
            forward_block(qkv, seg_col, seg_row, mixed, logsum, h, rows)
            return 0

        lax.fori_loop(0, seg_col.shape[0] // block, step, 0)


def backward_body(
    heads, block, qkv, mixed, logsum, g, seg_col, seg_row, cos, sin, out, dk, dv, dq
):
    dk[...] = jnp.zeros_like(dk)
    dv[...] = jnp.zeros_like(dv)
    steps = seg_col.shape[0] // block
    for h in range(heads):

        def step(i, _):
            rows = pl.ds(pl.multiple_of(i * block, block), block)
            backward_block(qkv, mixed, logsum, g, seg_col, seg_row, dk, dv, dq, h, rows)
            return 0

        lax.fori_loop(0, steps, step, 0)

    def finish(i, _):
        rows = pl.ds(pl.multiple_of(i * block, block), block)
        c, s = cos[rows, :], sin[rows, :]
        for j, d in enumerate((dq, dk)):
            for t in range(heads * HD // 128):
                w = slice(t * 128, (t + 1) * 128)
                v = d[rows, w] * (HD**-0.5)
                out[j, rows, w] = (v * c - swap_halves(v) * s).astype(BF)
        out[2, rows, :] = dv[rows, :].astype(BF)
        return 0

    lax.fori_loop(0, steps, finish, 0)


def attention_forward(qkv, seg_col, seg_row, block=512):
    _, group, width = qkv.shape
    heads = width // HD
    return pl.pallas_call(
        functools.partial(forward_body, heads, block),
        out_shape=(
            jax.ShapeDtypeStruct((group, width), BF),
            jax.ShapeDtypeStruct((heads, group), jnp.float32),
        ),
        in_specs=[VM] * 3,
        out_specs=(VM, VM),
        compiler_params=pltpu.CompilerParams(vmem_limit_bytes=VMEM_ALL),
    )(qkv, seg_col, seg_row)


def attention_backward(qkv, mixed, logsum, g, seg_col, seg_row, cos, sin, block=512):
    _, group, width = qkv.shape
    total = pltpu.VMEM((group, width), jnp.float32)
    return pl.pallas_call(
        functools.partial(backward_body, width // HD, block),
        out_shape=jax.ShapeDtypeStruct((3, group, width), BF),
        in_specs=[VM] * 8,
        out_specs=VM,
        scratch_shapes=[total] * 3,
        compiler_params=pltpu.CompilerParams(vmem_limit_bytes=VMEM_ALL),
    )(qkv, mixed, logsum, g, seg_col, seg_row, cos, sin)


def project_body(h, w, cos, sin, out):
    y = jnp.dot(h[...], w[...], preferred_element_type=jnp.float32)
    turned = (pl.program_id(0) < 2).astype(jnp.float32)
    c = cos[...] * turned + (1.0 - turned)
    s = sin[...] * turned
    for t in range(y.shape[1] // 128):
        w_ = slice(t * 128, (t + 1) * 128)
        out[0, :, w_] = (y[:, w_] * c + swap_halves(y[:, w_]) * s).astype(BF)


def project(h, w, cos, sin, block=512):
    rows, width = h.shape
    const = lambda j, n: (0, 0)
    per = width // block
    return pl.pallas_call(
        project_body,
        grid=(3, per),
        out_shape=jax.ShapeDtypeStruct((3, rows, width), BF),
        in_specs=[
            pl.BlockSpec((rows, width), const),
            pl.BlockSpec((width, block), lambda j, n: (0, j * per + n)),
            pl.BlockSpec((rows, 128), const),
            pl.BlockSpec((rows, 128), const),
        ],
        out_specs=pl.BlockSpec((1, rows, block), lambda j, n: (j, 0, n)),
        compiler_params=pltpu.CompilerParams(vmem_limit_bytes=VMEM_ALL),
    )(h, w, cos, sin)


def time_embedding(steps):
    half = TEMB // 2
    freqs = jnp.exp(-math.log(BASE) * jnp.arange(half, dtype=jnp.float32) / half)
    angles = steps.astype(jnp.float32)[:, None] * freqs[None, :]
    return jnp.concatenate([jnp.sin(angles), jnp.cos(angles)], axis=-1)


def layout(lens, places):
    ends = jnp.cumsum(lens)
    starts = ends - lens
    member = (places[:, None] >= starts[None, :]) & (places[:, None] < ends[None, :])
    labels = jnp.arange(NSEQ, dtype=jnp.int32)
    segment = jnp.sum(jnp.where(member, labels[None, :], 0), axis=1)
    offset = places - jnp.sum(jnp.where(member, starts[None, :], 0), axis=1)
    return (member.astype(jnp.float32), segment, offset)


def turn_tables(offset):
    half = HD // 2
    freqs = jnp.exp(-math.log(BASE) * jnp.arange(half, dtype=jnp.float32) * 2.0 / HD)
    angles = offset.astype(jnp.float32)[:, None] * freqs[None, :]
    c, s = jnp.cos(angles), jnp.sin(angles)
    return jnp.concatenate([c] * 4, axis=1), jnp.concatenate([-s, s, -s, s], axis=1)


def norm_mod(values, scale):
    centre = jnp.mean(values, axis=-1, keepdims=True)
    centred = values - centre
    spread = jnp.mean(centred * centred, axis=-1, keepdims=True)
    return centred * lax.rsqrt(spread + EPS) * (1.0 + scale)


def pick_rows(data, wanted, labels):
    pick = (wanted[:, None] == labels[None, :]).astype(BF)
    return jnp.dot(pick, data.reshape(-1, data.shape[-1]), preferred_element_type=jnp.float32)


def on_device(tokens, lengths, time_steps, order, w_time, w_qkv, w_out, w_up, w_down, cotangent):
    rows, width = tokens.shape[1:]
    slices, shards = lax.axis_size("seq"), lax.axis_size("fsdp")
    group = rows * slices
    lens, places = lengths[0], order[0]
    gathered, (order_all, cot_all) = gather_all(
        slices, shards, width, [w_time, w_qkv, w_out, w_up, w_down], [order, cotangent[0]]
    )
    f_time, f_qkv, f_out, f_up, f_down = gathered
    order_all = order_all.reshape(group)

    member, _, offset = layout(lens, places)
    _, segment_all, offset_all = layout(lens, order_all)
    seg_col, seg_row = segment_all[:, None], segment_all[None, :]
    emb = time_embedding(time_steps[0]).astype(BF)
    scales_seq = jnp.dot(emb, f_time, preferred_element_type=jnp.float32)
    scales = jnp.dot(member, scales_seq, precision=lax.Precision.HIGHEST)
    scale_one, scale_two = scales[:, :width], scales[:, width:]
    inputs = tokens[0].astype(jnp.float32)
    normed_one, pull_one = jax.vjp(norm_mod, inputs, scale_one)
    h_one = normed_one.astype(BF)

    cos, sin = turn_tables(offset)
    packed = project(h_one, f_qkv, cos, sin)
    heads_qkv = lax.all_to_all(packed, "seq", split_axis=2, concat_axis=1, tiled=True)
    mixed_heads, logsum = attention_forward(heads_qkv, seg_col, seg_row)
    mixed = lax.all_to_all(mixed_heads, "seq", split_axis=0, concat_axis=1, tiled=True)

    x_two = inputs + jnp.dot(mixed, f_out, preferred_element_type=jnp.float32)
    normed_two, pull_two = jax.vjp(norm_mod, x_two, scale_two)
    h_two = normed_two.astype(BF)
    up = jnp.dot(h_two, f_up, preferred_element_type=jnp.float32)
    activated, pull_gelu = jax.vjp(jax.nn.gelu, up)
    hidden = activated.astype(BF)
    result = (x_two + jnp.dot(hidden, f_down, preferred_element_type=jnp.float32)).astype(BF)

    d_result = pick_rows(cot_all, places, jnp.arange(group, dtype=jnp.int32))
    d_low = d_result.astype(BF)
    grad_down = dot(hidden, d_low, 0, 0).astype(BF)
    d_up = pull_gelu(dot(d_low, f_down, 1, 1))[0].astype(BF)
    grad_up = dot(h_two, d_up, 0, 0).astype(BF)
    d_xpart, d_scale_two = pull_two(dot(d_up, f_up, 1, 1))
    d_xtwo = d_result + d_xpart
    d_attn = d_xtwo.astype(BF)
    grad_out = dot(mixed, d_attn, 0, 0).astype(BF)
    d_mixed = dot(d_attn, f_out, 1, 1).astype(BF)

    d_heads = lax.all_to_all(d_mixed, "seq", split_axis=1, concat_axis=0, tiled=True)
    cos_all, sin_all = turn_tables(offset_all)
    d_qkv_heads = attention_backward(
        heads_qkv, mixed_heads, logsum, d_heads, seg_col, seg_row, cos_all, sin_all
    )
    d_packed = lax.all_to_all(d_qkv_heads, "seq", split_axis=1, concat_axis=2, tiled=True)
    d_qkv = d_packed.transpose(1, 0, 2).reshape(rows, 3 * width)
    grad_qkv = dot(h_one, d_qkv, 0, 0).astype(BF)
    d_xone, d_scale_one = pull_one(dot(d_qkv, f_qkv, 1, 1))
    input_grad = d_xtwo + d_xone
    d_scales = lax.dot_general(
        member,
        jnp.concatenate([d_scale_one, d_scale_two], axis=1),
        (((0,), (0,)), ((), ())),
        precision=lax.Precision.HIGHEST,
        preferred_element_type=jnp.float32,
    )
    grad_time = lax.dot_general(
        emb.astype(jnp.float32),
        d_scales,
        (((0,), (0,)), ((), ())),
        precision=lax.Precision.HIGHEST,
        preferred_element_type=jnp.float32,
    ).astype(BF)

    grads, (result_all,) = sum_grads(
        slices, shards, width, "duoqt",
        [grad_down, grad_up, grad_out, grad_qkv, grad_time], [result], 1,
    )
    s_down, s_up, s_out, s_qkv, s_time = [g.astype(jnp.float32) for g in grads]
    mine = lax.axis_index("seq") * rows + jnp.arange(rows, dtype=jnp.int32)
    output = pick_rows(result_all, mine, order_all).astype(BF)
    return (output[None], input_grad[None], s_time, s_qkv, s_out, s_up, s_down)


def solution(mesh):
    row, tok, mat = P("fsdp", None), P("fsdp", "seq", None), P("fsdp", None)
    return jax.shard_map(
        on_device,
        mesh=mesh,
        in_specs=(tok, row, row, P("fsdp", "seq"), mat, mat, mat, mat, mat, tok),
        out_specs=(tok, tok, mat, mat, mat, mat, mat),
        check_vma=False,
    )
```

time: 1460 us -> 615 us (0.42)
  waiting for transfers between devices: 870 us -> 62.5 us
  Pallas kernels: 0 us -> 388 us
  local copies, waits for them, and re-layouts: 174 us -> 35.1 us
  matrix products: 213 us -> 75.5 us
  blocking collectives: 70.8 us -> 0 us
  other arithmetic: 65.3 us -> 29.7 us
  loops' own time: 27.9 us -> 0 us
    reduce_scatter x5 -> x0, waiting for transfers between devices: 443 us -> none  [weight_grad(): lax.psum_scatter(term().astype(jnp.bfloat16), 'fsdp', scatter_dimension=0...]
    pallas_call x0 -> x5, Pallas kernels: none -> 388 us  [the longest x1 170 us: sum_grads(): pl.pallas_call(functools.partial(sum_body, slices, shards, items, nw, nr)...]
    all_gather x7 -> x0, waiting for transfers between devices: 338 us -> none  [the longest x5 310 us: weight_rows(): lax.all_gather(weight, 'fsdp', axis=0, tiled=True)]
    dot_general x102 -> x17, matrix products: 213 us -> 75.5 us  [the longest x8 48.9 us: dot(): lax.dot_general(a, b, (((ca,), (cb,)), ((), ())), preferred_element_type=...]
    psum x1 -> x0, waiting for transfers between devices: 69.2 us -> none  [weight_grad(): shard = lax.psum(shard.astype(jnp.bfloat16), 'seq').astype(jnp.float32)]
    dynamic_slice x96 -> x0, local copies, waits for them, and re-layouts: 64.7 us -> none  [the longest x24 30.8 us: slice_cols(): return lax.dynamic_slice_in_dim(matrix, start, HD, 1)]
    dynamic_update_slice x52 -> x0, local copies, waits for them, and re-layouts: 52.4 us -> none  [the longest x24 45.4 us: head_backward(): lax.scan(step, (zeros, zeros), jnp.arange(group // block))]
    all_to_all x3 -> x4, waiting for transfers between devices: 15.3 us -> 62.5 us  [the longest x1 30.5 us: on_device(): lax.all_to_all(packed, 'seq', split_axis=2, concat_axis=1, tiled=True)]
  transfers between devices with their start and end apart: 16 -> 4, of which waited for: 12 -> 4; matrix products, arithmetic and copies ran while one was open for 28% -> 6% of each run, Pallas kernels for 0% -> 0%
where the time goes in v1:
time: 615 us; the launch traced here: 609 us
  Pallas kernels  388 us (63%)
  matrix products  75.5 us (12%)
  waiting for transfers between devices  62.5 us (10%)
  local copies, waits for them, and re-layouts  35.1 us (6%)
  other arithmetic  29.7 us (5%)
  starting transfers between devices  17.2 us (3%)
    pallas_call x1, Pallas kernels, sum_grads(): pl.pallas_call(functools.partial(sum_body, slices, shards, items, nw, nr)...  170 us
    pallas_call x1, Pallas kernels, gather_all(): pl.pallas_call(functools.partial(gather_body, slices, shards, items, nw),...  141 us
    dot_general x8, matrix products, dot(): lax.dot_general(a, b, (((ca,), (cb,)), ((), ())), preferred_element_type=...  48.9 us
    pallas_call x1, Pallas kernels, attention_backward(): pl.pallas_call(functools.partial(backward_body, width // HD, block), out_...  37.8 us
    all_to_all x1, waiting for transfers between devices, on_device(): lax.all_to_all(packed, 'seq', split_axis=2, concat_axis=1, tiled=True)  30.5 us
    pallas_call x1, Pallas kernels, attention_forward(): pl.pallas_call(functools.partial(forward_body, heads, block), out_shape=(...  30.2 us
    all_to_all x1, waiting for transfers between devices, on_device(): lax.all_to_all(d_qkv_heads, 'seq', split_axis=1, concat_axis=2, tiled=True)  24 us
  transfers between devices with their start and end apart: 4, of which 4 were waited for; matrix products, arithmetic and copies ran while one was open for 6% of the time, Pallas kernels for 0%

profile of v1, /device:TPU:0, one launch (start us, length us, event | category | flops | bytes accessed | tf_op | source)
XLA Modules:
  0.0 609.2 jit_solution(97053453076906075)
XLA Ops:
  5.4 141.0 %shard_map.153 = (bf16[4,2,32,2048]{3,2,1,0:T(8,128)(2,1)}, bf16[4,2,128,3072]{3,2,1,0:T(8,128)(2,1)}, bf16[4,2,128,1024]{3,2,1,0:T(8,128)(2,1)}, bf16[4,2,128,4...) custom-call(bf16[32,2048]{1,0:T(8,128)(2,1)} %refs_0_.1, ...), custom_call_target="tpu_custom_call" | custom-call | tf_op jit(solution)/shard_map/pallas_call | solution.py:262
  154.9 9.1 %shard_map.154 = bf16[3,384,1024]{2,1,0:T(8,128)(2,1)} custom-call(bf16[384,1024]{1,0:T(8,128)(2,1)} %fusion.22.h, bf16[1024,3072]{1,0:T(8,128)(2,1)} %bitcast.107, f32[384,128]{1,0:T(8,128)} %get-tuple-element.59.cos, f32[384,128]{1,0:T(8,128)} %get-tuple-element.60.sin), custom_call_target="tpu_custom_call" | custom-call | tf_op jit(solution)/shard_map/pallas_call | solution.py:642
  164.0 5.8 copy.51
  169.8 4.1 all-to-all-start
  175.9 4.4 fusion.43
  180.3 30.5 %all-to-all-done = bf16[3,384,1024]{1,0,2:T(4,128)(2,1)S(1)} async-done(((bf16[3,384,1024]{1,0,2:T(4,128)(2,1)}), bf16[3,384,1024]{1,0,2:T(4,128)(2,1)S(1)}, u32[]{:S(2)}, u32[]{:S(2)}) %all-to-all-start) | async-done | bytes 2359328 | tf_op jit(solution)/shard_map/all_to_all | solution.py:718
  210.8 4.0 copy.52
  214.8 30.2 %shard_map.155 = (bf16[1536,256]{1,0:T(8,128)(2,1)}, f32[4,1536]{1,0:T(4,128)}) custom-call(bf16[3,1536,256]{2,1,0:T(8,128)(2,1)} %bitcast.98, s32[1536,1]{1,0:T(8,128)} %broadcast_in_dim.80.seg_col, s32[1,1536]{1,0:T(1,128)} %broadcast_in_dim.73.seg_row), custom_call_target="tpu_custom_call" | custom-call | tf_op jit(solution)/shard_map/pallas_call | solution.py:603
  247.4 4.1 all-to-all-start.1
  254.6 3.4 fusion.11
  258.0 5.1 all-to-all-done.1
  263.1 3.0 fusion.57
  266.8 6.0 fusion.58
  272.8 2.6 copy-done.51
  275.4 5.0 add_convert_fusion.refs_5_
  280.4 10.3 %fusion.6 = bf16[384,4096]{1,0:T(8,128)(2,1)S(1)} fusion(f32[384,4096]{1,0:T(8,128)} %copy-done.51, bf16[4096,1024]{1,0:T(8,128)(2,1)} %bitcast.127, f32[384,1024]{1,0:T(8,128)S(1)} %fusion.11), kind=kOutput, calls=%fused_computation.10 | convolution fusion | flops 3253075968 | bytes 19398656 | tf_op jit(solution)/shard_map/dot_general | solution.py:523
  290.8 3.8 multiply_reduce_fusion
  300.0 4.2 all-to-all-start.2
  304.2 8.7 %convolution_convert_fusion = bf16[1024,4096]{1,0:T(8,128)(2,1)} fusion(bf16[384,1024]{1,0:T(8,128)(2,1)S(1)} %multiply_convert_fusion.1, bf16[384,4096]{1,0:T(8,128)(2,1)} %copy-done.52), kind=kOutput, calls=%fused_computation.2 | convolution fusion | flops 3225419776 | bytes 12320768 | tf_op jit(solution)/shard_map/dot_general | solution.py:523
  312.9 3.0 all-to-all-done.2
  315.9 37.8 %shard_map.156 = bf16[3,1536,256]{2,1,0:T(8,128)(2,1)} custom-call(bf16[3,1536,256]{2,1,0:T(8,128)(2,1)} %bitcast.99, bf16[1536,256]{1,0:T(8,128)(2,1)} %get-tuple-element.25.mixed, f32[4,1536]{1,0:T(4,128)} %get-tuple-element.30.logsum, bf16[1536,256]{1,0:T(8,128)(2,1)} %bitcast.25.g, s32[1536,1]{1,0:T(8,128)} %broadcast_in_dim.80.seg_col, ...), custom_call_target="tpu_custom_call" | custom-call | tf_op jit(solution)/shard_map/pallas_call | solution.py:618
  353.7 5.7 copy.58
  359.3 4.8 all-to-all-start.3
  364.2 2.6 convolution_convert_fusion.4
  366.7 10.4 %convolution_convert_fusion.1 = bf16[4096,1024]{1,0:T(8,128)(2,1)} fusion(f32[384,1024]{1,0:T(8,128)S(1)} %copy-done.20, f32[384,4096]{1,0:T(8,128)} %copy-done.51), kind=kOutput, calls=%fused_computation.3 | convolution fusion | flops 3239968768 | bytes 16252928 | tf_op jit(solution)/shard_map/dot_general | solution.py:523
  377.1 24.0 %all-to-all-done.3 = bf16[3,1536,256]{2,0,1:T(4,128)(2,1)} async-done(((bf16[3,1536,256]{2,0,1:T(4,128)(2,1)}), bf16[3,1536,256]{2,0,1:T(4,128)(2,1)}, u32[]{:S(2)}, u32[]{:S(2)}) %all-to-all-start.3) | async-done | bytes 2359328 | tf_op jit(solution)/shard_map/all_to_all | solution.py:746
  401.1 3.6 copy.59
  404.7 4.5 copy.60
  409.2 6.7 %fusion.24 = (f32[384]{0:T(512)S(1)}, f32[384,1024]{1,0:T(8,128)S(1)}) fusion(bf16[1,384,1024]{2,1,0:T(8,128)(2,1)} %param.10, f32[384]{0:T(512)S(1)} %copy-done.31, f32[384,2048]{1,0:T(8,128)S(1)} %copy-done.2, bf16[384,3072]{0,1:T(8,128)(2,1)} %bitcast.112, bf16[1024,3072]{1,0:T(8,128)(2,1)} %bitcast.108), kind=kOutput, calls=%fused_computation.37 | convolution fusion | flops 2418277888 | bytes 12585984 | tf_op jit(solution)/shard_map/dot_general | solution.py:523
  416.0 5.4 convolution_convert_fusion.2
  427.1 169.8 %shard_map.157 = (bf16[512,1024]{1,0:T(8,128)(2,1)}, bf16[128,4096]{1,0:T(8,128)(2,1)}, bf16[128,1024]{1,0:T(8,128)(2,1)}, bf16[128,3072]{1,0:T(8,128)(2,1)}, bf...) custom-call(bf16[4,2,512,1024]{3,2,1,0:T(8,128)(2,1)} %bitcast.103, bf16[4,2,128,4096]{3,2,1,0:T(8,128)(2,1)} %bitcast.102, ...), custom_call_target="tpu_custom_call" | custom-call | tf_op jit(solution)/shard_map/pallas_call | solution.py:508
  596.9 2.8 convert_element_type.115
  (163 shorter events, 41.6 us)
Async XLA Ops:
  146.4 3.8 copy-start.3
  147.9 3.8 copy-start.38
  147.9 3.8 copy-start.48
  150.4 4.5 copy-start.30
  169.8 4.2 copy-start.46
  169.8 4.2 copy-start.40
  169.8 4.2 copy-start.43
  169.8 6.1 %copy-start.49 = (f32[32]{0:T(128)S(1)}, f32[32]{0:T(128)}, u32[]{:S(2)}) copy-start(f32[32]{0:T(128)} %multiply_exponential_fusion) | copy-start | bytes 388
  169.8 41.0 %all-to-all-start = ((bf16[3,384,1024]{1,0,2:T(4,128)(2,1)}), bf16[3,384,1024]{1,0,2:T(4,128)(2,1)S(1)}, u32[]{:S(2)}, u32[]{:S(2)}) async-start(bf16[3,384,1024]{1,0,2:T(4,128)(2,1)} %copy.51), calls=%async_computation | async-start | bytes 6291456 | tf_op jit(solution)/shard_map/all_to_all | solution.py:718
  174.0 40.8 %copy-start.25 = (s32[1536]{0:T(1024)}, s32[1536]{0:T(1024)S(1)}, u32[]{:S(2)}) copy-start(s32[1536]{0:T(1024)S(1)} %eq.29) | copy-start | bytes 18436
  245.0 6.5 %copy-start.14 = (f32[1536,32]{1,0:T(8,128)S(1)}, f32[1536,32]{1,0:T(8,128)}, u32[]{:S(2)}) copy-start(f32[1536,32]{1,0:T(8,128)} %get-tuple-element.45) | copy-start | bytes 589828
  245.0 6.6 %copy-start.15 = (f32[1536,32]{1,0:T(8,128)S(1)}, f32[1536,32]{1,0:T(8,128)}, u32[]{:S(2)}) copy-start(f32[1536,32]{1,0:T(8,128)} %get-tuple-element.46) | copy-start | bytes 589828
  245.0 6.6 %copy-start.16 = (f32[1536,32]{1,0:T(8,128)S(1)}, f32[1536,32]{1,0:T(8,128)}, u32[]{:S(2)}) copy-start(f32[1536,32]{1,0:T(8,128)} %get-tuple-element.47) | copy-start | bytes 589828
  247.4 15.7 %all-to-all-start.1 = ((bf16[4,384,256]{1,2,0:T(8,128)(2,1)}), bf16[4,384,256]{1,2,0:T(8,128)(2,1)S(1)}, u32[]{:S(2)}, u32[]{:S(2)}) async-start(bf16[4,384,256]{1,2,0:T(8,128)(2,1)} %copy.54), calls=%async_computation.1 | async-start | bytes 1572864 | tf_op jit(solution)/shard_map/all_to_all | solution.py:720
  254.6 8.5 %copy-start.4 = (bf16[1,384,1024]{2,1,0:T(8,128)(2,1)S(1)}, bf16[1,384,1024]{2,1,0:T(8,128)(2,1)}, u32[]{:S(2)}) copy-start(bf16[1,384,1024]{2,1,0:T(8,128)(2,1)} %param.10) | copy-start | bytes 2359300
  258.0 38.3 %copy-start.19 = (f32[384,1024]{1,0:T(8,128)}, f32[384,1024]{1,0:T(8,128)S(1)}, u32[]{:S(2)}) copy-start(f32[384,1024]{1,0:T(8,128)S(1)} %fusion.11) | copy-start | bytes 4718596
  266.4 9.0 %slice-start.2 = ((s8[8388608]{0:T(1024)(128)(4,1)}), s8[4194304]{0:T(1024)(128)(4,1)S(1)}, s32[]{:S(2)}) async-start(s8[8388608]{0:T(1024)(128)(4,1)} %bitcast.128), calls=%async_computation.6 | async-start | bytes 8388608
  266.8 8.7 %slice-start.3 = ((s8[8388608]{0:T(1024)(128)(4,1)}), s8[4194304]{0:T(1024)(128)(4,1)S(1)}, s32[]{:S(2)}) async-start(s8[8388608]{0:T(1024)(128)(4,1)} %bitcast.128), calls=%async_computation.7 | async-start | bytes 8388608
  275.4 15.3 %slice-start = ((s8[8388608]{0:T(1024)(128)(4,1)}), s8[4194304]{0:T(1024)(128)(4,1)S(1)}, s32[]{:S(2)}) async-start(s8[8388608]{0:T(1024)(128)(4,1)} %bitcast.124), calls=%async_computation.4 | async-start | bytes 8388608
  280.4 10.3 %slice-start.1 = ((s8[8388608]{0:T(1024)(128)(4,1)}), s8[4194304]{0:T(1024)(128)(4,1)S(1)}, s32[]{:S(2)}) async-start(s8[8388608]{0:T(1024)(128)(4,1)} %bitcast.124), calls=%async_computation.5 | async-start | bytes 8388608
  290.7 3.8 copy-start.52
  300.0 15.9 %all-to-all-start.2 = ((bf16[384,4,256]{2,0,1:T(8,128)(2,1)}), bf16[384,4,256]{2,0,1:T(8,128)(2,1)}, u32[]{:S(2)}, u32[]{:S(2)}) async-start(bf16[384,4,256]{2,0,1:T(8,128)(2,1)} %bitcast.97), calls=%async_computation.2 | async-start | bytes 1572864 | tf_op jit(solution)/shard_map/all_to_all | solution.py:741
  359.3 4.8 copy-start.7
  359.3 4.8 copy-start.10
  359.3 41.8 %all-to-all-start.3 = ((bf16[3,1536,256]{2,0,1:T(4,128)(2,1)}), bf16[3,1536,256]{2,0,1:T(4,128)(2,1)}, u32[]{:S(2)}, u32[]{:S(2)}) async-start(bf16[3,1536,256]{2,0,1:T(4,128)(2,1)} %copy.58), calls=%async_computation.3 | async-start | bytes 6291456 | tf_op jit(solution)/shard_map/all_to_all | solution.py:746
  404.7 4.5 copy-start.2
  404.7 4.5 copy-start.31
  409.2 6.8 %copy-start.13 = (bf16[384,1024]{1,0:T(8,128)(2,1)S(1)}, bf16[384,1024]{1,0:T(8,128)(2,1)}, u32[]{:S(2)}) copy-start(bf16[384,1024]{1,0:T(8,128)(2,1)} %fusion.22.h) | copy-start | bytes 2359300
  409.2 6.8 %copy-start.17 = (bf16[3,384,4,256]{1,3,2,0:T(8,128)(2,1)S(1)}, bf16[3,384,4,256]{1,3,2,0:T(8,128)(2,1)}, u32[]{:S(2)}) copy-start(bf16[3,384,4,256]{1,3,2,0:T(8,128)(2,1)} %copy.60) | copy-start | bytes 7077892
  416.0 5.4 copy-start.33
  416.0 5.5 copy-start.5
  416.0 5.5 copy-start.35
  (29 other events, 67.6 us)

commit v2 on v1

--- a/solution.py
+++ b/solution.py
@@ -27,8 +27,8 @@
 MESH = pl.DeviceIdType.MESH
 VMEM_ALL = 67043328
 
-GATHER_CLASS = {"t": "D", "q": "DCD", "o": "D", "u": "CDDC", "d": "DCDD"}
-SUM_CLASS = {"t": "DD", "q": "CDC", "o": "D", "u": "CDCD", "d": "CDCC"}
+GATHER_CLASS = {"t": "D", "q": "CDC", "o": "C", "u": "CDCD", "d": "CDCD"}
+SUM_CLASS = {"t": "DD", "q": "CDC", "o": "C", "u": "CCDC", "d": "CDCC"}
 
 
 class Place:
@@ -52,13 +52,13 @@
         return lax.rem(self.z + d, self.Z)
 
 
-def greet(place, fsdp=True):
+def greet(place, seq=False):
     barrier = pltpu.get_barrier_semaphore()
-    others = [place.at(c=1 - place.c)]
+    others = [place.at(c=1 - place.c), place.at(x=1 - place.x)]
     others += [place.at(y=place.next_y(d)) for d in range(1, place.Y)]
-    if fsdp:
-        others += [place.at(x=1 - place.x)]
-        others += [place.at(z=place.next_z(d)) for d in range(1, place.Z)]
+    others += [place.at(z=place.next_z(d)) for d in range(1, place.Z)]
+    if seq:
+        others += [place.at(y=place.next_y(d), c=1 - place.c) for d in range(1, place.Y)]
     for other in others:
         pl.semaphore_signal(barrier, inc=1, device_id=other, device_id_type=MESH)
     pl.semaphore_wait(barrier, len(others))
@@ -84,10 +84,27 @@
 
 
 def pipeline(plan, stages):
-    for t in range(len(plan) + len(stages) - 1):
-        for k, stage in enumerate(stages):
-            if stage is not None and 0 <= t - k < len(plan):
-                stage(plan[t - k])
+    return [
+        functools.partial(stage, plan[t - k])
+        for t in range(len(plan) + len(stages) - 1)
+        for k, stage in enumerate(stages)
+        if 0 <= t - k < len(plan)
+    ]
+
+
+def run(steps):
+    for step in steps:
+        step()
+
+
+def interleave(steps, work, ahead, per):
+    run(steps[:ahead])
+    rest = steps[ahead:]
+    for piece in work:
+        piece()
+        now, rest = rest[:per], rest[per:]
+        run(now)
+    run(rest)
 
 
 class RowGather:
@@ -225,60 +242,80 @@
         return [self.over_z, self.over_x, self.over_y, self.over_c, self.finish]
 
 
-def gather_body(slices, shards, items, nw, *refs):
-    ws, rows_in = refs[:nw], refs[nw : nw + 2]
-    outs, rows_out = refs[nw + 2 : 2 * nw + 2], refs[2 * nw + 2 : 2 * nw + 4]
-    bounce, ssem, rsem, lsem, b0, b1, sseq, rseq, lseq = refs[2 * nw + 4 :]
+def gather_scratch(slices, shards, items, rows):
+    Y, Z = slices // CORES, shards // XS
+    n = len(items)
+    widest = max(cn // CORES // (Y if kind == "D" else 1) for _, _, _, _, cn, kind in items)
+    return [pltpu.VMEM((n, rows, widest), BF), DMA((n, Z + Y)), DMA((n, Z + Y)), DMA((n,))]
+
+
+def gathered_shapes(slices, shards, ws, rows_in):
+    Y, Z = slices // CORES, shards // XS
+    return [jax.ShapeDtypeStruct((Z, XS) + w.shape, w.dtype) for w in ws] + [
+        jax.ShapeDtypeStruct((Y, CORES) + r.shape, r.dtype) for r in rows_in
+    ]
+
+
+def row_scratch(slices, rows_in):
+    Y = slices // CORES
+    out = []
+    for r in rows_in:
+        out += [pltpu.VMEM(r.shape, r.dtype), DMA((Y,)), DMA((Y,)), DMA((1,))]
+    return out
+
+
+def row_gathers(place, rows_in, rows_out, scratch):
+    rows = []
+    for k, (src, out) in enumerate(zip(rows_in, rows_out)):
+        b, s, r, m = scratch[4 * k : 4 * k + 4]
+        rows.append(RowGather(place, src, out, b, s, r, m.at[0]))
+    return rows
+
+
+def merged(fulls):
+    return [g.reshape(-1, g.shape[-1]) for g in fulls]
+
+
+def gather_body(slices, shards, items, nw, nr, *refs):
+    ws, rows_in = refs[:nw], refs[nw : nw + nr]
+    outs, rows_out = refs[nw + nr : 2 * nw + nr], refs[2 * nw + nr : 2 * (nw + nr)]
+    scratch = refs[2 * (nw + nr) :]
     place = Place(slices, shards)
-    gather = WeightGather(place, items, ws, outs, bounce, ssem, rsem, lsem)
-    rows = [
-        RowGather(place, src, out, b, sseq.at[k], rseq.at[k], lseq.at[k])
-        for k, (src, out, b) in enumerate(zip(rows_in, rows_out, (b0, b1)))
-    ]
+    gather = WeightGather(place, items, ws, outs, *scratch[:4])
+    rows = row_gathers(place, rows_in, rows_out, scratch[4:])
     gather.load()
     for r in rows:
         r.load()
     greet(place)
-    gather.over_z(gather.plan[0])
-    rows[0].start()
-    rows[1].start()
+    steps = pipeline(gather.plan, gather.stages())
+    run(steps[:1])
+    for r in rows:
+        r.start()
     gather.store()
-    stages = gather.stages()
-    first = gather.plan[0]
-    stages[0] = lambda p: None if p is first else gather.over_z(p)
-    pipeline(gather.plan, stages)
+    run(steps[1:])
     for r in rows:
         r.middle()
     for r in rows:
         r.end()
 
 
-def gather_all(slices, shards, width, ws, rows_in):
-    Y, Z = slices // CORES, shards // XS
-    rows = ws[1].shape[0]
-    items = pieces(rows, width, "tqoud", GATHER_CLASS)
-    n, nw = len(items), len(ws)
-    widest = max(cn // CORES // (Y if kind == "D" else 1) for _, _, _, _, cn, kind in items)
+def gather_weights(slices, shards, width, which, ws, rows_in, cid):
+    rows = width // shards
+    items = pieces(rows, width, which, GATHER_CLASS)
+    nw, nr = len(ws), len(rows_in)
     out = pl.pallas_call(
-        functools.partial(gather_body, slices, shards, items, nw),
-        out_shape=[jax.ShapeDtypeStruct((Z, XS) + w.shape, w.dtype) for w in ws]
-        + [jax.ShapeDtypeStruct((Y, CORES) + r.shape, r.dtype) for r in rows_in],
-        in_specs=[ANY] * (nw + 2),
-        out_specs=[ANY] * (nw + 2),
-        scratch_shapes=[
-            pltpu.VMEM((n, rows, widest), BF),
-            DMA((n, Z + Y)),
-            DMA((n, Z + Y)),
-            DMA((n,)),
-        ]
-        + [pltpu.VMEM(r.shape, r.dtype) for r in rows_in]
-        + [DMA((2, Y)), DMA((2, Y)), DMA((2,))],
+        functools.partial(gather_body, slices, shards, items, nw, nr),
+        out_shape=gathered_shapes(slices, shards, ws, rows_in),
+        in_specs=[ANY] * (nw + nr),
+        out_specs=[ANY] * (nw + nr),
+        scratch_shapes=gather_scratch(slices, shards, items, rows) + row_scratch(slices, rows_in),
         compiler_params=pltpu.CompilerParams(
-            collective_id=0, has_side_effects=True, vmem_limit_bytes=VMEM_ALL
+            collective_id=cid, has_side_effects=True, vmem_limit_bytes=VMEM_ALL
         ),
     )(*ws, *rows_in)
-    full = [g.reshape(-1, g.shape[-1]) for g in out[:nw]]
-    return full, [g.reshape((slices,) + r.shape) for g, r in zip(out[nw:], rows_in)]
+    return merged(out[:nw]), [
+        g.reshape((slices,) + r.shape) for g, r in zip(out[nw:], rows_in)
+    ]
 
 
 def add_into(dst, src, rn):
@@ -308,6 +345,7 @@
         self.plan = []
         for i, (w, r0, rn, c0, cn, kind) in enumerate(items):
             p = dict(i=i, w=w, kind=kind, rn=rn, c0=c0, half=cn // CORES)
+            p["k"] = sum(q["kind"] == kind for q in self.plan)
             p.update(rows=pl.ds(r0, rn), vr=pl.ds(0, rn), sends=[])
             self.plan.append(p)
 
@@ -365,7 +403,7 @@
                         p,
                         d,
                         self.acc.at[i, y, :, :, vr, :],
-                        self.ry.at[i, d - 1, :, :, vr, :],
+                        self.ry.at[p["k"], d - 1, :, :, vr, :],
                         place.at(y=y),
                     )
                 )
@@ -374,7 +412,7 @@
         place, i, vr = self.place, p["i"], p["vr"]
         for d, copy in enumerate(p["y"]):
             copy.wait_recv()
-            add_into(self.acc.at[i, place.y], self.ry.at[i, d], p["rn"])
+            add_into(self.acc.at[i, place.y], self.ry.at[p["k"], d], p["rn"])
         other = 1 - place.x
         if p["kind"] == "D":
             src, dst = self.acc.at[i, place.y, :, other, vr, :], self.rx.at[i, 0, :, vr, :]
@@ -412,14 +450,14 @@
             if p["kind"] == "D":
                 self.fin[i, 0, vr, :] = total.astype(BF)
             else:
-                self.rf[i, place.y, part, vr, :] = total.astype(BF)
+                self.rf[p["k"], place.y, part, vr, :] = total.astype(BF)
         first = place.Z + place.Y - 1
         p["f"], p["st"] = [], []
         if p["kind"] == "D":
             src, dst = self.fin.at[i, 0, vr, :], self.region(p, place.c, place.y)
             p["st"].append(keep(src, dst, self.lsem.at[i, 0]))
         else:
-            src = dst = self.rf.at[i, place.y, :, vr, :]
+            src = dst = self.rf.at[p["k"], place.y, :, vr, :]
         for d in range(1, place.Y):
             p["f"].append(self.post(p, first + d, src, dst, place.at(y=place.next_y(d))))
 
@@ -429,9 +467,9 @@
             copy.wait_recv()
         if p["kind"] == "C":
             for part in range(place.Y):
-                total = self.rf[i, 0, part, vr, :].astype(jnp.float32)
+                total = self.rf[p["k"], 0, part, vr, :].astype(jnp.float32)
                 for y in range(1, place.Y):
-                    total = total + self.rf[i, y, part, vr, :].astype(jnp.float32)
+                    total = total + self.rf[p["k"], y, part, vr, :].astype(jnp.float32)
                 self.fin[i, part, vr, :] = total.astype(BF)
                 src, dst = self.fin.at[i, part, vr, :], self.region(p, place.c, part)
                 p["st"].append(keep(src, dst, self.lsem.at[i, part]))
@@ -460,63 +498,48 @@
 def sum_scratch(slices, shards, items, rows):
     Y, Z = slices // CORES, shards // XS
     n, wide = len(items), items[0][4] // CORES // Y
+    nd = max(1, sum(item[5] == "D" for item in items))
+    nc = max(1, n - nd)
     return [
         pltpu.VMEM((n, Y, Z, XS, rows, wide), BF),
         pltpu.VMEM((n, Y, Z, XS, rows, wide), BF),
-        pltpu.VMEM((n, Y - 1, Z, XS, rows, wide), BF),
+        pltpu.VMEM((nd, Y - 1, Z, XS, rows, wide), BF),
         pltpu.VMEM((n, Y, Z, rows, wide), BF),
         pltpu.VMEM((n, Z - 1, Y, rows, wide), BF),
         pltpu.VMEM((n, Y, rows, wide), BF),
-        pltpu.VMEM((n, Y, Y, rows, wide), BF),
+        pltpu.VMEM((nc, Y, Y, rows, wide), BF),
         DMA((n, Y)),
         DMA((n, Z + 3 * Y)),
         DMA((n, Z + 3 * Y)),
     ]
 
 
-def sum_body(slices, shards, items, nw, nr, *refs):
-    grads, rows_in = refs[:nw], refs[nw : nw + nr]
-    outs, rows_out = refs[nw + nr : 2 * nw + nr], refs[2 * nw + nr : 2 * (nw + nr)]
-    scratch = refs[2 * (nw + nr) :]
+def sum_body(slices, shards, items, nw, *refs):
     place = Place(slices, shards)
-    sums = GradSum(place, items, grads, outs, *scratch[:10])
-    rows = []
-    for k in range(nr):
-        b, s, r, m = scratch[10 + 4 * k : 14 + 4 * k]
-        rows.append(RowGather(place, rows_in[k], rows_out[k], b, s, r, m.at[0]))
-    for r in rows:
-        r.load()
+    sums = GradSum(place, items, refs[:nw], refs[nw : 2 * nw], *refs[2 * nw :])
     greet(place)
-    for r in rows:
-        r.start()
-    pipeline(sums.plan, sums.stages())
-    for r in rows:
-        r.middle()
-    for r in rows:
-        r.end()
-
-
-def sum_grads(slices, shards, width, which, grads, rows_in, cid):
-    Y, Z = slices // CORES, shards // XS
+    run(pipeline(sums.plan, sums.stages()))
+
+
+def split_grads(shards, grads):
+    return [g.reshape(shards // XS, XS, -1, g.shape[1]) for g in grads]
+
+
+def sum_grads(slices, shards, width, which, grads, cid):
     rows = width // shards
     items = pieces(rows, width, which, SUM_CLASS)
-    nw, nr = len(grads), len(rows_in)
-    grads = [g.reshape(Z, XS, -1, g.shape[1]) for g in grads]
-    extra = []
-    for r in rows_in:
-        extra += [pltpu.VMEM(r.shape, r.dtype), DMA((Y,)), DMA((Y,)), DMA((1,))]
-    out = pl.pallas_call(
-        functools.partial(sum_body, slices, shards, items, nw, nr),
-        out_shape=[jax.ShapeDtypeStruct(g.shape[2:], BF) for g in grads]
-        + [jax.ShapeDtypeStruct((Y, CORES) + r.shape, r.dtype) for r in rows_in],
-        in_specs=[ANY] * (nw + nr),
-        out_specs=[ANY] * (nw + nr),
-        scratch_shapes=sum_scratch(slices, shards, items, rows) + extra,
+    nw = len(grads)
+    grads = split_grads(shards, grads)
+    return pl.pallas_call(
+        functools.partial(sum_body, slices, shards, items, nw),
+        out_shape=[jax.ShapeDtypeStruct(g.shape[2:], BF) for g in grads],
+        in_specs=[ANY] * nw,
+        out_specs=[ANY] * nw,
+        scratch_shapes=sum_scratch(slices, shards, items, rows),
         compiler_params=pltpu.CompilerParams(
             collective_id=cid, has_side_effects=True, vmem_limit_bytes=VMEM_ALL
         ),
-    )(*grads, *rows_in)
-    return out[:nw], [g.reshape((slices,) + r.shape) for g, r in zip(out[nw:], rows_in)]
+    )(*grads)
 
 
 def dot(a, b, ca, cb):
@@ -542,8 +565,9 @@
     logsum[h : h + 1, rows] = peak + jnp.log2(total)
 
 
-def backward_block(qkv, mixed, logsum, g, seg_col, seg_row, dk, dv, dq, h, rows):
+def backward_block(qkv, mixed, logsum, g, seg_col, seg_row, dk, dv, dq, h, rows, slot):
     lanes = slice(h * HD, (h + 1) * HD)
+    side = slice(slot * HD, (slot + 1) * HD)
     q, gb = qkv[0, rows, lanes], g[rows, lanes]
     k, v = qkv[1, :, lanes], qkv[2, :, lanes]
     prod = gb.astype(jnp.float32) * mixed[rows, lanes].astype(jnp.float32)
@@ -552,77 +576,221 @@
     same = seg_col[...] == seg_row[:, rows]
     probs = jnp.where(same, jnp.exp2(s - logsum[h : h + 1, rows]), 0.0)
     ds = (probs * (dot(v, gb, 1, 1) - delta)).astype(BF)
-    dv[:, lanes] += dot(probs.astype(BF), gb, 1, 0)
-    dk[:, lanes] += dot(ds, q, 1, 0)
-    dq[rows, lanes] = dot(ds, k, 0, 0)
-
-
-def forward_body(heads, block, qkv, seg_col, seg_row, mixed, logsum):
-    for h in range(heads):
-
+    dv[:, side] += dot(probs.astype(BF), gb, 1, 0)
+    dk[:, side] += dot(ds, q, 1, 0)
+    dq[rows, side] = dot(ds, k, 0, 0)
+
+
+class Exchange:
+    def __init__(self, place, ssem, rsem, lsem):
+        self.place, self.ssem, self.rsem, self.lsem = place, ssem, rsem, lsem
+        self.me = place.y * CORES + place.c
+        self.peers = []
+        for dy in list(range(1, place.Y)) + [0]:
+            for dc in (range(CORES) if dy else (1,)):
+                y, c = place.next_y(dy), lax.rem(place.c + dc, CORES)
+                self.peers.append((dy * CORES + dc, y * CORES + c, place.at(y=y, c=c)))
+        self.copies = {}
+
+    def give(self, k, src, dst):
+        slot, _, device = self.peers[k]
+        self.copies[k] = push(src, dst, self.ssem.at[slot], self.rsem.at[slot], device)
+
+    def mine(self, src, dst):
+        self.own = keep(src, dst, self.lsem)
+
+    def take(self):
+        for copy in self.copies.values():
+            copy.wait_recv()
+        self.own.wait()
+
+    def close(self):
+        for copy in self.copies.values():
+            copy.wait_send()
+
+
+def span(index, size):
+    return pl.ds(pl.multiple_of(index * size, size), size)
+
+
+def forward_body(slices, shards, items, nw, *refs):
+    ws, packed, seg_col, seg_row = refs[:nw], *refs[nw : nw + 3]
+    outs = refs[nw + 3 : 2 * nw + 3]
+    qkv, mixed_heads, logsum, mixed = refs[2 * nw + 3 : 2 * nw + 7]
+    scratch = refs[2 * nw + 7 :]
+    place = Place(slices, shards)
+    rows, part = mixed.shape[0], mixed_heads.shape[1]
+    gather = WeightGather(place, items, ws, outs, *scratch[:4])
+    pairs = part // 128
+    come, *backs = [
+        Exchange(place, *[r.at[t] for r in scratch[4:7]]) for t in range(1 + pairs)
+    ]
+    me = come.me
+    gather.load()
+    come.mine(packed.at[:, :, span(me, part)], qkv.at[:, span(me, rows), :])
+    greet(place, seq=True)
+    for k, (_, peer, _) in enumerate(come.peers):
+        come.give(k, packed.at[:, :, span(peer, part)], qkv.at[:, span(me, rows), :])
+    steps = pipeline(gather.plan, gather.stages())
+    run(steps[:1])
+    gather.store()
+
+    block = 256
+
+    def attend(h):
         def step(i, _):
-            rows = pl.ds(pl.multiple_of(i * block, block), block)
-            forward_block(qkv, seg_col, seg_row, mixed, logsum, h, rows)
+            forward_block(qkv, seg_col, seg_row, mixed_heads, logsum, h, span(i, block))
             return 0
 
         lax.fori_loop(0, seg_col.shape[0] // block, step, 0)
 
-
-def backward_body(
-    heads, block, qkv, mixed, logsum, g, seg_col, seg_row, cos, sin, out, dk, dv, dq
+    def finish(t, k, owner):
+        src = mixed_heads.at[span(owner, rows), t * 128 : (t + 1) * 128]
+        first = pl.multiple_of(me * part + t * 128, 128)
+        dst = mixed.at[:, pl.ds(first, 128)]
+        if k < len(come.peers):
+            backs[t].give(k, src, dst)
+        else:
+            backs[t].mine(src, dst)
+
+    work = [come.take]
+    owners = [peer for _, peer, _ in come.peers] + [me]
+    for t in range(pairs):
+        work += [functools.partial(attend, h) for h in (2 * t, 2 * t + 1)]
+        work += [functools.partial(finish, t, k, owner) for k, owner in enumerate(owners)]
+    interleave(steps[1:], work, 12, 4)
+    for back in backs:
+        back.take()
+    for ex in [come] + backs:
+        ex.close()
+
+
+def attention_forward(slices, shards, width, which, ws, packed, seg_col, seg_row, cid):
+    rows = packed.shape[1]
+    group, part = rows * slices, width // slices
+    items = pieces(width // shards, width, which, GATHER_CLASS)
+    nw = len(ws)
+    out = pl.pallas_call(
+        functools.partial(forward_body, slices, shards, items, nw),
+        out_shape=gathered_shapes(slices, shards, ws, [])
+        + [
+            jax.ShapeDtypeStruct((3, group, part), BF),
+            jax.ShapeDtypeStruct((group, part), BF),
+            jax.ShapeDtypeStruct((part // HD, group), jnp.float32),
+            jax.ShapeDtypeStruct((rows, width), BF),
+        ],
+        in_specs=[ANY] * (nw + 1) + [VM] * 2,
+        out_specs=[ANY] * nw + [VM] * 4,
+        scratch_shapes=gather_scratch(slices, shards, items, width // shards)
+        + [DMA((1 + part // 128, slices))] * 2
+        + [DMA((1 + part // 128,))],
+        compiler_params=pltpu.CompilerParams(
+            collective_id=cid, has_side_effects=True, vmem_limit_bytes=VMEM_ALL
+        ),
+    )(*ws, packed, seg_col, seg_row)
+    return merged(out[:nw]), out[nw:]
+
+
+def backward_body(slices, shards, items, nw, nr, *refs):
+    grads, rows_in = refs[:nw], refs[nw : nw + nr]
+    at = nw + nr
+    d_mixed, qkv, mixed, logsum, seg_col, seg_row, cos, sin = refs[at : at + 8]
+    at += 8
+    sums_out, rows_out, out = refs[at : at + nw], refs[at + nw : at + nw + nr], refs[at + nw + nr]
+    scratch = refs[at + nw + nr + 1 :]
+    place = Place(slices, shards)
+    sums = GradSum(place, items, grads, sums_out, *scratch[:10])
+    gathers = row_gathers(place, rows_in, rows_out, scratch[10:])
+    g, dk, dv, dq, turned, ssem, rsem, lsem = scratch[10 + 4 * nr :]
+    rows, part = d_mixed.shape[0], g.shape[1]
+    pairs = part // 128
+    come = Exchange(place, ssem.at[0], rsem.at[0], lsem.at[0])
+    backs = [
+        Exchange(place, ssem.at[1 + t], rsem.at[1 + t], lsem.at[1 + t]) for t in range(pairs)
+    ]
+    me = come.me
+    come.mine(d_mixed.at[:, span(me, part)], g.at[span(me, rows), :])
+    for r in gathers:
+        r.load()
+    greet(place, seq=True)
+    for k, (_, peer, _) in enumerate(come.peers):
+        come.give(k, d_mixed.at[:, span(peer, part)], g.at[span(me, rows), :])
+    for r in gathers:
+        r.start()
+
+    block = 256
+
+    def attend(h):
+        if h % 2 == 0:
+            dk[...] = jnp.zeros_like(dk)
+            dv[...] = jnp.zeros_like(dv)
+
+        def step(i, _):
+            backward_block(
+                qkv, mixed, logsum, g, seg_col, seg_row, dk, dv, dq, h, span(i, block), h % 2
+            )
+            return 0
+
+        lax.fori_loop(0, seg_col.shape[0] // block, step, 0)
+
+    def finish(t, k, owner):
+        own = span(owner, rows)
+        c, s = cos[own, :], sin[own, :]
+        for j, d in enumerate((dq, dk)):
+            v = d[own, :] * (HD**-0.5)
+            turned[t, j, own, :] = (v * c - swap_halves(v) * s).astype(BF)
+        turned[t, 2, own, :] = dv[own, :].astype(BF)
+        first = pl.multiple_of(me * part + t * 128, 128)
+        src, dst = turned.at[t, :, own, :], out.at[:, :, pl.ds(first, 128)]
+        if k < len(come.peers):
+            backs[t].give(k, src, dst)
+        else:
+            backs[t].mine(src, dst)
+
+    work = [come.take]
+    owners = [peer for _, peer, _ in come.peers] + [me]
+    for t in range(pairs):
+        work += [functools.partial(attend, h) for h in (2 * t, 2 * t + 1)]
+        work += [functools.partial(finish, t, k, owner) for k, owner in enumerate(owners)]
+    steps = pipeline(sums.plan, sums.stages())
+    interleave(steps, work, 10, 4)
+    for r in gathers:
+        r.middle()
+    for back in backs:
+        back.take()
+    for r in gathers:
+        r.end()
+    for ex in [come] + backs:
+        ex.close()
+
+
+def attention_backward(
+    slices, shards, width, which, grads, rows_in, d_mixed, kept, seg_col, seg_row, cos, sin, cid
 ):
-    dk[...] = jnp.zeros_like(dk)
-    dv[...] = jnp.zeros_like(dv)
-    steps = seg_col.shape[0] // block
-    for h in range(heads):
-
-        def step(i, _):
-            rows = pl.ds(pl.multiple_of(i * block, block), block)
-            backward_block(qkv, mixed, logsum, g, seg_col, seg_row, dk, dv, dq, h, rows)
-            return 0
-
-        lax.fori_loop(0, steps, step, 0)
-
-    def finish(i, _):
-        rows = pl.ds(pl.multiple_of(i * block, block), block)
-        c, s = cos[rows, :], sin[rows, :]
-        for j, d in enumerate((dq, dk)):
-            for t in range(heads * HD // 128):
-                w = slice(t * 128, (t + 1) * 128)
-                v = d[rows, w] * (HD**-0.5)
-                out[j, rows, w] = (v * c - swap_halves(v) * s).astype(BF)
-        out[2, rows, :] = dv[rows, :].astype(BF)
-        return 0
-
-    lax.fori_loop(0, steps, finish, 0)
-
-
-def attention_forward(qkv, seg_col, seg_row, block=512):
-    _, group, width = qkv.shape
-    heads = width // HD
-    return pl.pallas_call(
-        functools.partial(forward_body, heads, block),
-        out_shape=(
-            jax.ShapeDtypeStruct((group, width), BF),
-            jax.ShapeDtypeStruct((heads, group), jnp.float32),
+    rows = d_mixed.shape[0]
+    group, part = rows * slices, width // slices
+    items = pieces(width // shards, width, which, SUM_CLASS)
+    nw, nr, pairs = len(grads), len(rows_in), part // 128
+    grads = split_grads(shards, grads)
+    total = pltpu.VMEM((group, 128), jnp.float32)
+    out = pl.pallas_call(
+        functools.partial(backward_body, slices, shards, items, nw, nr),
+        out_shape=[jax.ShapeDtypeStruct(w.shape[2:], BF) for w in grads]
+        + gathered_shapes(slices, shards, [], rows_in)
+        + [jax.ShapeDtypeStruct((3, rows, width), BF)],
+        in_specs=[ANY] * (nw + nr + 1) + [VM] * 7,
+        out_specs=[ANY] * (nw + nr) + [VM],
+        scratch_shapes=sum_scratch(slices, shards, items, width // shards)
+        + row_scratch(slices, rows_in)
+        + [pltpu.VMEM((group, part), BF), total, total, total]
+        + [pltpu.VMEM((pairs, 3, group, 128), BF)]
+        + [DMA((1 + pairs, slices)), DMA((1 + pairs, slices)), DMA((1 + pairs,))],
+        compiler_params=pltpu.CompilerParams(
+            collective_id=cid, has_side_effects=True, vmem_limit_bytes=VMEM_ALL
         ),
-        in_specs=[VM] * 3,
-        out_specs=(VM, VM),
-        compiler_params=pltpu.CompilerParams(vmem_limit_bytes=VMEM_ALL),
-    )(qkv, seg_col, seg_row)
-
-
-def attention_backward(qkv, mixed, logsum, g, seg_col, seg_row, cos, sin, block=512):
-    _, group, width = qkv.shape
-    total = pltpu.VMEM((group, width), jnp.float32)
-    return pl.pallas_call(
-        functools.partial(backward_body, width // HD, block),
-        out_shape=jax.ShapeDtypeStruct((3, group, width), BF),
-        in_specs=[VM] * 8,
-        out_specs=VM,
-        scratch_shapes=[total] * 3,
-        compiler_params=pltpu.CompilerParams(vmem_limit_bytes=VMEM_ALL),
-    )(qkv, mixed, logsum, g, seg_col, seg_row, cos, sin)
+    )(*grads, *rows_in, d_mixed, *kept, seg_col, seg_row, cos, sin)
+    full = [g.reshape((slices,) + r.shape) for g, r in zip(out[nw:], rows_in)]
+    return out[:nw], full, out[nw + nr]
 
 
 def project_body(h, w, cos, sin, out):
@@ -696,10 +864,9 @@
     slices, shards = lax.axis_size("seq"), lax.axis_size("fsdp")
     group = rows * slices
     lens, places = lengths[0], order[0]
-    gathered, (order_all, cot_all) = gather_all(
-        slices, shards, width, [w_time, w_qkv, w_out, w_up, w_down], [order, cotangent[0]]
+    (f_time, f_qkv), (order_all, cot_all) = gather_weights(
+        slices, shards, width, "tq", [w_time, w_qkv], [order, cotangent[0]], 0
     )
-    f_time, f_qkv, f_out, f_up, f_down = gathered
     order_all = order_all.reshape(group)
 
     member, _, offset = layout(lens, places)
@@ -715,9 +882,9 @@
 
     cos, sin = turn_tables(offset)
     packed = project(h_one, f_qkv, cos, sin)
-    heads_qkv = lax.all_to_all(packed, "seq", split_axis=2, concat_axis=1, tiled=True)
-    mixed_heads, logsum = attention_forward(heads_qkv, seg_col, seg_row)
-    mixed = lax.all_to_all(mixed_heads, "seq", split_axis=0, concat_axis=1, tiled=True)
+    (f_out, f_up, f_down), (heads_qkv, mixed_heads, logsum, mixed) = attention_forward(
+        slices, shards, width, "oud", [w_out, w_up, w_down], packed, seg_col, seg_row, 1
+    )
 
     x_two = inputs + jnp.dot(mixed, f_out, preferred_element_type=jnp.float32)
     normed_two, pull_two = jax.vjp(norm_mod, x_two, scale_two)
@@ -738,12 +905,22 @@
     grad_out = dot(mixed, d_attn, 0, 0).astype(BF)
     d_mixed = dot(d_attn, f_out, 1, 1).astype(BF)
 
-    d_heads = lax.all_to_all(d_mixed, "seq", split_axis=1, concat_axis=0, tiled=True)
     cos_all, sin_all = turn_tables(offset_all)
-    d_qkv_heads = attention_backward(
-        heads_qkv, mixed_heads, logsum, d_heads, seg_col, seg_row, cos_all, sin_all
+    sums, (result_all,), d_packed = attention_backward(
+        slices,
+        shards,
+        width,
+        "duo",
+        [grad_down, grad_up, grad_out],
+        [result],
+        d_mixed,
+        (heads_qkv, mixed_heads, logsum),
+        seg_col,
+        seg_row,
+        cos_all,
+        sin_all,
+        2,
     )
-    d_packed = lax.all_to_all(d_qkv_heads, "seq", split_axis=1, concat_axis=2, tiled=True)
     d_qkv = d_packed.transpose(1, 0, 2).reshape(rows, 3 * width)
     grad_qkv = dot(h_one, d_qkv, 0, 0).astype(BF)
     d_xone, d_scale_one = pull_one(dot(d_qkv, f_qkv, 1, 1))
@@ -763,11 +940,8 @@
         preferred_element_type=jnp.float32,
     ).astype(BF)
 
-    grads, (result_all,) = sum_grads(
-        slices, shards, width, "duoqt",
-        [grad_down, grad_up, grad_out, grad_qkv, grad_time], [result], 1,
-    )
-    s_down, s_up, s_out, s_qkv, s_time = [g.astype(jnp.float32) for g in grads]
+    sums = sums + sum_grads(slices, shards, width, "qt", [grad_qkv, grad_time], 3)
+    s_down, s_up, s_out, s_qkv, s_time = [g.astype(jnp.float32) for g in sums]
     mine = lax.axis_index("seq") * rows + jnp.arange(rows, dtype=jnp.int32)
     output = pick_rows(result_all, mine, order_all).astype(BF)
     return (output[None], input_grad[None], s_time, s_qkv, s_out, s_up, s_down)

time: 615 us -> 557 us (0.906)
  waiting for transfers between devices: 62.5 us -> 0 us
  Pallas kernels: 388 us -> 437 us
  local copies, waits for them, and re-layouts: 35.1 us -> 11.7 us
  starting transfers between devices: 17.2 us -> 0 us
    all_to_all x4 -> x0, waiting for transfers between devices: 62.5 us -> none  [the longest x1 30.5 us: on_device(): lax.all_to_all(packed, 'seq', split_axis=2, concat_axis=1, tiled=True)]
    pallas_call x4, Pallas kernels: 379 us -> 427 us  [the longest x1 169 us: attention_backward(): pl.pallas_call(functools.partial(backward_body, slices, shards, items, nw...]
    all_to_all x4 -> x0, starting transfers between devices: 17.2 us -> none  [the longest x1 4.8 us: on_device(): lax.all_to_all(d_qkv_heads, 'seq', split_axis=1, concat_axis=2, tiled=True)]
    all_to_all x5 -> x0, local copies, waits for them, and re-layouts: 15.5 us -> none  [the longest x2 8.1 us: on_device(): lax.all_to_all(d_qkv_heads, 'seq', split_axis=1, concat_axis=2, tiled=True)]
    pallas_call x2 -> x0, local copies, waits for them, and re-layouts: 11.4 us -> none  [the longest x1 5.78 us: project(): pl.pallas_call(project_body, grid=(3, per), out_shape=jax.ShapeDtypeStruc...]
  transfers between devices with their start and end apart: 4 -> 0, of which waited for: 4 -> 0; matrix products, arithmetic and copies ran while one was open for 6% -> 0% of each run, Pallas kernels for 0% -> 0%
where the time goes in v2:
time: 557 us; the launch traced here: 553 us
  Pallas kernels  437 us (78%)
  matrix products  73.9 us (13%)
  other arithmetic  29.3 us (5%)
  local copies, waits for them, and re-layouts  11.7 us (2%)
    pallas_call x1, Pallas kernels, attention_backward(): pl.pallas_call(functools.partial(backward_body, slices, shards, items, nw...  169 us
    pallas_call x1, Pallas kernels, attention_forward(): pl.pallas_call(functools.partial(forward_body, slices, shards, items, nw)...  135 us
    pallas_call x1, Pallas kernels, sum_grads(): pl.pallas_call(functools.partial(sum_body, slices, shards, items, nw), ou...  66 us
    pallas_call x1, Pallas kernels, gather_weights(): pl.pallas_call(functools.partial(gather_body, slices, shards, items, nw,...  56.4 us
    dot_general x8, matrix products, dot(): lax.dot_general(a, b, (((ca,), (cb,)), ((), ())), preferred_element_type=...  46.2 us

profile of v2, /device:TPU:0, one launch (start us, length us, event | category | flops | bytes accessed | tf_op | source)
XLA Modules:
  0.0 552.8 jit_solution(10745137096766599769)
XLA Ops:
  5.4 56.4 %shard_map.153 = (bf16[4,2,32,2048]{3,2,1,0:T(8,128)(2,1)}, bf16[4,2,128,3072]{3,2,1,0:T(8,128)(2,1)}, s32[2,2,1,384]{3,2,1,0:T(1,128)}, bf16[2,2,384,1024]{3,2,1,0:T(8,128)(2,1)}) custom-call(bf16[32,2048]{1,0:T(8,128)(2,1)} %refs_0_.2, bf16[128,3072]{1,0:T(8,128)(2,1)} %refs_1_.2, s32[1,384]{1,0:T(1,128)} %refs_2_.2, bf16[384,1024]{1,0:T(8,128)(2,1)} %bitcast.88), custom_call_target="tpu_custom_call" | custom-call | tf_op jit(solution)/shard_map/pallas_call | solution.py:306
  63.3 1.5 fusion.49
  64.8 2.2 fusion.54
  69.7 9.6 %shard_map.154.refs_3_ = bf16[3,384,1024]{2,1,0:T(8,128)(2,1)} custom-call(bf16[384,1024]{1,0:T(8,128)(2,1)} %fusion.22.h, bf16[1024,3072]{1,0:T(8,128)(2,1)} %bitcast.80, f32[384,128]{1,0:T(8,128)} %get-tuple-element.65.cos, f32[384,128]{1,0:T(8,128)} %get-tuple-element.66.sin), custom_call_target="tpu_custom_call" | custom-call | tf_op jit(solution)/shard_map/pallas_call | solution.py:810
  80.7 1.4 select_reduce_fusion
  83.8 135.1 %shard_map.155 = (bf16[4,2,128,1024]{3,2,1,0:T(8,128)(2,1)}, bf16[4,2,128,4096]{3,2,1,0:T(8,128)(2,1)}, bf16[4,2,512,1024]{3,2,1,0:T(8,128)(2,1)}, bf16[3,1536,2...) custom-call(bf16[128,1024]{1,0:T(8,128)(2,1)} %refs_0_.3, ...), custom_call_target="tpu_custom_call" | custom-call | tf_op jit(solution)/shard_map/pallas_call | solution.py:673
  219.0 3.2 fusion.57
  222.9 8.9 %fusion.58 = f32[384,4096]{1,0:T(8,128)} fusion(bf16[384,1024]{1,0:T(8,128)(2,1)S(1)} %multiply_convert_fusion.1, bf16[1024,4096]{1,0:T(8,128)(2,1)} %bitcast.97), kind=kOutput, calls=%fused_computation.106 | convolution fusion | flops 3221225472 | bytes 15466496 | tf_op jit(solution)/shard_map/dot_general | solution.py:892
  231.8 1.4 fusion.11
  233.3 8.9 %fusion.6 = bf16[384,4096]{1,0:T(8,128)(2,1)S(1)} fusion(f32[384,4096]{1,0:T(8,128)} %fusion.58, bf16[4096,1024]{1,0:T(8,128)(2,1)S(1)} %bitcast.95, f32[384,1024]{1,0:T(8,128)S(1)} %fusion.11), kind=kOutput, calls=%fused_computation.10 | convolution fusion | flops 3253075968 | bytes 19398656 | tf_op jit(solution)/shard_map/dot_general | solution.py:546
  242.2 6.3 %multiply_reduce_fusion = (f32[384]{0:T(512)S(1)}, f32[384,1024]{1,0:T(8,128)S(1)}) fusion(f32[384,1024]{1,0:T(8,128)S(1)} %get-tuple-element.60, f32[384]{0:T(512)S(1)} %broadcast_multiply_fusion, f32[384,2048]{1,0:T(8,128)S(1)} %copy-done.1, bf16[384,4096]{1,0:T(8,128)(2,1)S(1)} %fusion.6, bf16[1024,4096]{1,0:T(8,128)(2,1)} %bitcast.98), kind=kOutput, calls=%fused_computation.43 | convolution fusion | flops 3223191040 | bytes 16256000 | tf_op jit(solution)/shard_map/dot_general | solution.py:546
  248.5 1.8 fusion.56
  250.5 1.4 copy-done.41
  251.9 2.0 convolution_convert_fusion.5.refs_4_
  253.9 5.0 add_convert_fusion.refs_3_
  258.9 2.6 convolution_convert_fusion.4
  261.6 7.0 %convolution_convert_fusion = bf16[1024,4096]{1,0:T(8,128)(2,1)} fusion(bf16[384,1024]{1,0:T(8,128)(2,1)S(1)} %multiply_convert_fusion.1, bf16[384,4096]{1,0:T(8,128)(2,1)S(1)} %fusion.6), kind=kOutput, calls=%fused_computation.2 | convolution fusion | flops 3225419776 | bytes 12320768 | tf_op jit(solution)/shard_map/dot_general | solution.py:546
  268.6 7.2 %convolution_convert_fusion.1 = bf16[4096,1024]{1,0:T(8,128)(2,1)} fusion(f32[384,1024]{1,0:T(8,128)S(1)} %fusion.11, f32[384,4096]{1,0:T(8,128)S(1)} %bitcast.107), kind=kOutput, calls=%fused_computation.3 | convolution fusion | flops 3239968768 | bytes 16252928 | tf_op jit(solution)/shard_map/dot_general | solution.py:546
  275.9 2.8 fusion.43
  278.7 2.4 pad_maximum_fusion
  281.1 169.4 %shard_map.156 = (bf16[512,1024]{1,0:T(8,128)(2,1)}, bf16[128,4096]{1,0:T(8,128)(2,1)}, bf16[128,1024]{1,0:T(8,128)(2,1)}, bf16[2,2,384,1024]{3,2,1,0:T(8,128)(2,1)}, bf16[3,384,1024]{2,1,0:T(8,128)(2,1)}) custom-call(bf16[4,2,512,1024]{3,2,1,0:T(8,128)(2,1)} %bitcast.79, bf16[4,2,128,4096]{3,2,1,0:T(8,128)(2,1)} %bitcast.78, ...), custom_call_target="tpu_custom_call" | custom-call | tf_op jit(solution)/shard_map/pallas_call | solution.py:776
  450.6 4.6 copy.27
  455.2 6.7 %fusion.24 = (f32[384]{0:T(512)S(1)}, f32[384,1024]{1,0:T(8,128)S(1)}) fusion(bf16[1,384,1024]{2,1,0:T(8,128)(2,1)} %param.10, f32[384]{0:T(512)S(1)} %copy-done.23, f32[384,2048]{1,0:T(8,128)S(1)} %copy-done.2, bf16[384,3072]{0,1:T(8,128)(2,1)} %bitcast.84, bf16[1024,3072]{1,0:T(8,128)(2,1)} %bitcast.81), kind=kOutput, calls=%fused_computation.37 | convolution fusion | flops 2418277888 | bytes 12585984 | tf_op jit(solution)/shard_map/dot_general | solution.py:546
  462.0 2.4 fusion.55
  465.6 2.0 convolution_convert_fusion.3
  467.6 5.5 convolution_convert_fusion.2
  473.1 66.0 %shard_map.157 = (bf16[128,3072]{1,0:T(8,128)(2,1)}, bf16[32,2048]{1,0:T(8,128)(2,1)}) custom-call(bf16[4,2,128,3072]{3,2,1,0:T(8,128)(2,1)} %bitcast.82, bf16[4,2,32,2048]{3,2,1,0:T(8,128)(2,1)} %bitcast.83), custom_call_target="tpu_custom_call" | custom-call | tf_op jit(solution)/shard_map/pallas_call | solution.py:533
  539.1 2.6 convert_element_type.113
  542.4 2.9 add_bitcast_fusion
  545.3 1.5 convert_element_type.115
  546.8 1.6 convert_element_type.116
  549.5 2.3 fusion.30
  (132 shorter events, 16.9 us)
Async XLA Ops:
  1.3 4.1 copy-start.18
  2.2 3.3 copy-start.32
  61.8 5.2 copy-start.5
  67.0 2.8 copy-start
  67.2 2.6 copy-start.22
  219.0 3.6 copy-start.1
  222.5 10.7 %slice-start = ((s8[8388608]{0:T(1024)(128)(4,1)}), s8[4194304]{0:T(1024)(128)(4,1)S(1)}, s32[]{:S(2)}) async-start(s8[8388608]{0:T(1024)(128)(4,1)} %bitcast.93), calls=%async_computation | async-start | bytes 8388608
  222.9 8.9 %copy-start.19 = (s32[384]{0:T(512)S(1)}, s32[384]{0:T(512)}, u32[]{:S(2)}) copy-start(s32[384]{0:T(512)} %copy-done.18) | copy-start | bytes 4612
  222.9 8.9 %copy-start.40 = (bf16[2,2,384,1024]{3,2,1,0:T(8,128)(2,1)S(1)}, bf16[2,2,384,1024]{3,2,1,0:T(8,128)(2,1)}, u32[]{:S(2)}) copy-start(bf16[2,2,384,1024]{3,2,1,0:T(8,128)(2,1)} %get-tuple-element.31) | copy-start | bytes 9437188
  222.9 10.4 %slice-start.1 = ((s8[8388608]{0:T(1024)(128)(4,1)}), s8[4194304]{0:T(1024)(128)(4,1)S(1)}, s32[]{:S(2)}) async-start(s8[8388608]{0:T(1024)(128)(4,1)} %bitcast.93), calls=%async_computation.1 | async-start | bytes 8388608
  248.5 5.4 slice-start.2
  250.3 3.6 slice-start.3
  251.9 7.0 %copy-start.3 = (f32[384,1024]{1,0:T(8,128)}, f32[384,1024]{1,0:T(8,128)S(1)}, u32[]{:S(2)}) copy-start(f32[384,1024]{1,0:T(8,128)S(1)} %add_add_fusion.2) | copy-start | bytes 4718596
  253.9 5.0 copy-start.12
  258.9 9.6 %slice-start.4 = ((s8[6291456]{0:T(1024)(128)(4,1)}), s8[4194304]{0:T(1024)(128)(4,1)S(1)}, s32[]{:S(2)}) async-start(s8[6291456]{0:T(1024)(128)(4,1)} %bitcast.106), calls=%async_computation.4 | async-start | bytes 8388608
  261.6 7.0 %slice-start.5 = ((s8[6291456]{0:T(1024)(128)(4,1)}), s8[2097152]{0:T(1024)(128)(4,1)S(1)}, s32[]{:S(2)}) async-start(s8[6291456]{0:T(1024)(128)(4,1)} %bitcast.106), calls=%async_computation.5 | async-start | bytes 4194304
  268.6 7.3 %copy-start.16 = (s32[1536]{0:T(1024)S(1)}, s32[1536]{0:T(1024)}, u32[]{:S(2)}) copy-start(s32[1536]{0:T(1024)} %copy-done.15) | copy-start | bytes 18436
  268.6 7.3 %copy-start.21 = (s32[1536]{0:T(1024)S(1)}, s32[1536]{0:T(1024)}, u32[]{:S(2)}) copy-start(s32[1536]{0:T(1024)} %get-tuple-element.43) | copy-start | bytes 18436
  268.6 7.3 %copy-start.38 = (f32[32]{0:T(128)S(1)}, f32[32]{0:T(128)}, u32[]{:S(2)}) copy-start(f32[32]{0:T(128)} %copy-done.37) | copy-start | bytes 388
  450.6 4.6 copy-start.2
  450.6 4.6 copy-start.23
  455.2 6.7 %copy-start.25 = (f32[384]{0:T(512)S(1)}, f32[384]{0:T(512)}, u32[]{:S(2)}) copy-start(f32[384]{0:T(512)} %copy-done.24) | copy-start | bytes 4612
  455.2 6.7 %copy-start.6 = (bf16[1,384,1024]{2,1,0:T(8,128)(2,1)S(1)}, bf16[1,384,1024]{2,1,0:T(8,128)(2,1)}, u32[]{:S(2)}) copy-start(bf16[1,384,1024]{2,1,0:T(8,128)(2,1)} %param.10) | copy-start | bytes 2359300
  455.2 6.7 %copy-start.27 = (f32[384]{0:T(512)S(1)}, f32[384]{0:T(512)}, u32[]{:S(2)}) copy-start(f32[384]{0:T(512)} %copy-done.26) | copy-start | bytes 4612
  461.9 2.5 copy-start.7
  464.4 3.2 copy-start.8
  464.4 3.2 copy-start.9
  539.0 2.6 copy-start.14
  539.1 3.3 copy-start.36
  539.1 3.3 copy-start.4
  542.4 2.9 copy-start.11
  546.8 2.7 copy-start.39
  (16 other events, 22.2 us)

commit v3 on v2

--- a/solution.py
+++ b/solution.py
@@ -26,6 +26,8 @@
 DMA = pltpu.SemaphoreType.DMA
 MESH = pl.DeviceIdType.MESH
 VMEM_ALL = 67043328
+CUT = 2
+LAG = 2
 
 GATHER_CLASS = {"t": "D", "q": "CDC", "o": "C", "u": "CDCD", "d": "CDCD"}
 SUM_CLASS = {"t": "DD", "q": "CDC", "o": "C", "u": "CCDC", "d": "CDCC"}
@@ -84,11 +86,12 @@
 
 
 def pipeline(plan, stages):
+    lags = [LAG * k for k in range(len(stages))]
     return [
-        functools.partial(stage, plan[t - k])
-        for t in range(len(plan) + len(stages) - 1)
-        for k, stage in enumerate(stages)
-        if 0 <= t - k < len(plan)
+        functools.partial(stage, plan[t - lag])
+        for t in range(len(plan) + lags[-1])
+        for lag, stage in zip(lags, stages)
+        if 0 <= t - lag < len(plan)
     ]
 
 
@@ -97,14 +100,13 @@
         step()
 
 
-def interleave(steps, work, ahead, per):
-    run(steps[:ahead])
-    rest = steps[ahead:]
-    for piece in work:
+def interleave(steps, work):
+    done = 0
+    for piece, count in work:
         piece()
-        now, rest = rest[:per], rest[per:]
-        run(now)
-    run(rest)
+        run(steps[done : done + count])
+        done += count
+    run(steps[done:])
 
 
 class RowGather:
@@ -140,18 +142,22 @@
 
 
 def pieces(rows, width, which, classes):
-    out = []
+    whole = []
     for j, name in enumerate(which):
         if name == "t":
             for k, kind in enumerate(classes["t"]):
                 span = 2 * width // len(classes["t"])
-                out.append((j, 0, rows // 4, k * span, span, kind))
+                whole.append((j, 0, rows // 4, k * span, span, kind))
         elif name == "d":
             for k, kind in enumerate(classes["d"]):
-                out.append((j, k * rows, rows, 0, width, kind))
+                whole.append((j, k * rows, rows, 0, width, kind))
         else:
             for k, kind in enumerate(classes[name]):
-                out.append((j, 0, rows, k * width, width, kind))
+                whole.append((j, 0, rows, k * width, width, kind))
+    out = []
+    for j, r0, rn, c0, cn, kind in whole:
+        cuts = CUT if rn % (16 * CUT) == 0 else 1
+        out += [(j, r0 + k * rn // cuts, rn // cuts, c0, cn, kind) for k in range(cuts)]
     return out
 
 
@@ -242,9 +248,9 @@
         return [self.over_z, self.over_x, self.over_y, self.over_c, self.finish]
 
 
-def gather_scratch(slices, shards, items, rows):
+def gather_scratch(slices, shards, items):
     Y, Z = slices // CORES, shards // XS
-    n = len(items)
+    n, rows = len(items), max(item[2] for item in items)
     widest = max(cn // CORES // (Y if kind == "D" else 1) for _, _, _, _, cn, kind in items)
     return [pltpu.VMEM((n, rows, widest), BF), DMA((n, Z + Y)), DMA((n, Z + Y)), DMA((n,))]
 
@@ -308,7 +314,7 @@
         out_shape=gathered_shapes(slices, shards, ws, rows_in),
         in_specs=[ANY] * (nw + nr),
         out_specs=[ANY] * (nw + nr),
-        scratch_shapes=gather_scratch(slices, shards, items, rows) + row_scratch(slices, rows_in),
+        scratch_shapes=gather_scratch(slices, shards, items) + row_scratch(slices, rows_in),
         compiler_params=pltpu.CompilerParams(
             collective_id=cid, has_side_effects=True, vmem_limit_bytes=VMEM_ALL
         ),
@@ -495,9 +501,10 @@
         ]
 
 
-def sum_scratch(slices, shards, items, rows):
+def sum_scratch(slices, shards, items):
     Y, Z = slices // CORES, shards // XS
     n, wide = len(items), items[0][4] // CORES // Y
+    rows = max(item[2] for item in items)
     nd = max(1, sum(item[5] == "D" for item in items))
     nc = max(1, n - nd)
     return [
@@ -535,7 +542,7 @@
         out_shape=[jax.ShapeDtypeStruct(g.shape[2:], BF) for g in grads],
         in_specs=[ANY] * nw,
         out_specs=[ANY] * nw,
-        scratch_shapes=sum_scratch(slices, shards, items, rows),
+        scratch_shapes=sum_scratch(slices, shards, items),
         compiler_params=pltpu.CompilerParams(
             collective_id=cid, has_side_effects=True, vmem_limit_bytes=VMEM_ALL
         ),
@@ -653,12 +660,12 @@
         else:
             backs[t].mine(src, dst)
 
-    work = [come.take]
+    work = [(lambda: None, 16), (come.take, 0)]
     owners = [peer for _, peer, _ in come.peers] + [me]
     for t in range(pairs):
-        work += [functools.partial(attend, h) for h in (2 * t, 2 * t + 1)]
-        work += [functools.partial(finish, t, k, owner) for k, owner in enumerate(owners)]
-    interleave(steps[1:], work, 12, 4)
+        work += [(functools.partial(attend, h), 8) for h in (2 * t, 2 * t + 1)]
+        work += [(functools.partial(finish, t, k, owner), 0) for k, owner in enumerate(owners)]
+    interleave(steps[1:], work)
     for back in backs:
         back.take()
     for ex in [come] + backs:
@@ -681,7 +688,7 @@
         ],
         in_specs=[ANY] * (nw + 1) + [VM] * 2,
         out_specs=[ANY] * nw + [VM] * 4,
-        scratch_shapes=gather_scratch(slices, shards, items, width // shards)
+        scratch_shapes=gather_scratch(slices, shards, items)
         + [DMA((1 + part // 128, slices))] * 2
         + [DMA((1 + part // 128,))],
         compiler_params=pltpu.CompilerParams(
@@ -715,9 +722,6 @@
     greet(place, seq=True)
     for k, (_, peer, _) in enumerate(come.peers):
         come.give(k, d_mixed.at[:, span(peer, part)], g.at[span(me, rows), :])
-    for r in gathers:
-        r.start()
-
     block = 256
 
     def attend(h):
@@ -747,13 +751,13 @@
         else:
             backs[t].mine(src, dst)
 
-    work = [come.take]
+    work = [(lambda: None, 10), (come.take, 0)] + [(r.start, 0) for r in gathers]
     owners = [peer for _, peer, _ in come.peers] + [me]
     for t in range(pairs):
-        work += [functools.partial(attend, h) for h in (2 * t, 2 * t + 1)]
-        work += [functools.partial(finish, t, k, owner) for k, owner in enumerate(owners)]
+        work += [(functools.partial(attend, h), 10) for h in (2 * t, 2 * t + 1)]
+        work += [(functools.partial(finish, t, k, owner), 0) for k, owner in enumerate(owners)]
     steps = pipeline(sums.plan, sums.stages())
-    interleave(steps, work, 10, 4)
+    interleave(steps, work)
     for r in gathers:
         r.middle()
     for back in backs:
@@ -780,7 +784,7 @@
         + [jax.ShapeDtypeStruct((3, rows, width), BF)],
         in_specs=[ANY] * (nw + nr + 1) + [VM] * 7,
         out_specs=[ANY] * (nw + nr) + [VM],
-        scratch_shapes=sum_scratch(slices, shards, items, width // shards)
+        scratch_shapes=sum_scratch(slices, shards, items)
         + row_scratch(slices, rows_in)
         + [pltpu.VMEM((group, part), BF), total, total, total]
         + [pltpu.VMEM((pairs, 3, group, 128), BF)]

time: 557 us -> 514 us (0.923)
  Pallas kernels: 437 us -> 393 us
    pallas_call x1, Pallas kernels: 135 us -> 117 us  [attention_forward(): pl.pallas_call(functools.partial(forward_body, slices, shards, items, nw)...]
    pallas_call x1, Pallas kernels: 169 us -> 157 us  [attention_backward(): pl.pallas_call(functools.partial(backward_body, slices, shards, items, nw...]
    pallas_call x1, Pallas kernels: 66 us -> 56.1 us  [sum_grads(): pl.pallas_call(functools.partial(sum_body, slices, shards, items, nw), ou...]
where the time goes in v3:
time: 514 us; the launch traced here: 510 us
  Pallas kernels  393 us (76%)
  matrix products  74.1 us (14%)
  other arithmetic  29.3 us (6%)
  local copies, waits for them, and re-layouts  11.6 us (2%)
    pallas_call x1, Pallas kernels, attention_backward(): pl.pallas_call(functools.partial(backward_body, slices, shards, items, nw...  157 us
    pallas_call x1, Pallas kernels, attention_forward(): pl.pallas_call(functools.partial(forward_body, slices, shards, items, nw)...  117 us
    pallas_call x1, Pallas kernels, sum_grads(): pl.pallas_call(functools.partial(sum_body, slices, shards, items, nw), ou...  56.1 us
    pallas_call x1, Pallas kernels, gather_weights(): pl.pallas_call(functools.partial(gather_body, slices, shards, items, nw,...  54.4 us
    dot_general x8, matrix products, dot(): lax.dot_general(a, b, (((ca,), (cb,)), ((), ())), preferred_element_type=...  46 us

profile of v3, /device:TPU:0, one launch (start us, length us, event | category | flops | bytes accessed | tf_op | source)
XLA Modules:
  0.0 509.7 jit_solution(10654897205209268391)
XLA Ops:
  5.4 54.4 %shard_map.153 = (bf16[4,2,32,2048]{3,2,1,0:T(8,128)(2,1)}, bf16[4,2,128,3072]{3,2,1,0:T(8,128)(2,1)}, s32[2,2,1,384]{3,2,1,0:T(1,128)}, bf16[2,2,384,1024]{3,2,1,0:T(8,128)(2,1)}) custom-call(bf16[32,2048]{1,0:T(8,128)(2,1)} %refs_0_.2, bf16[128,3072]{1,0:T(8,128)(2,1)} %refs_1_.2, s32[1,384]{1,0:T(1,128)} %refs_2_.2, bf16[384,1024]{1,0:T(8,128)(2,1)} %bitcast.88), custom_call_target="tpu_custom_call" | custom-call | tf_op jit(solution)/shard_map/pallas_call | solution.py:312
  61.3 1.5 fusion.49
  62.8 2.2 fusion.54
  67.8 9.3 %shard_map.154.refs_3_ = bf16[3,384,1024]{2,1,0:T(8,128)(2,1)} custom-call(bf16[384,1024]{1,0:T(8,128)(2,1)} %fusion.22.h, bf16[1024,3072]{1,0:T(8,128)(2,1)} %bitcast.80, f32[384,128]{1,0:T(8,128)} %get-tuple-element.65.cos, f32[384,128]{1,0:T(8,128)} %get-tuple-element.66.sin), custom_call_target="tpu_custom_call" | custom-call | tf_op jit(solution)/shard_map/pallas_call | solution.py:814
  78.4 1.4 select_reduce_fusion
  81.5 116.5 %shard_map.155 = (bf16[4,2,128,1024]{3,2,1,0:T(8,128)(2,1)}, bf16[4,2,128,4096]{3,2,1,0:T(8,128)(2,1)}, bf16[4,2,512,1024]{3,2,1,0:T(8,128)(2,1)}, bf16[3,1536,2...) custom-call(bf16[128,1024]{1,0:T(8,128)(2,1)} %refs_0_.3, ...), custom_call_target="tpu_custom_call" | custom-call | tf_op jit(solution)/shard_map/pallas_call | solution.py:680
  198.1 3.2 fusion.57
  202.0 9.3 %fusion.58 = f32[384,4096]{1,0:T(8,128)} fusion(bf16[384,1024]{1,0:T(8,128)(2,1)S(1)} %multiply_convert_fusion.1, bf16[1024,4096]{1,0:T(8,128)(2,1)} %bitcast.97), kind=kOutput, calls=%fused_computation.106 | convolution fusion | flops 3221225472 | bytes 15466496 | tf_op jit(solution)/shard_map/dot_general | solution.py:896
  211.3 1.4 fusion.11
  212.8 8.8 %fusion.6 = bf16[384,4096]{1,0:T(8,128)(2,1)S(1)} fusion(f32[384,4096]{1,0:T(8,128)} %fusion.58, bf16[4096,1024]{1,0:T(8,128)(2,1)S(1)} %bitcast.95, f32[384,1024]{1,0:T(8,128)S(1)} %fusion.11), kind=kOutput, calls=%fused_computation.10 | convolution fusion | flops 3253075968 | bytes 19398656 | tf_op jit(solution)/shard_map/dot_general | solution.py:553
  221.6 6.3 %multiply_reduce_fusion = (f32[384]{0:T(512)S(1)}, f32[384,1024]{1,0:T(8,128)S(1)}) fusion(f32[384,1024]{1,0:T(8,128)S(1)} %get-tuple-element.60, f32[384]{0:T(512)S(1)} %broadcast_multiply_fusion, f32[384,2048]{1,0:T(8,128)S(1)} %copy-done.1, bf16[384,4096]{1,0:T(8,128)(2,1)S(1)} %fusion.6, bf16[1024,4096]{1,0:T(8,128)(2,1)} %bitcast.98), kind=kOutput, calls=%fused_computation.43 | convolution fusion | flops 3223191040 | bytes 16256000 | tf_op jit(solution)/shard_map/dot_general | solution.py:553
  227.9 1.8 fusion.56
  229.9 1.4 copy-done.41
  231.3 2.0 convolution_convert_fusion.5.refs_4_
  233.3 5.0 add_convert_fusion.refs_3_
  238.3 2.6 convolution_convert_fusion.4
  240.9 6.8 %convolution_convert_fusion = bf16[1024,4096]{1,0:T(8,128)(2,1)} fusion(bf16[384,1024]{1,0:T(8,128)(2,1)S(1)} %multiply_convert_fusion.1, bf16[384,4096]{1,0:T(8,128)(2,1)S(1)} %fusion.6), kind=kOutput, calls=%fused_computation.2 | convolution fusion | flops 3225419776 | bytes 12320768 | tf_op jit(solution)/shard_map/dot_general | solution.py:553
  247.8 7.4 %convolution_convert_fusion.1 = bf16[4096,1024]{1,0:T(8,128)(2,1)} fusion(f32[384,1024]{1,0:T(8,128)S(1)} %fusion.11, f32[384,4096]{1,0:T(8,128)S(1)} %bitcast.107), kind=kOutput, calls=%fused_computation.3 | convolution fusion | flops 3239968768 | bytes 16252928 | tf_op jit(solution)/shard_map/dot_general | solution.py:553
  255.2 2.8 fusion.43
  258.0 2.4 pad_maximum_fusion
  260.4 156.9 %shard_map.156 = (bf16[512,1024]{1,0:T(8,128)(2,1)}, bf16[128,4096]{1,0:T(8,128)(2,1)}, bf16[128,1024]{1,0:T(8,128)(2,1)}, bf16[2,2,384,1024]{3,2,1,0:T(8,128)(2,1)}, bf16[3,384,1024]{2,1,0:T(8,128)(2,1)}) custom-call(bf16[4,2,512,1024]{3,2,1,0:T(8,128)(2,1)} %bitcast.79, bf16[4,2,128,4096]{3,2,1,0:T(8,128)(2,1)} %bitcast.78, ...), custom_call_target="tpu_custom_call" | custom-call | tf_op jit(solution)/shard_map/pallas_call | solution.py:780
  417.4 4.4 copy.27
  421.9 6.7 %fusion.24 = (f32[384]{0:T(512)S(1)}, f32[384,1024]{1,0:T(8,128)S(1)}) fusion(bf16[1,384,1024]{2,1,0:T(8,128)(2,1)} %param.10, f32[384]{0:T(512)S(1)} %copy-done.23, f32[384,2048]{1,0:T(8,128)S(1)} %copy-done.2, bf16[384,3072]{0,1:T(8,128)(2,1)} %bitcast.84, bf16[1024,3072]{1,0:T(8,128)(2,1)} %bitcast.81), kind=kOutput, calls=%fused_computation.37 | convolution fusion | flops 2418277888 | bytes 12585984 | tf_op jit(solution)/shard_map/dot_general | solution.py:553
  428.6 2.4 fusion.55
  432.2 2.0 convolution_convert_fusion.3
  434.2 5.5 %convolution_convert_fusion.2 = bf16[1024,3072]{1,0:T(8,128)(2,1)} fusion(bf16[384,1024]{1,0:T(8,128)(2,1)S(1)} %copy-done.8, bf16[384,3072]{0,1:T(8,128)(2,1)S(1)} %bitcast.85), kind=kOutput, calls=%fused_computation.12 | convolution fusion | flops 2419064832 | bytes 9437184 | tf_op jit(solution)/shard_map/dot_general | solution.py:553
  439.7 56.1 %shard_map.157 = (bf16[128,3072]{1,0:T(8,128)(2,1)}, bf16[32,2048]{1,0:T(8,128)(2,1)}) custom-call(bf16[4,2,128,3072]{3,2,1,0:T(8,128)(2,1)} %bitcast.82, bf16[4,2,32,2048]{3,2,1,0:T(8,128)(2,1)} %bitcast.83), custom_call_target="tpu_custom_call" | custom-call | tf_op jit(solution)/shard_map/pallas_call | solution.py:540
  495.8 2.6 convert_element_type.113
  499.1 2.9 add_bitcast_fusion
  502.0 1.5 convert_element_type.115
  503.6 1.6 convert_element_type.116
  506.2 2.3 fusion.30
  (132 shorter events, 16.9 us)
Async XLA Ops:
  1.3 4.1 copy-start.18
  2.2 3.3 copy-start.32
  59.9 5.2 %copy-start.5 = (bf16[1,384,1024]{2,1,0:T(8,128)(2,1)S(1)}, bf16[1,384,1024]{2,1,0:T(8,128)(2,1)}, u32[]{:S(2)}) copy-start(bf16[1,384,1024]{2,1,0:T(8,128)(2,1)} %param.10) | copy-start | bytes 2359300
  65.0 2.8 copy-start
  65.2 2.6 copy-start.22
  198.1 3.5 copy-start.1
  201.6 11.1 %slice-start = ((s8[8388608]{0:T(1024)(128)(4,1)}), s8[4194304]{0:T(1024)(128)(4,1)S(1)}, s32[]{:S(2)}) async-start(s8[8388608]{0:T(1024)(128)(4,1)} %bitcast.93), calls=%async_computation | async-start | bytes 8388608
  202.0 9.3 %copy-start.19 = (s32[384]{0:T(512)S(1)}, s32[384]{0:T(512)}, u32[]{:S(2)}) copy-start(s32[384]{0:T(512)} %copy-done.18) | copy-start | bytes 4612
  202.0 9.3 %copy-start.40 = (bf16[2,2,384,1024]{3,2,1,0:T(8,128)(2,1)S(1)}, bf16[2,2,384,1024]{3,2,1,0:T(8,128)(2,1)}, u32[]{:S(2)}) copy-start(bf16[2,2,384,1024]{3,2,1,0:T(8,128)(2,1)} %get-tuple-element.31) | copy-start | bytes 9437188
  202.0 10.8 %slice-start.1 = ((s8[8388608]{0:T(1024)(128)(4,1)}), s8[4194304]{0:T(1024)(128)(4,1)S(1)}, s32[]{:S(2)}) async-start(s8[8388608]{0:T(1024)(128)(4,1)} %bitcast.93), calls=%async_computation.1 | async-start | bytes 8388608
  227.9 5.4 %slice-start.2 = ((s8[6291456]{0:T(1024)(128)(4,1)}), s8[4194304]{0:T(1024)(128)(4,1)S(1)}, s32[]{:S(2)}) async-start(s8[6291456]{0:T(1024)(128)(4,1)} %bitcast.104), calls=%async_computation.2 | async-start | bytes 8388608
  229.6 3.6 slice-start.3
  231.3 7.0 %copy-start.3 = (f32[384,1024]{1,0:T(8,128)}, f32[384,1024]{1,0:T(8,128)S(1)}, u32[]{:S(2)}) copy-start(f32[384,1024]{1,0:T(8,128)S(1)} %add_add_fusion.2) | copy-start | bytes 4718596
  233.3 5.0 copy-start.12
  238.3 9.4 %slice-start.4 = ((s8[6291456]{0:T(1024)(128)(4,1)}), s8[4194304]{0:T(1024)(128)(4,1)S(1)}, s32[]{:S(2)}) async-start(s8[6291456]{0:T(1024)(128)(4,1)} %bitcast.106), calls=%async_computation.4 | async-start | bytes 8388608
  240.9 6.8 %slice-start.5 = ((s8[6291456]{0:T(1024)(128)(4,1)}), s8[2097152]{0:T(1024)(128)(4,1)S(1)}, s32[]{:S(2)}) async-start(s8[6291456]{0:T(1024)(128)(4,1)} %bitcast.106), calls=%async_computation.5 | async-start | bytes 4194304
  247.7 7.4 %copy-start.16 = (s32[1536]{0:T(1024)S(1)}, s32[1536]{0:T(1024)}, u32[]{:S(2)}) copy-start(s32[1536]{0:T(1024)} %copy-done.15) | copy-start | bytes 18436
  247.7 7.4 %copy-start.21 = (s32[1536]{0:T(1024)S(1)}, s32[1536]{0:T(1024)}, u32[]{:S(2)}) copy-start(s32[1536]{0:T(1024)} %get-tuple-element.43) | copy-start | bytes 18436
  247.7 7.4 %copy-start.38 = (f32[32]{0:T(128)S(1)}, f32[32]{0:T(128)}, u32[]{:S(2)}) copy-start(f32[32]{0:T(128)} %copy-done.37) | copy-start | bytes 388
  417.4 4.5 copy-start.2
  417.4 4.5 copy-start.23
  421.8 6.7 %copy-start.25 = (f32[384]{0:T(512)S(1)}, f32[384]{0:T(512)}, u32[]{:S(2)}) copy-start(f32[384]{0:T(512)} %copy-done.24) | copy-start | bytes 4612
  421.8 6.7 %copy-start.6 = (bf16[1,384,1024]{2,1,0:T(8,128)(2,1)S(1)}, bf16[1,384,1024]{2,1,0:T(8,128)(2,1)}, u32[]{:S(2)}) copy-start(bf16[1,384,1024]{2,1,0:T(8,128)(2,1)} %param.10) | copy-start | bytes 2359300
  421.9 6.7 %copy-start.27 = (f32[384]{0:T(512)S(1)}, f32[384]{0:T(512)}, u32[]{:S(2)}) copy-start(f32[384]{0:T(512)} %copy-done.26) | copy-start | bytes 4612
  428.6 2.5 copy-start.7
  431.0 3.2 copy-start.8
  431.0 3.2 copy-start.9
  495.8 2.6 copy-start.14
  495.8 3.3 copy-start.36
  495.8 3.3 copy-start.4
  499.1 2.9 copy-start.11
  503.6 2.7 copy-start.39
  (16 other events, 22.2 us)

commit v4 on v3

--- a/solution.py
+++ b/solution.py
@@ -29,8 +29,8 @@
 CUT = 2
 LAG = 2
 
-GATHER_CLASS = {"t": "D", "q": "CDC", "o": "C", "u": "CDCD", "d": "CDCD"}
-SUM_CLASS = {"t": "DD", "q": "CDC", "o": "C", "u": "CCDC", "d": "CDCC"}
+GATHER_CLASS = {"t": "D", "q": "CDC", "o": "C", "u": "DCDC", "d": "DCDC"}
+SUM_CLASS = {"t": "DD", "q": "CDC", "o": "C", "u": "CCDC", "d": "DCDC"}
 
 
 class Place:
@@ -178,6 +178,7 @@
                     i=i,
                     w=w,
                     kind=kind,
+                    first=c0,
                     rows=pl.ds(r0, rn),
                     cols=pl.ds(pl.multiple_of(first, 128), width),
                     half=pl.ds(pl.multiple_of(c0 + place.c * half, 128), half),
@@ -280,48 +281,6 @@
 
 def merged(fulls):
     return [g.reshape(-1, g.shape[-1]) for g in fulls]
-
-
-def gather_body(slices, shards, items, nw, nr, *refs):
-    ws, rows_in = refs[:nw], refs[nw : nw + nr]
-    outs, rows_out = refs[nw + nr : 2 * nw + nr], refs[2 * nw + nr : 2 * (nw + nr)]
-    scratch = refs[2 * (nw + nr) :]
-    place = Place(slices, shards)
-    gather = WeightGather(place, items, ws, outs, *scratch[:4])
-    rows = row_gathers(place, rows_in, rows_out, scratch[4:])
-    gather.load()
-    for r in rows:
-        r.load()
-    greet(place)
-    steps = pipeline(gather.plan, gather.stages())
-    run(steps[:1])
-    for r in rows:
-        r.start()
-    gather.store()
-    run(steps[1:])
-    for r in rows:
-        r.middle()
-    for r in rows:
-        r.end()
-
-
-def gather_weights(slices, shards, width, which, ws, rows_in, cid):
-    rows = width // shards
-    items = pieces(rows, width, which, GATHER_CLASS)
-    nw, nr = len(ws), len(rows_in)
-    out = pl.pallas_call(
-        functools.partial(gather_body, slices, shards, items, nw, nr),
-        out_shape=gathered_shapes(slices, shards, ws, rows_in),
-        in_specs=[ANY] * (nw + nr),
-        out_specs=[ANY] * (nw + nr),
-        scratch_shapes=gather_scratch(slices, shards, items) + row_scratch(slices, rows_in),
-        compiler_params=pltpu.CompilerParams(
-            collective_id=cid, has_side_effects=True, vmem_limit_bytes=VMEM_ALL
-        ),
-    )(*ws, *rows_in)
-    return merged(out[:nw]), [
-        g.reshape((slices,) + r.shape) for g, r in zip(out[nw:], rows_in)
-    ]
 
 
 def add_into(dst, src, rn):
@@ -597,19 +556,21 @@
             for dc in (range(CORES) if dy else (1,)):
                 y, c = place.next_y(dy), lax.rem(place.c + dc, CORES)
                 self.peers.append((dy * CORES + dc, y * CORES + c, place.at(y=y, c=c)))
-        self.copies = {}
-
-    def give(self, k, src, dst):
-        slot, _, device = self.peers[k]
-        self.copies[k] = push(src, dst, self.ssem.at[slot], self.rsem.at[slot], device)
-
-    def mine(self, src, dst):
-        self.own = keep(src, dst, self.lsem)
+        self.copies, self.own = {}, []
+
+    def give(self, key, src, dst):
+        slot, _, device = self.peers[key[0]]
+        sems = self.ssem.at[slot, key[1]], self.rsem.at[slot, key[1]]
+        self.copies[key] = push(src, dst, *sems, device)
+
+    def mine(self, src, dst, t=0):
+        self.own.append(keep(src, dst, self.lsem.at[t]))
 
     def take(self):
         for copy in self.copies.values():
             copy.wait_recv()
-        self.own.wait()
+        for copy in self.own:
+            copy.wait()
 
     def close(self):
         for copy in self.copies.values():
@@ -620,27 +581,93 @@
     return pl.ds(pl.multiple_of(index * size, size), size)
 
 
+def after(steps, stage, hooks):
+    out = []
+    for step in steps:
+        out.append(step)
+        if step.func == stage:
+            out += hooks.get(step.args[0]["i"], [])
+    return out
+
+
 def forward_body(slices, shards, items, nw, *refs):
-    ws, packed, seg_col, seg_row = refs[:nw], *refs[nw : nw + 3]
-    outs = refs[nw + 3 : 2 * nw + 3]
-    qkv, mixed_heads, logsum, mixed = refs[2 * nw + 3 : 2 * nw + 7]
-    scratch = refs[2 * nw + 7 :]
+    ws, (order, cot) = refs[:nw], refs[nw : nw + 2]
+    tokens, member, ends, emb, cos, sin = refs[nw + 2 : nw + 8]
+    refs = refs[nw + 8 :]
+    outs, rows_out = refs[:nw], refs[nw : nw + 2]
+    h_one, scales, seg_col, seg_row, qkv, mixed_heads, logsum, mixed = refs[nw + 2 : nw + 10]
+    scratch = refs[nw + 10 :]
     place = Place(slices, shards)
-    rows, part = mixed.shape[0], mixed_heads.shape[1]
     gather = WeightGather(place, items, ws, outs, *scratch[:4])
+    order_rows, cot_rows = row_gathers(place, (order, cot), rows_out, scratch[4:12])
+    w_time, w_part, packed, places, csem, ssem, rsem, lsem = scratch[12:]
+    rows, width = tokens.shape
+    part = mixed_heads.shape[1]
     pairs = part // 128
-    come, *backs = [
-        Exchange(place, *[r.at[t] for r in scratch[4:7]]) for t in range(1 + pairs)
-    ]
-    me = come.me
-    gather.load()
-    come.mine(packed.at[:, :, span(me, part)], qkv.at[:, span(me, rows), :])
-    greet(place, seq=True)
-    for k, (_, peer, _) in enumerate(come.peers):
-        come.give(k, packed.at[:, :, span(peer, part)], qkv.at[:, span(me, rows), :])
-    steps = pipeline(gather.plan, gather.stages())
-    run(steps[:1])
-    gather.store()
+    ex = [Exchange(place, ssem.at[t], rsem.at[t], lsem.at[t]) for t in range(3 + pairs)]
+    comes, backs = ex[:3], ex[3:]
+    me, peers = comes[0].me, comes[0].peers
+
+    def first_norm():
+        copy = keep(outs[0], w_time, csem.at[0])
+        copy.wait()
+        for j in range(shards):
+            add = jnp.dot(
+                emb[j], w_time[j // XS, j % XS], preferred_element_type=jnp.float32
+            )
+            scales[...] = add if j == 0 else scales[...] + add
+
+        def step(i, _):
+            own = span(i, rows // 3)
+            v = tokens[own, :].astype(jnp.float32)
+            scale = sum(member[own, j : j + 1] * scales[j : j + 1, :width] for j in range(NSEQ))
+            centred = v - jnp.mean(v, axis=1, keepdims=True)
+            spread = jnp.mean(centred * centred, axis=1, keepdims=True)
+            h_one[own, :] = (centred * lax.rsqrt(spread + EPS) * (1.0 + scale)).astype(BF)
+            return 0
+
+        lax.fori_loop(0, 3, step, 0)
+
+    def project(j):
+        copy = keep(outs[1].at[:, :, :, j * width : (j + 1) * width], w_part, csem.at[1])
+        copy.wait()
+        wide = 256
+
+        def step(i, _):
+            cols = span(i, wide)
+            w = w_part[:, :, :, cols].reshape(width, wide)
+            y = jnp.dot(h_one[...], w, preferred_element_type=jnp.float32)
+            for t in range(wide // 128):
+                v = y[:, t * 128 : (t + 1) * 128]
+                if j < 2:
+                    v = v * cos[...] + swap_halves(v) * sin[...]
+                packed[j, i * (wide // 128) + t] = v.astype(BF)
+            return 0
+
+        lax.fori_loop(0, width // wide, step, 0)
+        for k, (_, peer, _) in enumerate(peers):
+            for t in range(pairs):
+                comes[j].give(
+                    (k, t),
+                    packed.at[j, peer * pairs + t],
+                    qkv.at[j, span(me, rows), t * 128 : (t + 1) * 128],
+                )
+        for t in range(pairs):
+            comes[j].mine(
+                packed.at[j, me * pairs + t], qkv.at[j, span(me, rows), t * 128 : (t + 1) * 128], t
+            )
+
+    def segments():
+        order_rows.middle()
+        order_rows.end()
+        copy = keep(rows_out[0], places, csem.at[2])
+        copy.wait()
+        row = jnp.concatenate(
+            [places[y, c] for y in range(place.Y) for c in range(CORES)], axis=1
+        )
+        seg = sum((row >= ends[j : j + 1, :1]).astype(jnp.float32) for j in range(NSEQ - 1))
+        seg_row[...] = seg
+        seg_col[...] = seg.T
 
     block = 256
 
@@ -655,47 +682,85 @@
         src = mixed_heads.at[span(owner, rows), t * 128 : (t + 1) * 128]
         first = pl.multiple_of(me * part + t * 128, 128)
         dst = mixed.at[:, pl.ds(first, 128)]
-        if k < len(come.peers):
-            backs[t].give(k, src, dst)
+        if k < len(peers):
+            backs[t].give((k, 0), src, dst)
         else:
             backs[t].mine(src, dst)
 
-    work = [(lambda: None, 16), (come.take, 0)]
-    owners = [peer for _, peer, _ in come.peers] + [me]
+    def take():
+        for come in comes:
+            come.take()
+
+    gather.load()
+    order_rows.load()
+    cot_rows.load()
+    greet(place, seq=True)
+    steps = pipeline(gather.plan, gather.stages())
+    last = {p["w"]: p["i"] for p in gather.plan}
+    ready = [[p["i"] for p in gather.plan if p["w"] == 1 and p["first"] == j * width][-1] for j in range(3)]
+    hooks = {last[0]: [segments, first_norm]}
+    for j in range(3):
+        hooks[ready[j]] = [functools.partial(project, j)]
+    steps = after(steps, gather.finish, hooks)
+    run(steps[:1])
+    order_rows.start()
+    gather.store()
+    ahead = steps.index(hooks[ready[2]][0]) + 1
+    run(steps[1:ahead])
+    work = [(lambda: None, 16), (take, 0), (cot_rows.start, 0)]
+    owners = [peer for _, peer, _ in peers] + [me]
     for t in range(pairs):
-        work += [(functools.partial(attend, h), 8) for h in (2 * t, 2 * t + 1)]
+        work += [(functools.partial(attend, h), 10) for h in (2 * t, 2 * t + 1)]
         work += [(functools.partial(finish, t, k, owner), 0) for k, owner in enumerate(owners)]
-    interleave(steps[1:], work)
+    work += [(cot_rows.middle, 0)]
+    interleave(steps[ahead:], work)
     for back in backs:
         back.take()
-    for ex in [come] + backs:
-        ex.close()
-
-
-def attention_forward(slices, shards, width, which, ws, packed, seg_col, seg_row, cid):
-    rows = packed.shape[1]
+    cot_rows.end()
+    for e in ex:
+        e.close()
+
+
+def forward(slices, shards, which, ws, rows_in, tokens, member, ends, emb, cos, sin, cid):
+    rows, width = tokens.shape
     group, part = rows * slices, width // slices
+    pairs = part // 128
     items = pieces(width // shards, width, which, GATHER_CLASS)
     nw = len(ws)
+    f32 = jnp.float32
     out = pl.pallas_call(
         functools.partial(forward_body, slices, shards, items, nw),
-        out_shape=gathered_shapes(slices, shards, ws, [])
+        out_shape=gathered_shapes(slices, shards, ws, rows_in)
         + [
+            jax.ShapeDtypeStruct((rows, width), BF),
+            jax.ShapeDtypeStruct((8, 2 * width), f32),
+            jax.ShapeDtypeStruct((group, 1), f32),
+            jax.ShapeDtypeStruct((1, group), f32),
             jax.ShapeDtypeStruct((3, group, part), BF),
             jax.ShapeDtypeStruct((group, part), BF),
-            jax.ShapeDtypeStruct((part // HD, group), jnp.float32),
+            jax.ShapeDtypeStruct((part // HD, group), f32),
             jax.ShapeDtypeStruct((rows, width), BF),
         ],
-        in_specs=[ANY] * (nw + 1) + [VM] * 2,
-        out_specs=[ANY] * nw + [VM] * 4,
+        in_specs=[ANY] * (nw + 2) + [VM] * 6,
+        out_specs=[ANY] * (nw + 2) + [VM] * 8,
         scratch_shapes=gather_scratch(slices, shards, items)
-        + [DMA((1 + part // 128, slices))] * 2
-        + [DMA((1 + part // 128,))],
+        + row_scratch(slices, rows_in)
+        + [
+            pltpu.VMEM((shards // XS, XS) + ws[0].shape, BF),
+            pltpu.VMEM((shards // XS, XS, width // shards, width), BF),
+            pltpu.VMEM((3, width // 128, rows, 128), BF),
+            pltpu.VMEM((slices // CORES, CORES, 1, rows), jnp.int32),
+            DMA((3,)),
+            DMA((3 + pairs, slices, pairs)),
+            DMA((3 + pairs, slices, pairs)),
+            DMA((3 + pairs, pairs)),
+        ],
         compiler_params=pltpu.CompilerParams(
             collective_id=cid, has_side_effects=True, vmem_limit_bytes=VMEM_ALL
         ),
-    )(*ws, packed, seg_col, seg_row)
-    return merged(out[:nw]), out[nw:]
+    )(*ws, *rows_in, tokens, member, ends, emb, cos, sin)
+    full = [g.reshape((slices,) + r.shape) for g, r in zip(out[nw:], rows_in)]
+    return merged(out[:nw]), full, out[nw + 2 :]
 
 
 def backward_body(slices, shards, items, nw, nr, *refs):
@@ -721,7 +786,7 @@
         r.load()
     greet(place, seq=True)
     for k, (_, peer, _) in enumerate(come.peers):
-        come.give(k, d_mixed.at[:, span(peer, part)], g.at[span(me, rows), :])
+        come.give((k, 0), d_mixed.at[:, span(peer, part)], g.at[span(me, rows), :])
     block = 256
 
     def attend(h):
@@ -747,14 +812,14 @@
         first = pl.multiple_of(me * part + t * 128, 128)
         src, dst = turned.at[t, :, own, :], out.at[:, :, pl.ds(first, 128)]
         if k < len(come.peers):
-            backs[t].give(k, src, dst)
+            backs[t].give((k, 0), src, dst)
         else:
             backs[t].mine(src, dst)
 
-    work = [(lambda: None, 10), (come.take, 0)] + [(r.start, 0) for r in gathers]
+    work = [(lambda: None, 20), (come.take, 0)] + [(r.start, 0) for r in gathers]
     owners = [peer for _, peer, _ in come.peers] + [me]
     for t in range(pairs):
-        work += [(functools.partial(attend, h), 10) for h in (2 * t, 2 * t + 1)]
+        work += [(functools.partial(attend, h), 16) for h in (2 * t, 2 * t + 1)]
         work += [(functools.partial(finish, t, k, owner), 0) for k, owner in enumerate(owners)]
     steps = pipeline(sums.plan, sums.stages())
     interleave(steps, work)
@@ -788,42 +853,13 @@
         + row_scratch(slices, rows_in)
         + [pltpu.VMEM((group, part), BF), total, total, total]
         + [pltpu.VMEM((pairs, 3, group, 128), BF)]
-        + [DMA((1 + pairs, slices)), DMA((1 + pairs, slices)), DMA((1 + pairs,))],
+        + [DMA((1 + pairs, slices, 1)), DMA((1 + pairs, slices, 1)), DMA((1 + pairs, 1))],
         compiler_params=pltpu.CompilerParams(
             collective_id=cid, has_side_effects=True, vmem_limit_bytes=VMEM_ALL
         ),
     )(*grads, *rows_in, d_mixed, *kept, seg_col, seg_row, cos, sin)
     full = [g.reshape((slices,) + r.shape) for g, r in zip(out[nw:], rows_in)]
     return out[:nw], full, out[nw + nr]
-
-
-def project_body(h, w, cos, sin, out):
-    y = jnp.dot(h[...], w[...], preferred_element_type=jnp.float32)
-    turned = (pl.program_id(0) < 2).astype(jnp.float32)
-    c = cos[...] * turned + (1.0 - turned)
-    s = sin[...] * turned
-    for t in range(y.shape[1] // 128):
-        w_ = slice(t * 128, (t + 1) * 128)
-        out[0, :, w_] = (y[:, w_] * c + swap_halves(y[:, w_]) * s).astype(BF)
-
-
-def project(h, w, cos, sin, block=512):
-    rows, width = h.shape
-    const = lambda j, n: (0, 0)
-    per = width // block
-    return pl.pallas_call(
-        project_body,
-        grid=(3, per),
-        out_shape=jax.ShapeDtypeStruct((3, rows, width), BF),
-        in_specs=[
-            pl.BlockSpec((rows, width), const),
-            pl.BlockSpec((width, block), lambda j, n: (0, j * per + n)),
-            pl.BlockSpec((rows, 128), const),
-            pl.BlockSpec((rows, 128), const),
-        ],
-        out_specs=pl.BlockSpec((1, rows, block), lambda j, n: (j, 0, n)),
-        compiler_params=pltpu.CompilerParams(vmem_limit_bytes=VMEM_ALL),
-    )(h, w, cos, sin)
 
 
 def time_embedding(steps):
@@ -868,27 +904,31 @@
     slices, shards = lax.axis_size("seq"), lax.axis_size("fsdp")
     group = rows * slices
     lens, places = lengths[0], order[0]
-    (f_time, f_qkv), (order_all, cot_all) = gather_weights(
-        slices, shards, width, "tq", [w_time, w_qkv], [order, cotangent[0]], 0
+    member, _, offset = layout(lens, places)
+    emb = time_embedding(time_steps[0]).astype(BF)
+    cos, sin = turn_tables(offset)
+    fulls, (order_all, cot_all), kept = forward(
+        slices,
+        shards,
+        "tqoud",
+        [w_time, w_qkv, w_out, w_up, w_down],
+        [order, cotangent[0]],
+        tokens[0],
+        jnp.pad(member, ((0, 0), (0, 8 - NSEQ))),
+        jnp.broadcast_to(jnp.pad(jnp.cumsum(lens), (0, 8 - NSEQ))[:, None], (8, 128)),
+        jnp.pad(emb, ((0, 8 - NSEQ), (0, 0))).reshape(8, shards, -1).transpose(1, 0, 2),
+        cos,
+        sin,
+        0,
     )
+    _, f_qkv, f_out, f_up, f_down = fulls
+    h_one, scales_seq, seg_col, seg_row, heads_qkv, mixed_heads, logsum, mixed = kept
     order_all = order_all.reshape(group)
-
-    member, _, offset = layout(lens, places)
-    _, segment_all, offset_all = layout(lens, order_all)
-    seg_col, seg_row = segment_all[:, None], segment_all[None, :]
-    emb = time_embedding(time_steps[0]).astype(BF)
-    scales_seq = jnp.dot(emb, f_time, preferred_element_type=jnp.float32)
-    scales = jnp.dot(member, scales_seq, precision=lax.Precision.HIGHEST)
+    _, _, offset_all = layout(lens, order_all)
+    scales = jnp.dot(member, scales_seq[:NSEQ], precision=lax.Precision.HIGHEST)
     scale_one, scale_two = scales[:, :width], scales[:, width:]
     inputs = tokens[0].astype(jnp.float32)
-    normed_one, pull_one = jax.vjp(norm_mod, inputs, scale_one)
-    h_one = normed_one.astype(BF)
-
-    cos, sin = turn_tables(offset)
-    packed = project(h_one, f_qkv, cos, sin)
-    (f_out, f_up, f_down), (heads_qkv, mixed_heads, logsum, mixed) = attention_forward(
-        slices, shards, width, "oud", [w_out, w_up, w_down], packed, seg_col, seg_row, 1
-    )
+    _, pull_one = jax.vjp(norm_mod, inputs, scale_one)
 
     x_two = inputs + jnp.dot(mixed, f_out, preferred_element_type=jnp.float32)
     normed_two, pull_two = jax.vjp(norm_mod, x_two, scale_two)

time: 514 us -> 504 us (0.981)
  Pallas kernels: 393 us -> 379 us
    pallas_call x3 -> x1, Pallas kernels: 180 us -> 165 us  [forward(): pl.pallas_call(functools.partial(forward_body, slices, shards, items, nw)...]
where the time goes in v4:
time: 504 us; the launch traced here: 495 us
  Pallas kernels  379 us (75%)
  matrix products  77.5 us (15%)
  other arithmetic  28.8 us (6%)
  local copies, waits for them, and re-layouts  8.75 us (2%)
    pallas_call x1, Pallas kernels, forward(): pl.pallas_call(functools.partial(forward_body, slices, shards, items, nw)...  165 us
    pallas_call x1, Pallas kernels, attention_backward(): pl.pallas_call(functools.partial(backward_body, slices, shards, items, nw...  157 us
    pallas_call x1, Pallas kernels, sum_grads(): pl.pallas_call(functools.partial(sum_body, slices, shards, items, nw), ou...  56.4 us
    dot_general x8, matrix products, dot(): lax.dot_general(a, b, (((ca,), (cb,)), ((), ())), preferred_element_type=...  50.6 us

profile of v4, /device:TPU:0, one launch (start us, length us, event | category | flops | bytes accessed | tf_op | source)
XLA Modules:
  0.0 495.4 jit_solution(12693425061142207971)
XLA Ops:
  4.5 1.3 convert_reduce_fusion
  9.4 1.1 pad_maximum_fusion.2
  10.5 165.1 %shard_map.153 = (bf16[4,2,32,2048]{3,2,1,0:T(8,128)(2,1)}, bf16[4,2,128,3072]{3,2,1,0:T(8,128)(2,1)}, bf16[4,2,128,1024]{3,2,1,0:T(8,128)(2,1)}, bf16[4,2,128,4...) custom-call(bf16[32,2048]{1,0:T(8,128)(2,1)} %refs_0_.1, ...), custom_call_target="tpu_custom_call" | custom-call | tf_op jit(solution)/shard_map/pallas_call | solution.py:731
  177.2 3.5 fusion.15
  180.8 1.1 fusion.51
  182.2 2.8 fusion.39
  185.0 1.6 pad_maximum_fusion.1.refs_11_
  186.6 1.6 pad_maximum_fusion.refs_10_
  188.2 1.4 fusion.41
  190.0 5.7 %fusion.52 = f32[384,4096]{1,0:T(8,128)} fusion(bf16[384,1024]{1,0:T(8,128)(2,1)S(1)} %multiply_convert_fusion.1, bf16[1024,4096]{1,0:T(8,128)(2,1)S(1)} %bitcast.77), kind=kOutput, calls=%fused_computation.101 | convolution fusion | flops 3221225472 | bytes 15466496 | tf_op jit(solution)/shard_map/dot_general | solution.py:936
  196.5 7.8 %add_convert_fusion.refs_3_ = bf16[384,1024]{1,0:T(8,128)(2,1)} fusion(f32[384,1024]{1,0:T(8,128)S(1)} %get-tuple-element.68, bf16[4096,1024]{1,0:T(8,128)(2,1)S(1)} %bitcast.82, f32[384,4096]{1,0:T(8,128)} %fusion.52), kind=kOutput, calls=%fused_computation.39 | convolution fusion | flops 3236167680 | bytes 17039360 | tf_op jit(solution)/shard_map/dot_general | solution.py:939
  204.3 13.9 %fusion.6 = bf16[384,4096]{1,0:T(8,128)(2,1)} fusion(f32[384,4096]{1,0:T(8,128)} %fusion.52, bf16[4096,1024]{1,0:T(8,128)(2,1)} %bitcast.79, f32[384,1024]{1,0:T(8,128)S(1)} %fusion.15), kind=kOutput, calls=%fused_computation.10 | convolution fusion | flops 3253075968 | bytes 19398656 | tf_op jit(solution)/shard_map/dot_general | solution.py:512
  218.3 5.7 %multiply_reduce_fusion = (f32[384]{0:T(512)S(1)}, f32[384,1024]{1,0:T(8,128)S(1)}) fusion(f32[384,1024]{1,0:T(8,128)S(1)} %get-tuple-element.68, f32[384]{0:T(512)S(1)} %broadcast_multiply_fusion.1, f32[384,2048]{1,0:T(8,128)S(1)} %fusion.41, bf16[384,4096]{1,0:T(8,128)(2,1)} %fusion.6, bf16[1024,4096]{1,0:T(8,128)(2,1)S(1)} %bitcast.78), kind=kOutput, calls=%fused_computation.41 | convolution fusion | flops 3223191040 | bytes 16256000 | tf_op jit(solution)/shard_map/dot_general | solution.py:512
  224.0 1.8 fusion.50
  226.1 1.9 convolution_convert_fusion.5.refs_4_
  228.2 7.4 %convolution_convert_fusion.1 = bf16[4096,1024]{1,0:T(8,128)(2,1)} fusion(f32[384,1024]{1,0:T(8,128)S(1)} %fusion.15, f32[384,4096]{1,0:T(8,128)S(1)} %bitcast.90), kind=kOutput, calls=%fused_computation.3 | convolution fusion | flops 3239968768 | bytes 16252928 | tf_op jit(solution)/shard_map/dot_general | solution.py:512
  235.6 2.6 convolution_convert_fusion.4
  238.3 6.8 %convolution_convert_fusion = bf16[1024,4096]{1,0:T(8,128)(2,1)} fusion(bf16[384,1024]{1,0:T(8,128)(2,1)S(1)} %multiply_convert_fusion.1, bf16[384,4096]{1,0:T(8,128)(2,1)S(1)} %copy-done.32), kind=kOutput, calls=%fused_computation.2 | convolution fusion | flops 3225419776 | bytes 12320768 | tf_op jit(solution)/shard_map/dot_general | solution.py:512
  245.0 157.2 %shard_map.154 = (bf16[512,1024]{1,0:T(8,128)(2,1)}, bf16[128,4096]{1,0:T(8,128)(2,1)}, bf16[128,1024]{1,0:T(8,128)(2,1)}, bf16[2,2,384,1024]{3,2,1,0:T(8,128)(2,1)}, bf16[3,384,1024]{2,1,0:T(8,128)(2,1)}) custom-call(bf16[4,2,512,1024]{3,2,1,0:T(8,128)(2,1)} %bitcast.59, bf16[4,2,128,4096]{3,2,1,0:T(8,128)(2,1)} %bitcast.60, ...), custom_call_target="tpu_custom_call" | custom-call | tf_op jit(solution)/shard_map/pallas_call | solution.py:845
  402.3 4.2 fusion.26
  406.5 4.6 copy.24
  411.2 6.8 %fusion.18 = (f32[384]{0:T(512)S(1)}, f32[384]{0:T(512)S(1)}, f32[384,1024]{1,0:T(8,128)S(1)}) fusion(f32[384]{0:T(512)S(1)} %copy-done.27, bf16[1,384,1024]{2,1,0:T(8,128)(2,1)} %param.10, f32[384,2048]{1,0:T(8,128)S(1)} %copy-done.1, bf16[384,3072]{0,1:T(8,128)(2,1)} %bitcast.64, bf16[1024,3072]{1,0:T(8,128)(2,1)} %bitcast.83), kind=kOutput, calls=%fused_computation.32 | convolution fusion | flops 2419063808 | bytes 12587520 | tf_op jit(solution)/shard_map/dot_general | solution.py:512
  419.4 1.2 fusion.7
  420.6 1.4 add_bitcast_fusion
  422.9 2.0 convolution_convert_fusion.3
  424.9 1.5 convert_element_type.111
  426.5 1.6 convert_element_type.112
  428.0 0.9 copy-done.7
  429.1 5.5 %convolution_convert_fusion.2 = bf16[1024,3072]{1,0:T(8,128)(2,1)} fusion(bf16[384,1024]{1,0:T(8,128)(2,1)S(1)} %copy-done.31, bf16[384,3072]{0,1:T(8,128)(2,1)S(1)} %bitcast.65), kind=kOutput, calls=%fused_computation.12 | convolution fusion | flops 2419064832 | bytes 9437184 | tf_op jit(solution)/shard_map/dot_general | solution.py:512
  434.5 56.4 %shard_map.155 = (bf16[128,3072]{1,0:T(8,128)(2,1)}, bf16[32,2048]{1,0:T(8,128)(2,1)}) custom-call(bf16[4,2,128,3072]{3,2,1,0:T(8,128)(2,1)} %bitcast.62, bf16[4,2,32,2048]{3,2,1,0:T(8,128)(2,1)} %bitcast.63), custom_call_target="tpu_custom_call" | custom-call | tf_op jit(solution)/shard_map/pallas_call | solution.py:499
  490.9 1.6 convert_element_type.108
  492.5 2.4 convert_element_type.109
  (115 shorter events, 13.3 us)
Async XLA Ops:
  1.5 9.0 %copy-start.17 = (s32[3,1]{0,1:T(1,128)}, s32[3,1]{0,1:T(1,128)S(1)}, u32[]{:S(2)}) copy-start(s32[3,1]{0,1:T(1,128)S(1)} %reduce-window.4) | copy-start | bytes 40
  2.1 8.4 %copy-start.20 = (s32[3]{0:T(128)}, s32[3]{0:T(128)S(1)}, u32[]{:S(2)}) copy-start(s32[3]{0:T(128)S(1)} %fusion.47) | copy-start | bytes 40
  2.1 8.4 %copy-start.28 = (f32[32]{0:T(128)}, f32[32]{0:T(128)S(1)}, u32[]{:S(2)}) copy-start(f32[32]{0:T(128)S(1)} %multiply_exponential_fusion) | copy-start | bytes 388
  2.9 3.5 copy-start.23
  3.0 3.5 copy-start.25
  4.3 6.2 %copy-start.12 = (s32[384]{0:T(512)}, s32[384]{0:T(512)S(1)}, u32[]{:S(2)}) copy-start(s32[384]{0:T(512)S(1)} %reduce) | copy-start | bytes 4612
  176.4 4.3 copy-start.15
  177.2 3.5 copy-start.4
  177.2 3.5 copy-start.10
  177.2 3.5 copy-start.30
  180.7 9.3 %slice-start = ((s8[8388608]{0:T(1024)(128)(4,1)}), s8[4194304]{0:T(1024)(128)(4,1)S(1)}, s32[]{:S(2)}) async-start(s8[8388608]{0:T(1024)(128)(4,1)} %bitcast.75), calls=%async_computation | async-start | bytes 8388608
  185.0 3.2 copy-start.13
  185.0 3.2 copy-start.16
  185.0 3.2 copy-start.18
  185.0 3.2 copy-start.21
  185.0 5.0 %slice-start.1 = ((s8[8388608]{0:T(1024)(128)(4,1)}), s8[4194304]{0:T(1024)(128)(4,1)S(1)}, s32[]{:S(2)}) async-start(s8[8388608]{0:T(1024)(128)(4,1)} %bitcast.75), calls=%async_computation.1 | async-start | bytes 8388608
  189.6 34.3 %copy-start = (f32[384,2048]{1,0:T(8,128)}, f32[384,2048]{1,0:T(8,128)S(1)}, u32[]{:S(2)}) copy-start(f32[384,2048]{1,0:T(8,128)S(1)} %fusion.41) | copy-start | bytes 9437188
  189.6 6.1 %slice-start.2 = ((s8[8388608]{0:T(1024)(128)(4,1)}), s8[4194304]{0:T(1024)(128)(4,1)S(1)}, s32[]{:S(2)}) async-start(s8[8388608]{0:T(1024)(128)(4,1)} %bitcast.80), calls=%async_computation.2 | async-start | bytes 8388608
  190.0 6.5 %slice-start.3 = ((s8[8388608]{0:T(1024)(128)(4,1)}), s8[4194304]{0:T(1024)(128)(4,1)S(1)}, s32[]{:S(2)}) async-start(s8[8388608]{0:T(1024)(128)(4,1)} %bitcast.80), calls=%async_computation.3 | async-start | bytes 8388608
  224.0 4.0 slice-start.4
  225.8 2.4 slice-start.5
  226.0 9.6 %copy-start.2 = (f32[384,1024]{1,0:T(8,128)}, f32[384,1024]{1,0:T(8,128)S(1)}, u32[]{:S(2)}) copy-start(f32[384,1024]{1,0:T(8,128)S(1)} %add_add_fusion.2) | copy-start | bytes 4718596
  235.6 2.6 copy-start.32
  406.5 4.6 copy-start.1
  406.5 4.7 copy-start.27
  411.2 6.8 %copy-start.5 = (bf16[1,384,1024]{2,1,0:T(8,128)(2,1)S(1)}, bf16[1,384,1024]{2,1,0:T(8,128)(2,1)}, u32[]{:S(2)}) copy-start(bf16[1,384,1024]{2,1,0:T(8,128)(2,1)} %param.10) | copy-start | bytes 2359300
  420.6 2.3 copy-start.24
  420.6 2.3 copy-start.26
  420.6 4.3 copy-start.9
  422.1 4.4 copy-start.8
  426.5 2.4 copy-start.7
  426.5 2.6 copy-start.31
  (7 other events, 10.3 us)

commit v5 on v4

--- a/solution.py
+++ b/solution.py
@@ -29,8 +29,8 @@
 CUT = 2
 LAG = 2
 
-GATHER_CLASS = {"t": "D", "q": "CDC", "o": "C", "u": "DCDC", "d": "DCDC"}
-SUM_CLASS = {"t": "DD", "q": "CDC", "o": "C", "u": "CCDC", "d": "DCDC"}
+GATHER_CLASS = {"t": "D", "q": "DDC", "o": "C", "u": "CCCC", "d": "CCDC"}
+SUM_CLASS = {'q': 'DCD', 'o': 'C', 'u': 'CCCC', 'd': 'CDCC'}
 
 
 class Place:
@@ -301,15 +301,16 @@
 
 
 class GradSum:
-    def __init__(self, place, items, grads, outs, acc, rc, ry, rx, rz, fin, rf, lsem, ssem, rsem):
+    def __init__(self, place, items, grads, outs, acc, own, ry, rx, rz, fin, rf, lsem, ssem, rsem):
         self.place, self.grads, self.outs = place, grads, outs
-        self.acc, self.rc, self.ry, self.rx, self.rz = acc, rc, ry, rx, rz
+        self.acc, self.own, self.ry, self.rx, self.rz = acc, own, ry, rx, rz
         self.fin, self.rf = fin, rf
         self.lsem, self.ssem, self.rsem = lsem, ssem, rsem
         self.wide = acc.shape[-1]
         self.plan = []
         for i, (w, r0, rn, c0, cn, kind) in enumerate(items):
             p = dict(i=i, w=w, kind=kind, rn=rn, c0=c0, half=cn // CORES)
+            p["first"] = c0
             p["k"] = sum(q["kind"] == kind for q in self.plan)
             p.update(rows=pl.ds(r0, rn), vr=pl.ds(0, rn), sends=[])
             self.plan.append(p)
@@ -337,7 +338,7 @@
             p["own"].append(
                 keep(
                     g.at[:, :, p["rows"], self.cols(p, place.c, part)],
-                    self.acc.at[i, part, :, :, vr, :],
+                    self.own.at[i % (LAG + 1), part, :, :, vr, :],
                     self.lsem.at[i, part],
                 )
             )
@@ -346,7 +347,7 @@
                     p,
                     first + part,
                     g.at[:, :, p["rows"], self.cols(p, 1 - place.c, part)],
-                    self.rc.at[i, part, :, :, vr, :],
+                    self.acc.at[i, part, :, :, vr, :],
                     place.at(c=1 - place.c),
                 )
             )
@@ -358,7 +359,7 @@
         for copy in p["c"]:
             copy.wait_recv()
         for part in range(place.Y):
-            add_into(self.acc.at[i, part], self.rc.at[i, part], p["rn"])
+            add_into(self.acc.at[i, part], self.own.at[i % (LAG + 1), part], p["rn"])
         p["y"] = []
         if p["kind"] == "D":
             for d in range(1, place.Y):
@@ -468,7 +469,7 @@
     nc = max(1, n - nd)
     return [
         pltpu.VMEM((n, Y, Z, XS, rows, wide), BF),
-        pltpu.VMEM((n, Y, Z, XS, rows, wide), BF),
+        pltpu.VMEM((LAG + 1, Y, Z, XS, rows, wide), BF),
         pltpu.VMEM((nd, Y - 1, Z, XS, rows, wide), BF),
         pltpu.VMEM((n, Y, Z, rows, wide), BF),
         pltpu.VMEM((n, Z - 1, Y, rows, wide), BF),
@@ -480,32 +481,57 @@
     ]
 
 
-def sum_body(slices, shards, items, nw, *refs):
-    place = Place(slices, shards)
-    sums = GradSum(place, items, refs[:nw], refs[nw : 2 * nw], *refs[2 * nw :])
-    greet(place)
-    run(pipeline(sums.plan, sums.stages()))
-
-
 def split_grads(shards, grads):
     return [g.reshape(shards // XS, XS, -1, g.shape[1]) for g in grads]
 
 
-def sum_grads(slices, shards, width, which, grads, cid):
-    rows = width // shards
-    items = pieces(rows, width, which, SUM_CLASS)
-    nw = len(grads)
-    grads = split_grads(shards, grads)
+def spread_body(slices, shards, mine, out, group, total, ssem, rsem):
+    place = Place(slices, shards)
+    seq = place.y * CORES + place.c
+    fsdp = place.z * XS + place.x
+    near, far = [], []
+    for d in range(1, slices):
+        near.append({"seq": lax.rem(seq + d, slices), "fsdp": fsdp})
+    for d in range(1, shards):
+        far.append({"seq": seq, "fsdp": lax.rem(fsdp + d, shards)})
+    barrier = pltpu.get_barrier_semaphore()
+    for other in near + far:
+        pl.semaphore_signal(barrier, inc=1, device_id=other, device_id_type=MESH)
+    pl.semaphore_wait(barrier, len(near + far))
+    copies = [
+        push(mine, group.at[seq], ssem.at[d], rsem.at[d], other) for d, other in enumerate(near)
+    ]
+    group[seq] = mine[...]
+    for copy in copies:
+        copy.wait_recv()
+    total[...] = sum(group[k] for k in range(slices))
+    first = slices - 1
+    copies += [
+        push(total, out.at[fsdp], ssem.at[first + d], rsem.at[first + d], other)
+        for d, other in enumerate(far)
+    ]
+    out[fsdp] = total[...]
+    for copy in copies[first:]:
+        copy.wait_recv()
+    for copy in copies:
+        copy.wait_send()
+
+
+def spread(slices, shards, mine, cid):
+    n = slices + shards
     return pl.pallas_call(
-        functools.partial(sum_body, slices, shards, items, nw),
-        out_shape=[jax.ShapeDtypeStruct(g.shape[2:], BF) for g in grads],
-        in_specs=[ANY] * nw,
-        out_specs=[ANY] * nw,
-        scratch_shapes=sum_scratch(slices, shards, items),
-        compiler_params=pltpu.CompilerParams(
-            collective_id=cid, has_side_effects=True, vmem_limit_bytes=VMEM_ALL
-        ),
-    )(*grads)
+        functools.partial(spread_body, slices, shards),
+        out_shape=jax.ShapeDtypeStruct((shards,) + mine.shape, mine.dtype),
+        in_specs=[VM],
+        out_specs=VM,
+        scratch_shapes=[
+            pltpu.VMEM((slices,) + mine.shape, mine.dtype),
+            pltpu.VMEM(mine.shape, mine.dtype),
+            DMA((n,)),
+            DMA((n,)),
+        ],
+        compiler_params=pltpu.CompilerParams(collective_id=cid, has_side_effects=True),
+    )(mine)
 
 
 def dot(a, b, ca, cb):
@@ -766,14 +792,15 @@
 def backward_body(slices, shards, items, nw, nr, *refs):
     grads, rows_in = refs[:nw], refs[nw : nw + nr]
     at = nw + nr
-    d_mixed, qkv, mixed, logsum, seg_col, seg_row, cos, sin = refs[at : at + 8]
-    at += 8
-    sums_out, rows_out, out = refs[at : at + nw], refs[at + nw : at + nw + nr], refs[at + nw + nr]
-    scratch = refs[at + nw + nr + 1 :]
+    d_mixed, qkv, mixed, logsum, seg_col, seg_row, cos, sin, h_one = refs[at : at + 9]
+    at += 9
+    sums_out, rows_out = refs[at : at + nw + 1], refs[at + nw + 1 : at + nw + 1 + nr]
+    out = refs[at + nw + 1 + nr]
+    scratch = refs[at + nw + nr + 2 :]
     place = Place(slices, shards)
-    sums = GradSum(place, items, grads, sums_out, *scratch[:10])
+    g, dk, dv, dq, turned, grad_qkv, ssem, rsem, lsem = scratch[10 + 4 * nr :]
+    sums = GradSum(place, items, list(grads) + [grad_qkv], sums_out, *scratch[:10])
     gathers = row_gathers(place, rows_in, rows_out, scratch[10:])
-    g, dk, dv, dq, turned, ssem, rsem, lsem = scratch[10 + 4 * nr :]
     rows, part = d_mixed.shape[0], g.shape[1]
     pairs = part // 128
     come = Exchange(place, ssem.at[0], rsem.at[0], lsem.at[0])
@@ -787,7 +814,7 @@
     greet(place, seq=True)
     for k, (_, peer, _) in enumerate(come.peers):
         come.give((k, 0), d_mixed.at[:, span(peer, part)], g.at[span(me, rows), :])
-    block = 256
+    block = min(256, 128 * 3072 // seg_col.shape[0])
 
     def attend(h):
         if h % 2 == 0:
@@ -816,17 +843,40 @@
         else:
             backs[t].mine(src, dst)
 
-    work = [(lambda: None, 20), (come.take, 0)] + [(r.start, 0) for r in gathers]
+    work = [(lambda: None, 14), (come.take, 0)] + [(r.start, 0) for r in gathers]
     owners = [peer for _, peer, _ in come.peers] + [me]
     for t in range(pairs):
-        work += [(functools.partial(attend, h), 16) for h in (2 * t, 2 * t + 1)]
+        work += [(functools.partial(attend, h), 10) for h in (2 * t, 2 * t + 1)]
         work += [(functools.partial(finish, t, k, owner), 0) for k, owner in enumerate(owners)]
+    work += [(r.middle, 0) for r in gathers]
+
+    def weigh(j):
+        if j == 0:
+            for back in backs:
+                back.take()
+        width, wide = h_one.shape[1], 256
+
+        def step(i, _):
+            cols = span(i, wide)
+            t = dot(h_one[...], out[j, :, cols], 0, 0).astype(BF)
+            shape = grad_qkv.shape[:3] + (wide,)
+            grad_qkv[:, :, :, pl.ds(pl.multiple_of(j * width + i * wide, wide), wide)] = t.reshape(shape)
+            return 0
+
+        lax.fori_loop(0, width // wide, step, 0)
+
+    width = h_one.shape[1]
     steps = pipeline(sums.plan, sums.stages())
-    interleave(steps, work)
-    for r in gathers:
-        r.middle()
-    for back in backs:
-        back.take()
+    cuts = []
+    for j in range(3):
+        piece = next(p for p in sums.plan if p["w"] == nw and p["first"] == j * width)
+        cuts.append(
+            next(k for k, st in enumerate(steps) if st.func == sums.over_c and st.args[0] is piece)
+        )
+    interleave(steps[: cuts[0]], work)
+    for j in range(3):
+        weigh(j)
+        run(steps[cuts[j] : (cuts + [len(steps)])[j + 1]])
     for r in gathers:
         r.end()
     for ex in [come] + backs:
@@ -834,7 +884,7 @@
 
 
 def attention_backward(
-    slices, shards, width, which, grads, rows_in, d_mixed, kept, seg_col, seg_row, cos, sin, cid
+    slices, shards, width, which, grads, rows_in, d_mixed, kept, seg_col, seg_row, cos, sin, h_one, cid
 ):
     rows = d_mixed.shape[0]
     group, part = rows * slices, width // slices
@@ -845,21 +895,23 @@
     out = pl.pallas_call(
         functools.partial(backward_body, slices, shards, items, nw, nr),
         out_shape=[jax.ShapeDtypeStruct(w.shape[2:], BF) for w in grads]
+        + [jax.ShapeDtypeStruct((width // shards, 3 * width), BF)]
         + gathered_shapes(slices, shards, [], rows_in)
         + [jax.ShapeDtypeStruct((3, rows, width), BF)],
-        in_specs=[ANY] * (nw + nr + 1) + [VM] * 7,
-        out_specs=[ANY] * (nw + nr) + [VM],
+        in_specs=[ANY] * (nw + nr + 1) + [VM] * 8,
+        out_specs=[ANY] * (nw + nr + 1) + [VM],
         scratch_shapes=sum_scratch(slices, shards, items)
         + row_scratch(slices, rows_in)
         + [pltpu.VMEM((group, part), BF), total, total, total]
         + [pltpu.VMEM((pairs, 3, group, 128), BF)]
+        + [pltpu.VMEM((shards // XS, XS, width // shards, 3 * width), BF)]
         + [DMA((1 + pairs, slices, 1)), DMA((1 + pairs, slices, 1)), DMA((1 + pairs, 1))],
         compiler_params=pltpu.CompilerParams(
             collective_id=cid, has_side_effects=True, vmem_limit_bytes=VMEM_ALL
         ),
-    )(*grads, *rows_in, d_mixed, *kept, seg_col, seg_row, cos, sin)
-    full = [g.reshape((slices,) + r.shape) for g, r in zip(out[nw:], rows_in)]
-    return out[:nw], full, out[nw + nr]
+    )(*grads, *rows_in, d_mixed, *kept, seg_col, seg_row, cos, sin, h_one)
+    full = [g.reshape((slices,) + r.shape) for g, r in zip(out[nw + 1 :], rows_in)]
+    return out[: nw + 1], full, out[nw + 1 + nr]
 
 
 def time_embedding(steps):
@@ -954,7 +1006,7 @@
         slices,
         shards,
         width,
-        "duo",
+        "duoq",
         [grad_down, grad_up, grad_out],
         [result],
         d_mixed,
@@ -963,10 +1015,10 @@
         seg_row,
         cos_all,
         sin_all,
-        2,
+        h_one,
+        1,
     )
     d_qkv = d_packed.transpose(1, 0, 2).reshape(rows, 3 * width)
-    grad_qkv = dot(h_one, d_qkv, 0, 0).astype(BF)
     d_xone, d_scale_one = pull_one(dot(d_qkv, f_qkv, 1, 1))
     input_grad = d_xtwo + d_xone
     d_scales = lax.dot_general(
@@ -976,16 +1028,23 @@
         precision=lax.Precision.HIGHEST,
         preferred_element_type=jnp.float32,
     )
-    grad_time = lax.dot_general(
-        emb.astype(jnp.float32),
-        d_scales,
+    emb_once = jnp.where(lax.axis_index("seq") == 0, emb.astype(jnp.float32), 0.0)
+    packed = jnp.concatenate(
+        [d_scales, jnp.pad(emb_once, ((0, 0), (0, 2 * width - TEMB)))], axis=0
+    )
+    spread_all = spread(slices, shards, jnp.pad(packed, ((0, 8 - 2 * NSEQ), (0, 0))), 2)
+    shard = w_time.shape[0]
+    emb_all = lax.dynamic_slice_in_dim(
+        spread_all[:, NSEQ : 2 * NSEQ], lax.axis_index("fsdp") * shard, shard, 2
+    )
+    s_time = lax.dot_general(
+        emb_all.reshape(-1, shard),
+        spread_all[:, :NSEQ].reshape(-1, 2 * width),
         (((0,), (0,)), ((), ())),
         precision=lax.Precision.HIGHEST,
         preferred_element_type=jnp.float32,
-    ).astype(BF)
-
-    sums = sums + sum_grads(slices, shards, width, "qt", [grad_qkv, grad_time], 3)
-    s_down, s_up, s_out, s_qkv, s_time = [g.astype(jnp.float32) for g in sums]
+    )
+    s_down, s_up, s_out, s_qkv = [g.astype(jnp.float32) for g in sums]
     mine = lax.axis_index("seq") * rows + jnp.arange(rows, dtype=jnp.int32)
     output = pick_rows(result_all, mine, order_all).astype(BF)
     return (output[None], input_grad[None], s_time, s_qkv, s_out, s_up, s_down)

time: 504 us -> 461 us (0.915)
  the two profiles are of different devices: /device:TPU:0 before, /device:TPU:11 now
where the time goes in v5:
time: 461 us; the launch traced here: 453 us
  Pallas kernels  344 us (75%)
  matrix products  71.1 us (15%)
  other arithmetic  26.6 us (6%)
  local copies, waits for them, and re-layouts  9.88 us (2%)
    pallas_call x1, Pallas kernels, attention_backward(): pl.pallas_call(functools.partial(backward_body, slices, shards, items, nw...  169 us
    pallas_call x1, Pallas kernels, forward(): pl.pallas_call(functools.partial(forward_body, slices, shards, items, nw)...  153 us
    dot_general x7, matrix products, dot(): lax.dot_general(a, b, (((ca,), (cb,)), ((), ())), preferred_element_type=...  45.1 us
    pallas_call x1, Pallas kernels, spread(): pl.pallas_call(functools.partial(spread_body, slices, shards), out_shape=...  21.6 us

profile of v5, /device:TPU:11, one launch (start us, length us, event | category | flops | bytes accessed | tf_op | source)
XLA Modules:
  0.0 452.9 jit_solution(5068116985352632234)
XLA Ops:
  0.6 0.8 reduce-window.4
  5.1 1.3 convert_reduce_fusion
  10.0 1.1 pad_maximum_fusion.2
  11.1 152.6 %shard_map.153 = (bf16[4,2,32,2048]{3,2,1,0:T(8,128)(2,1)}, bf16[4,2,128,3072]{3,2,1,0:T(8,128)(2,1)}, bf16[4,2,128,1024]{3,2,1,0:T(8,128)(2,1)}, bf16[4,2,128,4...) custom-call(bf16[32,2048]{1,0:T(8,128)(2,1)} %refs_0_.1, ...), custom_call_target="tpu_custom_call" | custom-call | tf_op jit(solution)/shard_map/pallas_call | solution.py:757
  165.2 3.5 fusion.15
  168.8 1.1 fusion.54
  170.2 2.8 fusion.39
  173.0 1.6 pad_maximum_fusion.1.refs_11_
  174.6 1.6 pad_maximum_fusion.refs_10_
  176.2 1.4 fusion.42
  178.0 5.7 %fusion.55 = f32[384,4096]{1,0:T(8,128)} fusion(bf16[384,1024]{1,0:T(8,128)(2,1)S(1)} %multiply_convert_fusion.1, bf16[1024,4096]{1,0:T(8,128)(2,1)S(1)} %bitcast.71), kind=kOutput, calls=%fused_computation.107 | convolution fusion | flops 3221225472 | bytes 15466496 | tf_op jit(solution)/shard_map/dot_general | solution.py:988
  184.5 7.8 %add_convert_fusion.refs_3_ = bf16[384,1024]{1,0:T(8,128)(2,1)} fusion(f32[384,1024]{1,0:T(8,128)S(1)} %get-tuple-element.68, bf16[4096,1024]{1,0:T(8,128)(2,1)S(1)} %bitcast.76, f32[384,4096]{1,0:T(8,128)} %fusion.55), kind=kOutput, calls=%fused_computation.38 | convolution fusion | flops 3236167680 | bytes 17039360 | tf_op jit(solution)/shard_map/dot_general | solution.py:991
  192.3 13.9 %fusion.6 = bf16[384,4096]{1,0:T(8,128)(2,1)} fusion(f32[384,4096]{1,0:T(8,128)} %fusion.55, bf16[4096,1024]{1,0:T(8,128)(2,1)} %bitcast.73, f32[384,1024]{1,0:T(8,128)S(1)} %fusion.15), kind=kOutput, calls=%fused_computation.10 | convolution fusion | flops 3253075968 | bytes 19398656 | tf_op jit(solution)/shard_map/dot_general | solution.py:538
  206.2 5.7 %multiply_reduce_fusion = (f32[384]{0:T(512)S(1)}, f32[384,1024]{1,0:T(8,128)S(1)}) fusion(f32[384,1024]{1,0:T(8,128)S(1)} %get-tuple-element.68, f32[384]{0:T(512)S(1)} %broadcast_multiply_fusion.1, f32[384,2048]{1,0:T(8,128)S(1)} %fusion.42, bf16[384,4096]{1,0:T(8,128)(2,1)} %fusion.6, bf16[1024,4096]{1,0:T(8,128)(2,1)S(1)} %bitcast.72), kind=kOutput, calls=%fused_computation.40 | convolution fusion | flops 3223191040 | bytes 16256000 | tf_op jit(solution)/shard_map/dot_general | solution.py:538
  212.0 1.8 fusion.52
  214.1 1.9 convolution_convert_fusion.3.refs_4_
  216.2 7.4 %convolution_convert_fusion.1 = bf16[4096,1024]{1,0:T(8,128)(2,1)} fusion(f32[384,1024]{1,0:T(8,128)S(1)} %fusion.15, f32[384,4096]{1,0:T(8,128)S(1)} %bitcast.84), kind=kOutput, calls=%fused_computation.3 | convolution fusion | flops 3239968768 | bytes 16252928 | tf_op jit(solution)/shard_map/dot_general | solution.py:538
  223.6 2.6 convolution_convert_fusion.2
  226.2 6.8 %convolution_convert_fusion = bf16[1024,4096]{1,0:T(8,128)(2,1)} fusion(bf16[384,1024]{1,0:T(8,128)(2,1)S(1)} %multiply_convert_fusion.1, bf16[384,4096]{1,0:T(8,128)(2,1)S(1)} %copy-done.28), kind=kOutput, calls=%fused_computation.2 | convolution fusion | flops 3225419776 | bytes 12320768 | tf_op jit(solution)/shard_map/dot_general | solution.py:538
  233.0 169.5 %shard_map.154 = (bf16[512,1024]{1,0:T(8,128)(2,1)}, bf16[128,4096]{1,0:T(8,128)(2,1)}, bf16[128,1024]{1,0:T(8,128)(2,1)}, bf16[128,3072]{1,0:T(8,128)(2,1)}, bf...) custom-call(bf16[4,2,512,1024]{3,2,1,0:T(8,128)(2,1)} %bitcast.56, bf16[4,2,128,4096]{3,2,1,0:T(8,128)(2,1)} %bitcast.57, ...), custom_call_target="tpu_custom_call" | custom-call | tf_op jit(solution)/shard_map/pallas_call | solution.py:895
  402.5 4.2 fusion.26
  406.7 4.6 %copy.31 = bf16[384,3,1024]{0,2,1:T(8,128)(2,1)} copy(bf16[384,3,1024]{2,0,1:T(8,128)(2,1)} %bitcast.59) | data formatting | bytes 4718592 | tf_op jit(solution)/shard_map/transpose | solution.py:1021
  411.4 6.8 %fusion.18 = (f32[384]{0:T(512)S(1)}, f32[384]{0:T(512)S(1)}, f32[384,1024]{1,0:T(8,128)S(1)}) fusion(f32[384]{0:T(512)S(1)} %copy-done.24, bf16[1,384,1024]{2,1,0:T(8,128)(2,1)} %param.10, f32[384,2048]{1,0:T(8,128)S(1)} %copy-done.1, bf16[384,3072]{0,1:T(8,128)(2,1)} %bitcast.60, bf16[1024,3072]{1,0:T(8,128)(2,1)} %bitcast.77), kind=kOutput, calls=%fused_computation.31 | convolution fusion | flops 2419063808 | bytes 12587520 | tf_op jit(solution)/shard_map/dot_general | solution.py:538
  419.6 1.2 fusion.7
  420.8 1.4 add_bitcast_fusion
  422.9 21.6 %shard_map.155 = f32[8,8,2048]{2,1,0:T(8,128)} custom-call(f32[8,2048]{1,0:T(8,128)} %pad.27.mine), custom_call_target="tpu_custom_call" | custom-call | tf_op jit(solution)/shard_map/pallas_call | solution.py:522
  444.6 1.4 fusion.53
  446.0 1.2 convolution_bitcast_fusion
  447.2 0.8 convert_element_type.105
  448.1 1.3 convert_element_type.104
  449.4 1.5 convert_element_type.106
  450.9 1.6 convert_element_type.107
  (110 shorter events, 12.8 us)
Async XLA Ops:
  1.5 9.6 %copy-start.18 = (s32[3,1]{0,1:T(1,128)}, s32[3,1]{0,1:T(1,128)S(1)}, u32[]{:S(2)}) copy-start(s32[3,1]{0,1:T(1,128)S(1)} %reduce-window.4) | copy-start | bytes 40
  2.1 8.9 %copy-start.21 = (s32[3]{0:T(128)}, s32[3]{0:T(128)S(1)}, u32[]{:S(2)}) copy-start(s32[3]{0:T(128)S(1)} %fusion.49) | copy-start | bytes 40
  2.1 8.9 %copy-start.25 = (f32[32]{0:T(128)}, f32[32]{0:T(128)S(1)}, u32[]{:S(2)}) copy-start(f32[32]{0:T(128)S(1)} %multiply_exponential_fusion) | copy-start | bytes 388
  4.2 6.8 %copy-start.12 = (s32[384]{0:T(512)}, s32[384]{0:T(512)S(1)}, u32[]{:S(2)}) copy-start(s32[384]{0:T(512)S(1)} %reduce) | copy-start | bytes 4612
  164.4 4.3 copy-start.15
  165.2 3.5 copy-start.4
  165.2 3.5 copy-start.10
  165.2 3.5 copy-start.27
  168.7 1.4 copy-start.26
  168.7 9.2 %slice-start = ((s8[8388608]{0:T(1024)(128)(4,1)}), s8[4194304]{0:T(1024)(128)(4,1)S(1)}, s32[]{:S(2)}) async-start(s8[8388608]{0:T(1024)(128)(4,1)} %bitcast.69), calls=%async_computation | async-start | bytes 8388608
  173.0 3.2 copy-start.13
  173.0 3.2 copy-start.16
  173.0 3.2 copy-start.19
  173.0 3.2 copy-start.22
  173.0 5.0 %slice-start.1 = ((s8[8388608]{0:T(1024)(128)(4,1)}), s8[4194304]{0:T(1024)(128)(4,1)S(1)}, s32[]{:S(2)}) async-start(s8[8388608]{0:T(1024)(128)(4,1)} %bitcast.69), calls=%async_computation.1 | async-start | bytes 8388608
  177.6 34.3 %copy-start = (f32[384,2048]{1,0:T(8,128)}, f32[384,2048]{1,0:T(8,128)S(1)}, u32[]{:S(2)}) copy-start(f32[384,2048]{1,0:T(8,128)S(1)} %fusion.42) | copy-start | bytes 9437188
  177.6 6.1 %slice-start.2 = ((s8[8388608]{0:T(1024)(128)(4,1)}), s8[4194304]{0:T(1024)(128)(4,1)S(1)}, s32[]{:S(2)}) async-start(s8[8388608]{0:T(1024)(128)(4,1)} %bitcast.74), calls=%async_computation.2 | async-start | bytes 8388608
  178.0 6.5 %slice-start.3 = ((s8[8388608]{0:T(1024)(128)(4,1)}), s8[4194304]{0:T(1024)(128)(4,1)S(1)}, s32[]{:S(2)}) async-start(s8[8388608]{0:T(1024)(128)(4,1)} %bitcast.74), calls=%async_computation.3 | async-start | bytes 8388608
  212.0 4.0 slice-start.4
  213.8 2.4 slice-start.5
  214.0 9.6 %copy-start.2 = (f32[384,1024]{1,0:T(8,128)}, f32[384,1024]{1,0:T(8,128)S(1)}, u32[]{:S(2)}) copy-start(f32[384,1024]{1,0:T(8,128)S(1)} %add_add_fusion.2) | copy-start | bytes 4718596
  223.6 2.6 copy-start.28
  406.7 4.7 %copy-start.1 = (f32[384,2048]{1,0:T(8,128)S(1)}, f32[384,2048]{1,0:T(8,128)}, u32[]{:S(2)}) copy-start(f32[384,2048]{1,0:T(8,128)} %copy-done) | copy-start | bytes 9437188
  406.7 4.7 %copy-start.24 = (f32[384]{0:T(512)S(1)}, f32[384]{0:T(512)}, u32[]{:S(2)}) copy-start(f32[384]{0:T(512)} %broadcast_multiply_fusion) | copy-start | bytes 4612
  411.4 6.8 %copy-start.5 = (bf16[1,384,1024]{2,1,0:T(8,128)(2,1)S(1)}, bf16[1,384,1024]{2,1,0:T(8,128)(2,1)}, u32[]{:S(2)}) copy-start(bf16[1,384,1024]{2,1,0:T(8,128)(2,1)} %param.10) | copy-start | bytes 2359300
  418.2 1.4 copy-start.6
  419.0 1.8 copy-start.3
  420.8 1.4 copy-start.17
  422.3 24.9 %copy-start.11 = (bf16[128,1024]{1,0:T(8,128)(2,1)S(1)}, bf16[128,1024]{1,0:T(8,128)(2,1)}, u32[]{:S(2)}) copy-start(bf16[128,1024]{1,0:T(8,128)(2,1)} %get-tuple-element.44) | copy-start | bytes 786436
  422.3 25.8 %copy-start.9 = (bf16[128,3072]{1,0:T(8,128)(2,1)S(1)}, bf16[128,3072]{1,0:T(8,128)(2,1)}, u32[]{:S(2)}) copy-start(bf16[128,3072]{1,0:T(8,128)(2,1)} %get-tuple-element.43) | copy-start | bytes 2359300
  444.6 4.8 %copy-start.8 = (bf16[128,4096]{1,0:T(8,128)(2,1)S(1)}, bf16[128,4096]{1,0:T(8,128)(2,1)}, u32[]{:S(2)}) copy-start(bf16[128,4096]{1,0:T(8,128)(2,1)} %get-tuple-element.45) | copy-start | bytes 3145732
  448.1 2.8 copy-start.7
  (3 other events, 4.2 us)

commit v6 on v5

--- a/solution.py
+++ b/solution.py
@@ -27,6 +27,7 @@
 MESH = pl.DeviceIdType.MESH
 VMEM_ALL = 67043328
 CUT = 2
+FIRST, PER = 14, 5
 LAG = 2
 
 GATHER_CLASS = {"t": "D", "q": "DDC", "o": "C", "u": "CCCC", "d": "CCDC"}
@@ -618,11 +619,12 @@
 
 def forward_body(slices, shards, items, nw, *refs):
     ws, (order, cot) = refs[:nw], refs[nw : nw + 2]
-    tokens, member, ends, emb, cos, sin = refs[nw + 2 : nw + 8]
-    refs = refs[nw + 8 :]
+    tokens, member, ends, emb, cos, sin, freqs = refs[nw + 2 : nw + 9]
+    refs = refs[nw + 9 :]
     outs, rows_out = refs[:nw], refs[nw : nw + 2]
     h_one, scales, seg_col, seg_row, qkv, mixed_heads, logsum, mixed = refs[nw + 2 : nw + 10]
-    scratch = refs[nw + 10 :]
+    cos_all, sin_all = refs[nw + 10 : nw + 12]
+    scratch = refs[nw + 12 :]
     place = Place(slices, shards)
     gather = WeightGather(place, items, ws, outs, *scratch[:4])
     order_rows, cot_rows = row_gathers(place, (order, cot), rows_out, scratch[4:12])
@@ -694,6 +696,21 @@
         seg = sum((row >= ends[j : j + 1, :1]).astype(jnp.float32) for j in range(NSEQ - 1))
         seg_row[...] = seg
         seg_col[...] = seg.T
+
+    def tables():
+        row = jnp.concatenate(
+            [places[y, c] for y in range(place.Y) for c in range(CORES)], axis=1
+        )
+        start = jnp.zeros_like(row)
+        for j in range(NSEQ - 1):
+            start = jnp.where(row >= ends[j : j + 1, :1], ends[j : j + 1, :1], start)
+        offset = (row - start).astype(jnp.float32).T
+        size = 256
+        for i in range(offset.shape[0] // size):
+            own = slice(i * size, (i + 1) * size)
+            angles = offset[own] * freqs[0:1, :]
+            cos_all[own, :] = jnp.cos(angles)
+            sin_all[own, :] = jnp.sin(angles) * freqs[1:2, :]
 
     block = 256
 
@@ -738,7 +755,7 @@
     for t in range(pairs):
         work += [(functools.partial(attend, h), 10) for h in (2 * t, 2 * t + 1)]
         work += [(functools.partial(finish, t, k, owner), 0) for k, owner in enumerate(owners)]
-    work += [(cot_rows.middle, 0)]
+    work += [(tables, 4), (cot_rows.middle, 0)]
     interleave(steps[ahead:], work)
     for back in backs:
         back.take()
@@ -747,7 +764,7 @@
         e.close()
 
 
-def forward(slices, shards, which, ws, rows_in, tokens, member, ends, emb, cos, sin, cid):
+def forward(slices, shards, which, ws, rows_in, tokens, member, ends, emb, cos, sin, freqs, cid):
     rows, width = tokens.shape
     group, part = rows * slices, width // slices
     pairs = part // 128
@@ -766,9 +783,11 @@
             jax.ShapeDtypeStruct((group, part), BF),
             jax.ShapeDtypeStruct((part // HD, group), f32),
             jax.ShapeDtypeStruct((rows, width), BF),
+            jax.ShapeDtypeStruct((group, 128), f32),
+            jax.ShapeDtypeStruct((group, 128), f32),
         ],
-        in_specs=[ANY] * (nw + 2) + [VM] * 6,
-        out_specs=[ANY] * (nw + 2) + [VM] * 8,
+        in_specs=[ANY] * (nw + 2) + [VM] * 7,
+        out_specs=[ANY] * (nw + 2) + [VM] * 10,
         scratch_shapes=gather_scratch(slices, shards, items)
         + row_scratch(slices, rows_in)
         + [
@@ -784,7 +803,7 @@
         compiler_params=pltpu.CompilerParams(
             collective_id=cid, has_side_effects=True, vmem_limit_bytes=VMEM_ALL
         ),
-    )(*ws, *rows_in, tokens, member, ends, emb, cos, sin)
+    )(*ws, *rows_in, tokens, member, ends, emb, cos, sin, freqs)
     full = [g.reshape((slices,) + r.shape) for g, r in zip(out[nw:], rows_in)]
     return merged(out[:nw]), full, out[nw + 2 :]
 
@@ -816,8 +835,8 @@
         come.give((k, 0), d_mixed.at[:, span(peer, part)], g.at[span(me, rows), :])
     block = min(256, 128 * 3072 // seg_col.shape[0])
 
-    def attend(h):
-        if h % 2 == 0:
+    def attend(h, half):
+        if h % 2 == 0 and half == 0:
             dk[...] = jnp.zeros_like(dk)
             dv[...] = jnp.zeros_like(dv)
 
@@ -827,7 +846,8 @@
             )
             return 0
 
-        lax.fori_loop(0, seg_col.shape[0] // block, step, 0)
+        steps = seg_col.shape[0] // block // 2
+        lax.fori_loop(half * steps, (half + 1) * steps, step, 0)
 
     def finish(t, k, owner):
         own = span(owner, rows)
@@ -843,10 +863,14 @@
         else:
             backs[t].mine(src, dst)
 
-    work = [(lambda: None, 14), (come.take, 0)] + [(r.start, 0) for r in gathers]
+    work = [(lambda: None, FIRST), (come.take, 0)] + [(r.start, 0) for r in gathers]
     owners = [peer for _, peer, _ in come.peers] + [me]
     for t in range(pairs):
-        work += [(functools.partial(attend, h), 10) for h in (2 * t, 2 * t + 1)]
+        work += [
+            (functools.partial(attend, h, half), PER)
+            for h in (2 * t, 2 * t + 1)
+            for half in range(2)
+        ]
         work += [(functools.partial(finish, t, k, owner), 0) for k, owner in enumerate(owners)]
     work += [(r.middle, 0) for r in gathers]
 
@@ -931,6 +955,14 @@
     return (member.astype(jnp.float32), segment, offset)
 
 
+def turn_rates():
+    half = HD // 2
+    freqs = jnp.exp(-math.log(BASE) * jnp.arange(half, dtype=jnp.float32) * 2.0 / HD)
+    ones = jnp.ones(half, jnp.float32)
+    sign = jnp.concatenate([-ones, ones, -ones, ones])
+    return jnp.pad(jnp.stack([jnp.tile(freqs, 4), sign]), ((0, 6), (0, 0)))
+
+
 def turn_tables(offset):
     half = HD // 2
     freqs = jnp.exp(-math.log(BASE) * jnp.arange(half, dtype=jnp.float32) * 2.0 / HD)
@@ -971,12 +1003,13 @@
         jnp.pad(emb, ((0, 8 - NSEQ), (0, 0))).reshape(8, shards, -1).transpose(1, 0, 2),
         cos,
         sin,
+        turn_rates(),
         0,
     )
     _, f_qkv, f_out, f_up, f_down = fulls
-    h_one, scales_seq, seg_col, seg_row, heads_qkv, mixed_heads, logsum, mixed = kept
+    h_one, scales_seq, seg_col, seg_row, heads_qkv, mixed_heads, logsum, mixed = kept[:8]
+    cos_all, sin_all = kept[8:]
     order_all = order_all.reshape(group)
-    _, _, offset_all = layout(lens, order_all)
     scales = jnp.dot(member, scales_seq[:NSEQ], precision=lax.Precision.HIGHEST)
     scale_one, scale_two = scales[:, :width], scales[:, width:]
     inputs = tokens[0].astype(jnp.float32)
@@ -1001,7 +1034,6 @@
     grad_out = dot(mixed, d_attn, 0, 0).astype(BF)
     d_mixed = dot(d_attn, f_out, 1, 1).astype(BF)
 
-    cos_all, sin_all = turn_tables(offset_all)
     sums, (result_all,), d_packed = attention_backward(
         slices,
         shards,
@@ -1018,8 +1050,10 @@
         h_one,
         1,
     )
-    d_qkv = d_packed.transpose(1, 0, 2).reshape(rows, 3 * width)
-    d_xone, d_scale_one = pull_one(dot(d_qkv, f_qkv, 1, 1))
+    d_hone = sum(
+        dot(d_packed[j], f_qkv[:, j * width : (j + 1) * width], 1, 1) for j in range(3)
+    )
+    d_xone, d_scale_one = pull_one(d_hone)
     input_grad = d_xtwo + d_xone
     d_scales = lax.dot_general(
         member,
@@ -1029,17 +1063,14 @@
         preferred_element_type=jnp.float32,
     )
     emb_once = jnp.where(lax.axis_index("seq") == 0, emb.astype(jnp.float32), 0.0)
-    packed = jnp.concatenate(
-        [d_scales, jnp.pad(emb_once, ((0, 0), (0, 2 * width - TEMB)))], axis=0
-    )
-    spread_all = spread(slices, shards, jnp.pad(packed, ((0, 8 - 2 * NSEQ), (0, 0))), 2)
-    shard = w_time.shape[0]
-    emb_all = lax.dynamic_slice_in_dim(
-        spread_all[:, NSEQ : 2 * NSEQ], lax.axis_index("fsdp") * shard, shard, 2
-    )
+    packed = jnp.concatenate([d_scales.reshape(-1, 128), emb_once.reshape(-1, 128)], axis=0)
+    rest = -packed.shape[0] % 8
+    spread_all = spread(slices, shards, jnp.pad(packed, ((0, rest), (0, 0))), 2)
+    shard, many = w_time.shape[0], d_scales.size // 128
+    emb_all = spread_all[:, many : many + emb.size // 128].reshape(shards * NSEQ, TEMB)
     s_time = lax.dot_general(
-        emb_all.reshape(-1, shard),
-        spread_all[:, :NSEQ].reshape(-1, 2 * width),
+        lax.dynamic_slice_in_dim(emb_all, lax.axis_index("fsdp") * shard, shard, 1),
+        spread_all[:, :many].reshape(shards * NSEQ, 2 * width),
         (((0,), (0,)), ((), ())),
         precision=lax.Precision.HIGHEST,
         preferred_element_type=jnp.float32,

time: 461 us -> 444 us (0.963)
  the two profiles are of different devices: /device:TPU:11 before, /device:TPU:0 now
where the time goes in v6:
time: 444 us; the launch traced here: 436 us
  Pallas kernels  336 us (76%)
  matrix products  69.7 us (16%)
  other arithmetic  21.1 us (5%)
  local copies, waits for them, and re-layouts  7.73 us (2%)
    pallas_call x1, Pallas kernels, attention_backward(): pl.pallas_call(functools.partial(backward_body, slices, shards, items, nw...  170 us
    pallas_call x1, Pallas kernels, forward(): pl.pallas_call(functools.partial(forward_body, slices, shards, items, nw)...  153 us
    dot_general x9, matrix products, dot(): lax.dot_general(a, b, (((ca,), (cb,)), ((), ())), preferred_element_type=...  43.4 us
    pallas_call x1, Pallas kernels, spread(): pl.pallas_call(functools.partial(spread_body, slices, shards), out_shape=...  13.1 us

profile of v6, /device:TPU:0, one launch (start us, length us, event | category | flops | bytes accessed | tf_op | source)
XLA Modules:
  0.0 436.0 jit_solution(18079954226009310129)
XLA Ops:
  4.6 1.3 convert_reduce_fusion
  6.5 1.3 select_maximum_fusion.1.refs_13_
  11.3 1.1 pad_maximum_fusion
  12.4 152.9 %shard_map.153 = (bf16[4,2,32,2048]{3,2,1,0:T(8,128)(2,1)}, bf16[4,2,128,3072]{3,2,1,0:T(8,128)(2,1)}, bf16[4,2,128,1024]{3,2,1,0:T(8,128)(2,1)}, bf16[4,2,128,4...) custom-call(bf16[32,2048]{1,0:T(8,128)(2,1)} %refs_0_.1, ...), custom_call_target="tpu_custom_call" | custom-call | tf_op jit(solution)/shard_map/pallas_call | solution.py:774
  166.7 3.5 fusion.15
  170.3 1.1 fusion.65
  171.7 1.4 fusion.54
  173.6 5.7 %fusion.66 = f32[384,4096]{1,0:T(8,128)} fusion(bf16[384,1024]{1,0:T(8,128)(2,1)S(1)} %multiply_convert_fusion.1, bf16[1024,4096]{1,0:T(8,128)(2,1)S(1)} %bitcast.79), kind=kOutput, calls=%fused_computation.111 | convolution fusion | flops 3221225472 | bytes 15466496 | tf_op jit(solution)/shard_map/dot_general | solution.py:1021
  180.0 7.8 %add_convert_fusion.refs_3_ = bf16[384,1024]{1,0:T(8,128)(2,1)} fusion(f32[384,1024]{1,0:T(8,128)S(1)} %get-tuple-element.69, bf16[4096,1024]{1,0:T(8,128)(2,1)S(1)} %bitcast.84, f32[384,4096]{1,0:T(8,128)} %fusion.66), kind=kOutput, calls=%fused_computation.44 | convolution fusion | flops 3236167680 | bytes 17039360 | tf_op jit(solution)/shard_map/dot_general | solution.py:1024
  187.8 13.9 %fusion.6 = bf16[384,4096]{1,0:T(8,128)(2,1)} fusion(f32[384,4096]{1,0:T(8,128)} %fusion.66, bf16[4096,1024]{1,0:T(8,128)(2,1)} %bitcast.81, f32[384,1024]{1,0:T(8,128)S(1)} %fusion.15), kind=kOutput, calls=%fused_computation.10 | convolution fusion | flops 3253075968 | bytes 19398656 | tf_op jit(solution)/shard_map/dot_general | solution.py:539
  201.8 5.7 %multiply_reduce_fusion = (f32[384]{0:T(512)S(1)}, f32[384,1024]{1,0:T(8,128)S(1)}) fusion(f32[384,1024]{1,0:T(8,128)S(1)} %get-tuple-element.69, f32[384]{0:T(512)S(1)} %broadcast_multiply_fusion.1, f32[384,2048]{1,0:T(8,128)S(1)} %fusion.54, bf16[384,4096]{1,0:T(8,128)(2,1)} %fusion.6, bf16[1024,4096]{1,0:T(8,128)(2,1)S(1)} %bitcast.80), kind=kOutput, calls=%fused_computation.46 | convolution fusion | flops 3223191040 | bytes 16256000 | tf_op jit(solution)/shard_map/dot_general | solution.py:539
  207.5 1.8 fusion.64
  209.6 1.9 convolution_convert_fusion.3.refs_4_
  211.5 0.9 slice-done.7
  212.4 7.4 %convolution_convert_fusion.1 = bf16[4096,1024]{1,0:T(8,128)(2,1)} fusion(f32[384,1024]{1,0:T(8,128)S(1)} %fusion.15, f32[384,4096]{1,0:T(8,128)S(1)} %bitcast.91), kind=kOutput, calls=%fused_computation.3 | convolution fusion | flops 3239968768 | bytes 16252928 | tf_op jit(solution)/shard_map/dot_general | solution.py:539
  219.8 2.6 convolution_convert_fusion.2
  222.4 6.8 %convolution_convert_fusion = bf16[1024,4096]{1,0:T(8,128)(2,1)} fusion(bf16[384,1024]{1,0:T(8,128)(2,1)S(1)} %multiply_convert_fusion.1, bf16[384,4096]{1,0:T(8,128)(2,1)S(1)} %copy-done.26), kind=kOutput, calls=%fused_computation.2 | convolution fusion | flops 3225419776 | bytes 12320768 | tf_op jit(solution)/shard_map/dot_general | solution.py:539
  229.2 169.8 %shard_map.154 = (bf16[512,1024]{1,0:T(8,128)(2,1)}, bf16[128,4096]{1,0:T(8,128)(2,1)}, bf16[128,1024]{1,0:T(8,128)(2,1)}, bf16[128,3072]{1,0:T(8,128)(2,1)}, bf...) custom-call(bf16[4,2,512,1024]{3,2,1,0:T(8,128)(2,1)} %bitcast.63, bf16[4,2,128,4096]{3,2,1,0:T(8,128)(2,1)} %bitcast.64, ...), custom_call_target="tpu_custom_call" | custom-call | tf_op jit(solution)/shard_map/pallas_call | solution.py:919
  399.0 4.4 %fusion.34 = bf16[1,384,1024]{2,1,0:T(8,128)(2,1)} fusion(bf16[1536,1024]{1,0:T(8,128)(2,1)} %bitcast.86, s32[1536]{0:T(1024)} %eq.32, s32[384]{0:T(512)} %iota_add_fusion), kind=kOutput, calls=%fused_computation.53 | convolution fusion | flops 1208942592 | bytes 3939840 | tf_op jit(solution)/shard_map/dot_general | solution.py:983
  403.4 0.8 convert_element_type.104
  404.3 1.3 convert_element_type.103
  405.6 2.6 fusion.18
  408.2 1.0 fusion.20
  409.2 0.8 copy-done.1
  410.3 1.5 fusion.24
  413.2 1.2 fusion.7
  415.0 1.4 add_bitcast_fusion
  416.4 13.1 %shard_map.155 = f32[8,56,128]{2,1,0:T(8,128)} custom-call(f32[56,128]{1,0:T(8,128)} %select_maximum_fusion.mine), custom_call_target="tpu_custom_call" | custom-call | tf_op jit(solution)/shard_map/pallas_call | solution.py:523
  430.3 0.9 slice.43
  431.3 1.2 fusion.56
  432.5 1.5 convert_element_type.105
  434.0 1.6 convert_element_type.106
  (112 shorter events, 14.2 us)
Async XLA Ops:
  1.5 10.9 %copy-start.19 = (s32[3,1]{0,1:T(1,128)}, s32[3,1]{0,1:T(1,128)S(1)}, u32[]{:S(2)}) copy-start(s32[3,1]{0,1:T(1,128)S(1)} %reduce-window.4) | copy-start | bytes 40
  2.1 10.3 %copy-start.22 = (s32[3]{0:T(128)}, s32[3]{0:T(128)S(1)}, u32[]{:S(2)}) copy-start(s32[3]{0:T(128)S(1)} %fusion.60) | copy-start | bytes 40
  4.2 8.2 %copy-start.13 = (s32[384]{0:T(512)}, s32[384]{0:T(512)S(1)}, u32[]{:S(2)}) copy-start(s32[384]{0:T(512)S(1)} %reduce) | copy-start | bytes 4612
  166.7 3.5 copy-start.4
  166.7 3.5 copy-start.10
  166.7 3.5 copy-start.25
  166.7 6.8 %slice-start.2 = ((s8[8388608]{0:T(1024)(128)(4,1)}), s8[4194304]{0:T(1024)(128)(4,1)S(1)}, s32[]{:S(2)}) async-start(s8[8388608]{0:T(1024)(128)(4,1)} %bitcast.77), calls=%async_computation.2 | async-start | bytes 8388608
  170.2 1.5 copy-start.14
  170.2 1.5 copy-start.16
  170.2 1.5 copy-start.20
  170.3 1.5 copy-start.23
  170.3 3.3 slice-start.3
  173.2 34.3 %copy-start = (f32[384,2048]{1,0:T(8,128)}, f32[384,2048]{1,0:T(8,128)S(1)}, u32[]{:S(2)}) copy-start(f32[384,2048]{1,0:T(8,128)S(1)} %fusion.54) | copy-start | bytes 9437188
  173.2 6.1 %slice-start.4 = ((s8[8388608]{0:T(1024)(128)(4,1)}), s8[4194304]{0:T(1024)(128)(4,1)S(1)}, s32[]{:S(2)}) async-start(s8[8388608]{0:T(1024)(128)(4,1)} %bitcast.82), calls=%async_computation.4 | async-start | bytes 8388608
  173.6 6.5 %slice-start.5 = ((s8[8388608]{0:T(1024)(128)(4,1)}), s8[4194304]{0:T(1024)(128)(4,1)S(1)}, s32[]{:S(2)}) async-start(s8[8388608]{0:T(1024)(128)(4,1)} %bitcast.82), calls=%async_computation.5 | async-start | bytes 8388608
  207.5 4.0 slice-start.6
  209.3 3.0 slice-start.7
  209.6 10.2 %copy-start.2 = (f32[384,1024]{1,0:T(8,128)}, f32[384,1024]{1,0:T(8,128)S(1)}, u32[]{:S(2)}) copy-start(f32[384,1024]{1,0:T(8,128)S(1)} %add_add_fusion.3) | copy-start | bytes 4718596
  219.8 2.6 copy-start.26
  399.0 4.4 %copy-start.12 = (bf16[128,1024]{1,0:T(8,128)(2,1)S(1)}, bf16[128,1024]{1,0:T(8,128)(2,1)}, u32[]{:S(2)}) copy-start(bf16[128,1024]{1,0:T(8,128)(2,1)} %get-tuple-element.48) | copy-start | bytes 786436
  399.0 5.3 %copy-start.9 = (bf16[128,3072]{1,0:T(8,128)(2,1)S(1)}, bf16[128,3072]{1,0:T(8,128)(2,1)}, u32[]{:S(2)}) copy-start(bf16[128,3072]{1,0:T(8,128)(2,1)} %get-tuple-element.47) | copy-start | bytes 2359300
  399.0 6.5 %copy-start.11 = (bf16[3,384,1024]{2,1,0:T(8,128)(2,1)S(1)}, bf16[3,384,1024]{2,1,0:T(8,128)(2,1)}, u32[]{:S(2)}) copy-start(bf16[3,384,1024]{2,1,0:T(8,128)(2,1)} %get-tuple-element.45) | copy-start | bytes 7077892
  399.0 9.1 %slice-start = ((s8[6291456]{0:T(1024)(128)(4,1)}), s8[4194304]{0:T(1024)(128)(4,1)S(1)}, s32[]{:S(2)}) async-start(s8[6291456]{0:T(1024)(128)(4,1)} %bitcast.67), calls=%async_computation | async-start | bytes 8388608
  403.4 4.8 %slice-start.1 = ((s8[6291456]{0:T(1024)(128)(4,1)}), s8[2097152]{0:T(1024)(128)(4,1)S(1)}, s32[]{:S(2)}) async-start(s8[6291456]{0:T(1024)(128)(4,1)} %bitcast.67), calls=%async_computation.1 | async-start | bytes 4194304
  408.2 1.9 copy-start.1
  408.2 2.1 copy-start.5
  408.2 2.1 copy-start.17
  411.8 1.4 copy-start.6
  412.6 1.8 copy-start.18
  412.6 2.4 copy-start.3
  416.4 16.1 %copy-start.8 = (bf16[128,4096]{1,0:T(8,128)(2,1)S(1)}, bf16[128,4096]{1,0:T(8,128)(2,1)}, u32[]{:S(2)}) copy-start(bf16[128,4096]{1,0:T(8,128)(2,1)} %get-tuple-element.49) | copy-start | bytes 3145732
  431.2 2.8 copy-start.7
  (3 other events, 4.2 us)
